TPU v7x, 32 devices: a whole 2x2x4 slice. The times are simulated.
32 devices in a mesh: gx: 4 (over z), gy: 4 (over y, x), gz: 2 (over core).
Axes of the slice: x: 2, y: 2, z: 4, core: 2. Of those that a mesh axis runs over, the one named last changes fastest.
Arguments:
- potential: float32 [16, 96, 512], P('gz', 'gx', 'gy'), may hold values from -6 to 6
- tissue_mask: int32 [16, 96, 512], P('gz', 'gx', 'gy'), may hold values from 0 to 2, as said below
- layer_index: int32 [16], P('gz'), may hold values from 0 to 15
- source: float32 [16, 96, 512], P('gz', 'gx', 'gy'), may hold values from -6 to 6
Outputs:
- phi_e: float32 [16, 96, 512], P('gz', 'gx', 'gy')
- residual: float32 [16, 96, 512], P('gz', 'gx', 'gy')
Inputs may be any that keep to these rules, and one draw needn't show every extreme that they name: `tissue_mask`: 0 marks cells outside every medium, 1 bath, 2 tissue.
All inputs are finite; a program needn't handle non-finite values.
Results may differ from a plain program's by a relative error of at most 0.0003.
Values sent between devices are 32-bit elements; how exact they have to be, the bound alone decides.
No kernel may reach another device: no remote copies, remote signals or barrier semaphores. Data moves between devices by JAX's collectives and lax.ppermute only.
A program may use at most 128 MiB of HBM per device.

v0:
```python
import math

import jax
import jax.numpy as jnp
from jax import lax
from jax.sharding import PartitionSpec as P

ITERS = 8
LAYERS = 16


OFFSETS = [
    (0, 1, 0),
    (0, 0, 1),
    (1, 0, 0),
    (0, 1, 1),
    (0, 1, -1),
    (1, 1, 0),
    (-1, 1, 0),
    (1, 0, 1),
    (-1, 0, 1),
]
bulk_long = 7.99
bulk_trans = 2.55
intra_long = 1.74
intra_trans = 0.19
bath_sigma = 5.0


def padded(value, sides, width):
    for axis, dim in sides:
        count, length = (lax.axis_size(axis), value.shape[dim])
        up = [(i, (i + 1) % count) for i in range(count - 1)]
        down = [(j, i) for i, j in up]
        last = lax.slice_in_dim(value, length - width, length, axis=dim)
        first = lax.slice_in_dim(value, 0, width, axis=dim)
        before = lax.ppermute(last, axis, up)
        after = lax.ppermute(first, axis, down)
        value = jnp.concatenate([before, value, after], axis=dim)
    return value


def tensor_table(layers, longitudinal, transverse):
    depth = jnp.arange(layers, dtype=jnp.float32) / (layers - 1)
    helix = math.pi / 3.0 * (1.0 - 2.0 * depth)
    tilted = 0.35 * jnp.cos(math.pi * depth)
    fiber_x = jnp.cos(tilted) * jnp.cos(helix)
    fiber_y = jnp.cos(tilted) * jnp.sin(helix)
    fiber_z = jnp.sin(tilted)
    spread = longitudinal - transverse
    s_xx = transverse + spread * fiber_x * fiber_x
    s_yy = transverse + spread * fiber_y * fiber_y
    s_zz = transverse + spread * fiber_z * fiber_z
    s_xy = spread * fiber_x * fiber_y
    s_xz = spread * fiber_x * fiber_z
    s_yz = spread * fiber_y * fiber_z
    columns = [
        s_xx - jnp.abs(s_xy) - jnp.abs(s_xz),
        s_yy - jnp.abs(s_xy) - jnp.abs(s_yz),
        s_zz - jnp.abs(s_xz) - jnp.abs(s_yz),
        jnp.maximum(s_xy, 0.0),
        jnp.maximum(-s_xy, 0.0),
        jnp.maximum(s_xz, 0.0),
        jnp.maximum(-s_xz, 0.0),
        jnp.maximum(s_yz, 0.0),
        jnp.maximum(-s_yz, 0.0),
    ]
    return jnp.stack(columns, axis=1)


def window(array, offset, extent):
    return array[
        1 + offset[0] : 1 + offset[0] + extent[0],
        1 + offset[1] : 1 + offset[1] + extent[1],
        1 + offset[2] : 1 + offset[2] + extent[2],
    ]


def cell_weight(planes, column, tissue_pad, bath_pad):
    weight = tissue_pad * planes[:, column][:, None, None]
    if bath_pad is not None and column < 3:
        weight = weight + bath_sigma * bath_pad
    return weight


def edge_pair(weight, medium_pad, offset, extent):
    backward = (-offset[0], -offset[1], -offset[2])
    centre = window(medium_pad, (0, 0, 0), extent)
    own_weight = window(weight, (0, 0, 0), extent)
    forward_edge = (
        centre
        * window(medium_pad, offset, extent)
        * (0.5 * (own_weight + window(weight, offset, extent)))
    )
    backward_edge = (
        centre
        * window(medium_pad, backward, extent)
        * (0.5 * (own_weight + window(weight, backward, extent)))
    )
    return (forward_edge, backward_edge)


def with_rim(field):
    return padded(field, (("gx", 1), ("gy", 2), ("gz", 0)), 1)


def operate(field, edge_list):
    extent = field.shape
    field_pad = with_rim(field)
    summed = jnp.zeros(extent, jnp.float32)
    for column, offset in enumerate(OFFSETS):
        backward = (-offset[0], -offset[1], -offset[2])
        forward_edge, backward_edge = edge_list[column]
        summed = (
            summed
            + forward_edge * (field - window(field_pad, offset, extent))
            + backward_edge * (field - window(field_pad, backward, extent))
        )
    return summed


def body(potential, tissue_mask, layer_index, source):
    extent = tissue_mask.shape
    mask_pad = padded(tissue_mask, (("gx", 1), ("gy", 2), ("gz", 0)), 1)
    layer_pad = padded(layer_index, (("gz", 0),), 1)
    selector = (layer_pad[:, None] == jnp.arange(LAYERS, dtype=jnp.int32)[None, :]).astype(
        jnp.float32
    )
    bulk_planes = jnp.dot(
        selector, tensor_table(LAYERS, bulk_long, bulk_trans), precision=lax.Precision.HIGHEST
    )
    intra_planes = jnp.dot(
        selector, tensor_table(LAYERS, intra_long, intra_trans), precision=lax.Precision.HIGHEST
    )
    tissue_pad = (mask_pad == 2).astype(jnp.float32)
    bath_pad = (mask_pad == 1).astype(jnp.float32)
    inside_pad = (mask_pad > 0).astype(jnp.float32)
    inside = window(inside_pad, (0, 0, 0), extent)
    bulk_edges = [
        edge_pair(
            cell_weight(bulk_planes, column, tissue_pad, bath_pad), inside_pad, offset, extent
        )
        for column, offset in enumerate(OFFSETS)
    ]
    intra_edges = [
        edge_pair(cell_weight(intra_planes, column, tissue_pad, None), tissue_pad, offset, extent)
        for column, offset in enumerate(OFFSETS)
    ]
    diagonal = jnp.zeros(extent, jnp.float32)
    for forward_edge, backward_edge in bulk_edges:
        diagonal = diagonal + forward_edge + backward_edge
    jacobi = inside / jnp.maximum(diagonal, 1.0)
    rhs = -operate(potential, intra_edges) + inside * source
    count, rhs_total = lax.psum((jnp.sum(inside), jnp.sum(rhs)), ("gx", "gy", "gz"))
    residual = rhs - inside * (rhs_total / count)
    solution = jnp.zeros(extent, jnp.float32)

    def coupled(current):
        scaled = jacobi * current
        image = operate(scaled, bulk_edges)
        scaled_total, cross_total, current_total, energy_total, image_total = lax.psum(
            (
                jnp.sum(scaled),
                jnp.sum(current * scaled),
                jnp.sum(current),
                jnp.sum(scaled * image),
                jnp.sum(image),
            ),
            ("gx", "gy", "gz"),
        )
        mean_value = scaled_total / count
        precond = scaled - inside * mean_value
        gamma_value = cross_total - mean_value * current_total
        delta_value = energy_total - mean_value * image_total
        return (precond, image, gamma_value, delta_value)

    precond, image, gamma_now, delta_now = coupled(residual)
    alpha = gamma_now / delta_now
    beta_value = jnp.zeros((), jnp.float32)
    direction = jnp.zeros(extent, jnp.float32)
    along = jnp.zeros(extent, jnp.float32)
    for step in range(ITERS):
        direction = precond + beta_value * direction
        along = image + beta_value * along
        solution = solution + alpha * direction
        residual = residual - alpha * along
        if step + 1 < ITERS:
            precond, image, gamma_next, delta_now = coupled(residual)
            beta_value = gamma_next / gamma_now
            alpha = gamma_next / (delta_now - beta_value * gamma_next / alpha)
            gamma_now = gamma_next
    return (solution, residual)


def solution(mesh):
    placed = (P("gz", "gx", "gy"), P("gz", "gx", "gy"), P("gz"), P("gz", "gx", "gy"))
    return jax.shard_map(
        body,
        mesh=mesh,
        in_specs=placed,
        out_specs=(P("gz", "gx", "gy"), P("gz", "gx", "gy")),
        check_vma=False,
    )
```

profile of v0, /device:TPU:0, one launch (start us, length us, event | category | flops | bytes accessed | tf_op | source)
XLA Modules:
  0.0 655.7 jit_solution(4429758000166814855)
XLA Ops:
  1.9 3.0 collective-permute-start.6
  7.0 4.3 collective-permute-start
  13.4 4.5 collective-permute-start.9
  22.1 2.4 collective-permute-done.8
  24.6 3.4 collective-permute-start.11
  29.5 4.6 collective-permute-start.2
  38.1 4.1 collective-permute-done.3
  52.6 40.0 %all-reduce.8 = (f32[]{:T(128)}, f32[]{:T(128)}) all-reduce(f32[]{:T(128)} %get-tuple-element.130, f32[]{:T(128)} %slice_reduce_fusion), channel_id=1, replica_groups=mesh['gx'=4,'gy'=4,'gz'=2] {'gx','gy','gz'}, use_global_device_ids=true, to_apply=%region_1.0 | all-reduce | flops 2 | bytes 16 | tf_op jit(solution)/shard_map/psum | solution.py:154
  93.9 3.3 fusion.452
  97.3 2.2 collective-permute-start.15
  100.9 4.2 collective-permute-done.14
  105.2 4.2 collective-permute-start.17
  111.9 4.4 collective-permute-done.16
  122.2 40.4 %all-reduce.7 = (f32[]{:T(128)}, f32[]{:T(128)}, f32[]{:T(128)}, f32[]{:T(128)}, f32[]{:T(128)}) all-reduce(f32[]{:T(128)} %get-tuple-element.40, f32[]{:T(128)} %get-tuple-element.39, f32[]{:T(128)} %get-tuple-element.41, f32[]{:T(128)} %get-tuple-element.38, ...), channel_id=1, replica_groups=mesh['gx'=4,'gy'=4,'gz'=2] {'gx','gy','gz'}, use_global_device_ids=true, to_apply=%region_5.0 | all-reduce | flops 5 | bytes 40 | tf_op jit(solution)/shard_map/psum | solution.py:161
  166.6 2.2 collective-permute-start.21
  170.1 4.2 collective-permute-done.20
  174.4 4.2 collective-permute-start.23
  181.1 4.4 collective-permute-done.22
  191.5 40.5 %all-reduce.6 = (f32[]{:T(128)}, f32[]{:T(128)}, f32[]{:T(128)}, f32[]{:T(128)}, f32[]{:T(128)}) all-reduce(f32[]{:T(128)} %get-tuple-element.35, f32[]{:T(128)} %get-tuple-element.34, f32[]{:T(128)} %get-tuple-element.36, f32[]{:T(128)} %get-tuple-element.33, ...), channel_id=1, replica_groups=mesh['gx'=4,'gy'=4,'gz'=2] {'gx','gy','gz'}, use_global_device_ids=true, to_apply=%region_15.0 | all-reduce | flops 5 | bytes 40 | tf_op jit(solution)/shard_map/psum | solution.py:161
  236.0 2.2 collective-permute-start.27
  239.5 4.2 collective-permute-done.26
  243.8 4.2 collective-permute-start.29
  250.5 4.4 collective-permute-done.28
  260.8 40.6 %all-reduce.5 = (f32[]{:T(128)}, f32[]{:T(128)}, f32[]{:T(128)}, f32[]{:T(128)}, f32[]{:T(128)}) all-reduce(f32[]{:T(128)} %get-tuple-element.30, f32[]{:T(128)} %get-tuple-element.29, f32[]{:T(128)} %get-tuple-element.31, f32[]{:T(128)} %get-tuple-element.28, ...), channel_id=1, replica_groups=mesh['gx'=4,'gy'=4,'gz'=2] {'gx','gy','gz'}, use_global_device_ids=true, to_apply=%region_25.0 | all-reduce | flops 5 | bytes 40 | tf_op jit(solution)/shard_map/psum | solution.py:161
  305.4 2.1 collective-permute-start.33
  308.9 4.2 collective-permute-done.32
  313.2 4.2 collective-permute-start.35
  319.9 4.4 collective-permute-done.34
  330.2 40.6 %all-reduce.4 = (f32[]{:T(128)}, f32[]{:T(128)}, f32[]{:T(128)}, f32[]{:T(128)}, f32[]{:T(128)}) all-reduce(f32[]{:T(128)} %get-tuple-element.25, f32[]{:T(128)} %get-tuple-element.24, f32[]{:T(128)} %get-tuple-element.26, f32[]{:T(128)} %get-tuple-element.23, ...), channel_id=1, replica_groups=mesh['gx'=4,'gy'=4,'gz'=2] {'gx','gy','gz'}, use_global_device_ids=true, to_apply=%region_35.0 | all-reduce | flops 5 | bytes 40 | tf_op jit(solution)/shard_map/psum | solution.py:161
  374.9 2.1 collective-permute-start.39
  378.2 4.2 collective-permute-done.38
  382.6 4.2 collective-permute-start.41
  389.3 4.4 collective-permute-done.40
  399.6 40.7 %all-reduce.3 = (f32[]{:T(128)}, f32[]{:T(128)}, f32[]{:T(128)}, f32[]{:T(128)}, f32[]{:T(128)}) all-reduce(f32[]{:T(128)} %get-tuple-element.20, f32[]{:T(128)} %get-tuple-element.19, f32[]{:T(128)} %get-tuple-element.21, f32[]{:T(128)} %get-tuple-element.18, ...), channel_id=1, replica_groups=mesh['gx'=4,'gy'=4,'gz'=2] {'gx','gy','gz'}, use_global_device_ids=true, to_apply=%region_45.0 | all-reduce | flops 5 | bytes 40 | tf_op jit(solution)/shard_map/psum | solution.py:161
  444.3 2.0 collective-permute-start.45
  447.6 4.2 collective-permute-done.44
  452.0 4.2 collective-permute-start.47
  458.6 4.4 collective-permute-done.46
  469.0 40.7 %all-reduce.2 = (f32[]{:T(128)}, f32[]{:T(128)}, f32[]{:T(128)}, f32[]{:T(128)}, f32[]{:T(128)}) all-reduce(f32[]{:T(128)} %get-tuple-element.15, f32[]{:T(128)} %get-tuple-element.14, f32[]{:T(128)} %get-tuple-element.16, f32[]{:T(128)} %get-tuple-element.13, ...), channel_id=1, replica_groups=mesh['gx'=4,'gy'=4,'gz'=2] {'gx','gy','gz'}, use_global_device_ids=true, to_apply=%region_55.0 | all-reduce | flops 5 | bytes 40 | tf_op jit(solution)/shard_map/psum | solution.py:161
  517.1 4.2 collective-permute-done.50
  521.4 4.2 collective-permute-start.53
  528.1 4.4 collective-permute-done.52
  539.1 40.7 %all-reduce.1 = (f32[]{:T(128)}, f32[]{:T(128)}, f32[]{:T(128)}, f32[]{:T(128)}, f32[]{:T(128)}) all-reduce(f32[]{:T(128)} %get-tuple-element.10, f32[]{:T(128)} %get-tuple-element.9, f32[]{:T(128)} %get-tuple-element.11, f32[]{:T(128)} %get-tuple-element.8, f32[]{:T(128)} %get-tuple-element.7), channel_id=1, replica_groups=mesh['gx'=4,'gy'=4,'gz'=2] {'gx','gy','gz'}, use_global_device_ids=true, to_apply=%region_65.0 | all-reduce | flops 5 | bytes 40 | tf_op jit(solution)/shard_map/psum | solution.py:161
  584.7 2.0 collective-permute-start.57
  588.1 4.2 collective-permute-done.56
  592.4 4.2 collective-permute-start.59
  599.1 4.4 collective-permute-done.58
  609.5 40.7 %all-reduce = (f32[]{:T(128)}, f32[]{:T(128)}, f32[]{:T(128)}, f32[]{:T(128)}, f32[]{:T(128)}) all-reduce(f32[]{:T(128)} %get-tuple-element.5, f32[]{:T(128)} %get-tuple-element.4, f32[]{:T(128)} %get-tuple-element.6, f32[]{:T(128)} %get-tuple-element.3, f32[]{:T(128)} %get-tuple-element.2), channel_id=1, replica_groups=mesh['gx'=4,'gy'=4,'gz'=2] {'gx','gy','gz'}, use_global_device_ids=true, to_apply=%region_75.0 | all-reduce | flops 5 | bytes 40 | tf_op jit(solution)/shard_map/psum | solution.py:161
  (194 shorter events, 109.6 us)
Async XLA Ops:
  1.9 17.1 %collective-permute-start.6 = (s32[1]{0:T(128)}, s32[1]{0:T(128)}, u32[]{:S(2)}, u32[]{:S(2)}) collective-permute-start(s32[1]{0:T(128)} %get-tuple-element.268), channel_id=1, source_target_pairs={{0,1},{2,3},{4,5},{6,7},{8,9},{10,11},{12,13},{14,15},{16,17},{18,... | collective-permute-start | bytes 20 | tf_op jit(solution)/shard_map/ppermute | solution.py:37
  4.9 15.4 %collective-permute-start.7 = (s32[1]{0:T(128)}, s32[1]{0:T(128)}, u32[]{:S(2)}, u32[]{:S(2)}) collective-permute-start(s32[1]{0:T(128)} %get-tuple-element.269), channel_id=1, source_target_pairs={{1,0},{3,2},{5,4},{7,6},{9,8},{11,10},{13,12},{15,14},{17,16},{19,... | collective-permute-start | bytes 20 | tf_op jit(solution)/shard_map/ppermute | solution.py:38
  7.0 22.4 %collective-permute-start = (s32[8,1,128]{2,1,0:T(1,128)S(1)}, s32[8,1,128]{2,1,0:T(1,128)S(1)}, u32[]{:S(2)}, u32[]{:S(2)}) collective-permute-start(s32[8,1,128]{2,1,0:T(1,128)S(1)} %get-tuple-element.232), channel_id=1, source_target_pairs={{0,8},{8,16},{16,24},{1,9},{9,17},{17,25},{2,10},{10,18},{18,26},{... | collective-permute-start | bytes 12296 | tf_op jit(solution)/shard_map/ppermute | solution.py:37
  11.3 18.1 %collective-permute-start.1 = (s32[8,1,128]{2,1,0:T(1,128)S(1)}, s32[8,1,128]{2,1,0:T(1,128)S(1)}, u32[]{:S(2)}, u32[]{:S(2)}) collective-permute-start(s32[8,1,128]{2,1,0:T(1,128)S(1)} %get-tuple-element.233), channel_id=1, source_target_pairs={{8,0},{16,8},{24,16},{9,1},{17,9},{25,17},{10,2},{18,10},{26,18},{... | collective-permute-start | bytes 12296 | tf_op jit(solution)/shard_map/ppermute | solution.py:38
  13.4 8.7 %collective-permute-start.9 = (f32[8,1,128]{2,1,0:T(1,128)S(1)}, f32[8,1,128]{2,1,0:T(1,128)S(1)}, u32[]{:S(2)}, u32[]{:S(2)}) collective-permute-start(f32[8,1,128]{2,1,0:T(1,128)S(1)} %get-tuple-element.230), channel_id=1, source_target_pairs={{0,8},{8,16},{16,24},{1,9},{9,17},{17,25},{2,10},{10,18},{18,26},{... | collective-permute-start | bytes 12296 | tf_op jit(solution)/shard_map/ppermute | solution.py:37
  19.0 5.5 collective-permute-start.8
  24.6 10.7 %collective-permute-start.11 = (f32[8,26,1]{2,1,0:T(8,128)S(1)}, f32[8,26,1]{2,1,0:T(8,128)S(1)}, u32[]{:S(2)}, u32[]{:S(2)}) collective-permute-start(f32[8,26,1]{2,1,0:T(8,128)S(1)} %get-tuple-element.192), channel_id=1, source_target_pairs={{0,2},{2,4},{4,6},{1,3},{3,5},{5,7},{8,10},{10,12},{12,14},{9,11},... | collective-permute-start | bytes 2504 | tf_op jit(solution)/shard_map/ppermute | solution.py:37
  28.1 7.3 %collective-permute-start.10 = (f32[8,26,1]{2,1,0:T(8,128)S(1)}, f32[8,26,1]{2,1,0:T(8,128)S(1)}, u32[]{:S(2)}, u32[]{:S(2)}) collective-permute-start(f32[8,26,1]{2,1,0:T(8,128)S(1)} %get-tuple-element.193), channel_id=1, source_target_pairs={{2,0},{4,2},{6,4},{3,1},{5,3},{7,5},{10,8},{12,10},{14,12},{11,9},... | collective-permute-start | bytes 2504 | tf_op jit(solution)/shard_map/ppermute | solution.py:38
  29.5 8.6 %collective-permute-start.2 = (s32[8,26,1]{2,1,0:T(8,128)S(1)}, s32[8,26,1]{2,1,0:T(8,128)S(1)}, u32[]{:S(2)}, u32[]{:S(2)}) collective-permute-start(s32[8,26,1]{2,1,0:T(8,128)S(1)} %get-tuple-element.194), channel_id=1, source_target_pairs={{0,2},{2,4},{4,6},{1,3},{3,5},{5,7},{8,10},{10,12},{12,14},{9,11},... | collective-permute-start | bytes 2504 | tf_op jit(solution)/shard_map/ppermute | solution.py:37
  34.1 8.1 %collective-permute-start.3 = (s32[8,26,1]{2,1,0:T(8,128)S(1)}, s32[8,26,1]{2,1,0:T(8,128)S(1)}, u32[]{:S(2)}, u32[]{:S(2)}) collective-permute-start(s32[8,26,1]{2,1,0:T(8,128)S(1)} %get-tuple-element.195), channel_id=1, source_target_pairs={{2,0},{4,2},{6,4},{3,1},{5,3},{7,5},{10,8},{12,10},{14,12},{11,9},... | collective-permute-start | bytes 2504 | tf_op jit(solution)/shard_map/ppermute | solution.py:38
  35.5 14.3 %collective-permute-start.13 = (f32[1,26,130]{2,1,0:T(8,128)S(1)}, f32[1,26,130]{2,1,0:T(8,128)S(1)}, u32[]{:S(2)}, u32[]{:S(2)}) collective-permute-start(f32[1,26,130]{2,1,0:T(8,128)S(1)} %get-tuple-element.170), channel_id=1, source_target_pairs={{0,1},{2,3},{4,5},{6,7},{8,9},{10,11},{12,13},{14,15},{16,17},{18,... | collective-permute-start | bytes 40568 | tf_op jit(solution)/shard_map/ppermute | solution.py:37
  36.8 13.0 %collective-permute-start.12 = (f32[1,26,130]{2,1,0:T(8,128)S(1)}, f32[1,26,130]{2,1,0:T(8,128)S(1)}, u32[]{:S(2)}, u32[]{:S(2)}) collective-permute-start(f32[1,26,130]{2,1,0:T(8,128)S(1)} %get-tuple-element.171), channel_id=1, source_target_pairs={{1,0},{3,2},{5,4},{7,6},{9,8},{11,10},{13,12},{15,14},{17,16},{19,... | collective-permute-start | bytes 40568 | tf_op jit(solution)/shard_map/ppermute | solution.py:38
  43.6 3.1 collective-permute-start.5
  97.3 3.6 collective-permute-start.15
  99.6 5.5 collective-permute-start.14
  105.2 6.7 %collective-permute-start.17 = (f32[8,26,1]{2,1,0:T(8,128)S(1)}, f32[8,26,1]{2,1,0:T(8,128)S(1)}, u32[]{:S(2)}, u32[]{:S(2)}) collective-permute-start(f32[8,26,1]{2,1,0:T(8,128)S(1)} %get-tuple-element.190), channel_id=1, source_target_pairs={{0,2},{2,4},{4,6},{1,3},{3,5},{5,7},{8,10},{10,12},{12,14},{9,11},... | collective-permute-start | bytes 2504 | tf_op jit(solution)/shard_map/ppermute | solution.py:37
  109.4 6.9 %collective-permute-start.16 = (f32[8,26,1]{2,1,0:T(8,128)S(1)}, f32[8,26,1]{2,1,0:T(8,128)S(1)}, u32[]{:S(2)}, u32[]{:S(2)}) collective-permute-start(f32[8,26,1]{2,1,0:T(8,128)S(1)} %get-tuple-element.191), channel_id=1, source_target_pairs={{2,0},{4,2},{6,4},{3,1},{5,3},{7,5},{10,8},{12,10},{14,12},{11,9},... | collective-permute-start | bytes 2504 | tf_op jit(solution)/shard_map/ppermute | solution.py:38
  117.6 3.1 collective-permute-start.18
  166.6 3.5 collective-permute-start.21
  168.8 5.5 collective-permute-start.20
  174.4 6.7 %collective-permute-start.23 = (f32[8,26,1]{2,1,0:T(8,128)S(1)}, f32[8,26,1]{2,1,0:T(8,128)S(1)}, u32[]{:S(2)}, u32[]{:S(2)}) collective-permute-start(f32[8,26,1]{2,1,0:T(8,128)S(1)} %get-tuple-element.188), channel_id=1, source_target_pairs={{0,2},{2,4},{4,6},{1,3},{3,5},{5,7},{8,10},{10,12},{12,14},{9,11},... | collective-permute-start | bytes 2504 | tf_op jit(solution)/shard_map/ppermute | solution.py:37
  178.6 6.9 %collective-permute-start.22 = (f32[8,26,1]{2,1,0:T(8,128)S(1)}, f32[8,26,1]{2,1,0:T(8,128)S(1)}, u32[]{:S(2)}, u32[]{:S(2)}) collective-permute-start(f32[8,26,1]{2,1,0:T(8,128)S(1)} %get-tuple-element.189), channel_id=1, source_target_pairs={{2,0},{4,2},{6,4},{3,1},{5,3},{7,5},{10,8},{12,10},{14,12},{11,9},... | collective-permute-start | bytes 2504 | tf_op jit(solution)/shard_map/ppermute | solution.py:38
  186.9 3.1 collective-permute-start.24
  236.0 3.5 collective-permute-start.27
  238.2 5.5 collective-permute-start.26
  243.8 6.7 %collective-permute-start.29 = (f32[8,26,1]{2,1,0:T(8,128)S(1)}, f32[8,26,1]{2,1,0:T(8,128)S(1)}, u32[]{:S(2)}, u32[]{:S(2)}) collective-permute-start(f32[8,26,1]{2,1,0:T(8,128)S(1)} %get-tuple-element.186), channel_id=1, source_target_pairs={{0,2},{2,4},{4,6},{1,3},{3,5},{5,7},{8,10},{10,12},{12,14},{9,11},... | collective-permute-start | bytes 2504 | tf_op jit(solution)/shard_map/ppermute | solution.py:37
  248.0 6.9 %collective-permute-start.28 = (f32[8,26,1]{2,1,0:T(8,128)S(1)}, f32[8,26,1]{2,1,0:T(8,128)S(1)}, u32[]{:S(2)}, u32[]{:S(2)}) collective-permute-start(f32[8,26,1]{2,1,0:T(8,128)S(1)} %get-tuple-element.187), channel_id=1, source_target_pairs={{2,0},{4,2},{6,4},{3,1},{5,3},{7,5},{10,8},{12,10},{14,12},{11,9},... | collective-permute-start | bytes 2504 | tf_op jit(solution)/shard_map/ppermute | solution.py:38
  256.3 3.1 collective-permute-start.30
  305.4 3.4 collective-permute-start.33
  307.6 5.5 collective-permute-start.32
  313.2 6.7 %collective-permute-start.35 = (f32[8,26,1]{2,1,0:T(8,128)S(1)}, f32[8,26,1]{2,1,0:T(8,128)S(1)}, u32[]{:S(2)}, u32[]{:S(2)}) collective-permute-start(f32[8,26,1]{2,1,0:T(8,128)S(1)} %get-tuple-element.184), channel_id=1, source_target_pairs={{0,2},{2,4},{4,6},{1,3},{3,5},{5,7},{8,10},{10,12},{12,14},{9,11},... | collective-permute-start | bytes 2504 | tf_op jit(solution)/shard_map/ppermute | solution.py:37
  317.4 6.9 %collective-permute-start.34 = (f32[8,26,1]{2,1,0:T(8,128)S(1)}, f32[8,26,1]{2,1,0:T(8,128)S(1)}, u32[]{:S(2)}, u32[]{:S(2)}) collective-permute-start(f32[8,26,1]{2,1,0:T(8,128)S(1)} %get-tuple-element.185), channel_id=1, source_target_pairs={{2,0},{4,2},{6,4},{3,1},{5,3},{7,5},{10,8},{12,10},{14,12},{11,9},... | collective-permute-start | bytes 2504 | tf_op jit(solution)/shard_map/ppermute | solution.py:38
  374.9 3.4 collective-permute-start.39
  376.9 5.5 collective-permute-start.38
  382.6 6.7 %collective-permute-start.41 = (f32[8,26,1]{2,1,0:T(8,128)S(1)}, f32[8,26,1]{2,1,0:T(8,128)S(1)}, u32[]{:S(2)}, u32[]{:S(2)}) collective-permute-start(f32[8,26,1]{2,1,0:T(8,128)S(1)} %get-tuple-element.182), channel_id=1, source_target_pairs={{0,2},{2,4},{4,6},{1,3},{3,5},{5,7},{8,10},{10,12},{12,14},{9,11},... | collective-permute-start | bytes 2504 | tf_op jit(solution)/shard_map/ppermute | solution.py:37
  386.8 6.9 %collective-permute-start.40 = (f32[8,26,1]{2,1,0:T(8,128)S(1)}, f32[8,26,1]{2,1,0:T(8,128)S(1)}, u32[]{:S(2)}, u32[]{:S(2)}) collective-permute-start(f32[8,26,1]{2,1,0:T(8,128)S(1)} %get-tuple-element.183), channel_id=1, source_target_pairs={{2,0},{4,2},{6,4},{3,1},{5,3},{7,5},{10,8},{12,10},{14,12},{11,9},... | collective-permute-start | bytes 2504 | tf_op jit(solution)/shard_map/ppermute | solution.py:38
  444.3 3.4 collective-permute-start.45
  446.3 5.5 collective-permute-start.44
  452.0 6.7 %collective-permute-start.47 = (f32[8,26,1]{2,1,0:T(8,128)S(1)}, f32[8,26,1]{2,1,0:T(8,128)S(1)}, u32[]{:S(2)}, u32[]{:S(2)}) collective-permute-start(f32[8,26,1]{2,1,0:T(8,128)S(1)} %get-tuple-element.180), channel_id=1, source_target_pairs={{0,2},{2,4},{4,6},{1,3},{3,5},{5,7},{8,10},{10,12},{12,14},{9,11},... | collective-permute-start | bytes 2504 | tf_op jit(solution)/shard_map/ppermute | solution.py:37
  456.2 6.9 %collective-permute-start.46 = (f32[8,26,1]{2,1,0:T(8,128)S(1)}, f32[8,26,1]{2,1,0:T(8,128)S(1)}, u32[]{:S(2)}, u32[]{:S(2)}) collective-permute-start(f32[8,26,1]{2,1,0:T(8,128)S(1)} %get-tuple-element.181), channel_id=1, source_target_pairs={{2,0},{4,2},{6,4},{3,1},{5,3},{7,5},{10,8},{12,10},{14,12},{11,9},... | collective-permute-start | bytes 2504 | tf_op jit(solution)/shard_map/ppermute | solution.py:38
  513.7 3.4 collective-permute-start.51
  515.8 5.5 collective-permute-start.50
  521.4 6.7 %collective-permute-start.53 = (f32[8,26,1]{2,1,0:T(8,128)S(1)}, f32[8,26,1]{2,1,0:T(8,128)S(1)}, u32[]{:S(2)}, u32[]{:S(2)}) collective-permute-start(f32[8,26,1]{2,1,0:T(8,128)S(1)} %get-tuple-element.178), channel_id=1, source_target_pairs={{0,2},{2,4},{4,6},{1,3},{3,5},{5,7},{8,10},{10,12},{12,14},{9,11},... | collective-permute-start | bytes 2504 | tf_op jit(solution)/shard_map/ppermute | solution.py:37
  525.6 6.9 %collective-permute-start.52 = (f32[8,26,1]{2,1,0:T(8,128)S(1)}, f32[8,26,1]{2,1,0:T(8,128)S(1)}, u32[]{:S(2)}, u32[]{:S(2)}) collective-permute-start(f32[8,26,1]{2,1,0:T(8,128)S(1)} %get-tuple-element.179), channel_id=1, source_target_pairs={{2,0},{4,2},{6,4},{3,1},{5,3},{7,5},{10,8},{12,10},{14,12},{11,9},... | collective-permute-start | bytes 2504 | tf_op jit(solution)/shard_map/ppermute | solution.py:38
  584.7 3.4 collective-permute-start.57
  586.8 5.5 collective-permute-start.56
  592.4 6.7 %collective-permute-start.59 = (f32[8,26,1]{2,1,0:T(8,128)S(1)}, f32[8,26,1]{2,1,0:T(8,128)S(1)}, u32[]{:S(2)}, u32[]{:S(2)}) collective-permute-start(f32[8,26,1]{2,1,0:T(8,128)S(1)} %get-tuple-element.176), channel_id=1, source_target_pairs={{0,2},{2,4},{4,6},{1,3},{3,5},{5,7},{8,10},{10,12},{12,14},{9,11},... | collective-permute-start | bytes 2504 | tf_op jit(solution)/shard_map/ppermute | solution.py:37
  596.6 6.9 %collective-permute-start.58 = (f32[8,26,1]{2,1,0:T(8,128)S(1)}, f32[8,26,1]{2,1,0:T(8,128)S(1)}, u32[]{:S(2)}, u32[]{:S(2)}) collective-permute-start(f32[8,26,1]{2,1,0:T(8,128)S(1)} %get-tuple-element.177), channel_id=1, source_target_pairs={{2,0},{4,2},{6,4},{3,1},{5,3},{7,5},{10,8},{12,10},{14,12},{11,9},... | collective-permute-start | bytes 2504 | tf_op jit(solution)/shard_map/ppermute | solution.py:38
  (18 other events, 53.3 us)
where the time goes:
time: 659 us; the launch traced here: 656 us
  blocking collectives  365 us (55%)
  starting transfers between devices  123 us (19%)
  waiting for transfers between devices  99 us (15%)
  between operations  34.8 us (5%)
  other arithmetic  28.8 us (4%)
    psum x8, blocking collectives, coupled(): lax.psum((jnp.sum(scaled), jnp.sum(current * scaled), jnp.sum(current), j...  325 us
    ppermute x31, waiting for transfers between devices, padded(): after = lax.ppermute(first, axis, down)  89.5 us
    ppermute x31, starting transfers between devices, padded(): before = lax.ppermute(last, axis, up)  83 us
    ppermute x31, starting transfers between devices, padded(): after = lax.ppermute(first, axis, down)  40.2 us
    psum x1, blocking collectives, body(): lax.psum((jnp.sum(inside), jnp.sum(rhs)), ('gx', 'gy', 'gz'))  40 us
  transfers between devices with their start and end apart: 62, of which 35 were waited for; matrix products, arithmetic and copies ran while one was open for 1% of the time, Pallas kernels for 0%

commit v1 on v0

v1 whole, which is shorter than its diff:
```python
import functools
import math

import jax
import jax.numpy as jnp
import numpy as np
from jax import lax
from jax.experimental import pallas as pl
from jax.experimental.pallas import tpu as pltpu
from jax.sharding import PartitionSpec as P

ITERS = 8
LAYERS = 16
HALO = ITERS + 1
LANES = 128
SLOT = 16
TOP = 16
VECS = ITERS + 1
SUMS = VECS * VECS

OFFSETS = [
    (0, 1, 0),
    (0, 0, 1),
    (1, 0, 0),
    (0, 1, 1),
    (0, 1, -1),
    (1, 1, 0),
    (-1, 1, 0),
    (1, 0, 1),
    (-1, 0, 1),
]
bulk_long = 7.99
bulk_trans = 2.55
intra_long = 1.74
intra_trans = 0.19
bath_sigma = 5.0

VMEM = pl.BlockSpec(memory_space=pltpu.VMEM)
SMEM = pl.BlockSpec(memory_space=pltpu.SMEM)


def tensor_table(layers, longitudinal, transverse):
    depth = np.arange(layers, dtype=np.float64) / (layers - 1)
    helix = math.pi / 3.0 * (1.0 - 2.0 * depth)
    tilted = 0.35 * np.cos(math.pi * depth)
    fiber_x = np.cos(tilted) * np.cos(helix)
    fiber_y = np.cos(tilted) * np.sin(helix)
    fiber_z = np.sin(tilted)
    spread = longitudinal - transverse
    s_xx = transverse + spread * fiber_x * fiber_x
    s_yy = transverse + spread * fiber_y * fiber_y
    s_zz = transverse + spread * fiber_z * fiber_z
    s_xy = spread * fiber_x * fiber_y
    s_xz = spread * fiber_x * fiber_z
    s_yz = spread * fiber_y * fiber_z
    columns = [
        s_xx - np.abs(s_xy) - np.abs(s_xz),
        s_yy - np.abs(s_xy) - np.abs(s_yz),
        s_zz - np.abs(s_xz) - np.abs(s_yz),
        np.maximum(s_xy, 0.0),
        np.maximum(-s_xy, 0.0),
        np.maximum(s_xz, 0.0),
        np.maximum(-s_xz, 0.0),
        np.maximum(s_yz, 0.0),
        np.maximum(-s_yz, 0.0),
    ]
    return np.stack(columns, axis=1).astype(np.float32)


def lane_iota(shape):
    return lax.broadcasted_iota(jnp.int32, shape, len(shape) - 1)


def roll(value, shift, axis=-1):
    axis = axis % value.ndim
    shift = shift % value.shape[axis]
    return value if shift == 0 else pltpu.roll(value, shift, axis)


def pack_y(geometry, offs, *refs):
    pieces, own_count, planes, rows, full = geometry
    piece_refs = refs[: len(pieces)]
    joined, left, right, sums = refs[len(pieces) :]
    for number, length in enumerate(pieces):
        for plane in range(length):
            at = offs[number] + plane
            for field in range(3):
                joined[field, at] = piece_refs[number][field, plane]
    lane = lane_iota((rows, LANES))
    count = jnp.zeros((rows, LANES), jnp.float32)
    total = jnp.zeros((rows, LANES), jnp.float32)
    for number, length in enumerate(pieces):
        if full or number == own_count:
            for plane in range(length):
                inside = jnp.minimum(piece_refs[number][2, plane], 1.0)
                count = count + inside
                total = total + inside * piece_refs[number][1, plane]
    sums[...] = jnp.zeros((8, LANES), jnp.float32)
    sums[0:1] = jnp.sum(count, axis=0, keepdims=True)
    sums[1:2] = jnp.sum(total, axis=0, keepdims=True)
    groups = -(-planes // 8)
    for field in range(3):
        for group in range(groups):
            to_left = jnp.zeros((rows, LANES), jnp.float32)
            to_right = jnp.zeros((rows, LANES), jnp.float32)
            for slot in range(min(8, planes - 8 * group)):
                value = joined[field, 8 * group + slot]
                here = (lane >= SLOT * slot) & (lane < SLOT * (slot + 1))
                to_left = jnp.where(here, roll(value, SLOT * slot), to_left)
                to_right = jnp.where(here, roll(value, SLOT * (slot + 1)), to_right)
            base = (field * groups + group) * rows
            left[base : base + rows] = to_left
            right[base : base + rows] = to_right
    last = 3 * groups * rows
    left[last : last + 8] = sums[...]
    right[last : last + 8] = sums[...]


def pack_x(geometry, joined, from_left, from_right, *refs):
    planes, rows, others = geometry
    other_refs = refs[:others]
    upper, lower, sums = refs[others:]
    groups = -(-planes // 8)
    last = 3 * groups * rows
    total = from_left[last : last + 8] + from_right[last : last + 8]
    for ref in other_refs:
        total = total + ref[...]
    sums[...] = total
    row = 0
    for field in range(3):
        for plane in range(planes):
            upper[row : row + HALO] = joined[field, plane, 0:HALO]
            lower[row : row + HALO] = joined[field, plane, rows - HALO : rows]
            row += HALO
    for strip in (from_left, from_right):
        for block in range(3 * groups):
            base = block * rows
            upper[row : row + HALO] = strip[base : base + HALO]
            lower[row : row + HALO] = strip[base + rows - HALO : base + rows]
            row += HALO
    row = -(-row // 8) * 8
    upper[row : row + 8] = total
    lower[row : row + 8] = total


def x_rows(planes):
    groups = -(-planes // 8)
    return -(-HALO * 3 * (planes + 2 * groups) // 8) * 8


def krylov(geometry, info, offs, table, *refs):
    pieces, planes, own_planes, rows, others = geometry
    layer_refs = refs[: len(pieces)]
    refs = refs[len(pieces) :]
    joined, from_left, from_right, from_upper, from_lower, total_in = refs[:6]
    refs = refs[6:]
    gram, basis, metric, extra = refs[:4]
    layer, pot, med, edge, edge_r, vec, vec_l, vec_r, jac, kap, acc, rowsum = refs[4:]
    groups = -(-planes // 8)
    tiles = 2
    high = TOP + rows + 16
    inner = (rows + 16) // 8
    lane = lane_iota((8, LANES))
    has_left, has_right, has_upper, has_lower, first = (info[i] for i in range(5))

    layer[0] = 0
    layer[planes + 1] = 0
    for number, length in enumerate(pieces):
        for plane in range(length):
            layer[offs[number] + plane + 1] = layer_refs[number][plane]

    count = jnp.sum(total_in[0:1], axis=1, keepdims=True)
    mean = jnp.sum(total_in[1:2], axis=1, keepdims=True) / count

    zero = jnp.zeros((8, LANES), jnp.float32)
    as_float = lambda flag: flag.astype(jnp.float32)
    keep_left = as_float(has_left)
    keep_right = as_float(has_right)
    keep_upper = as_float(has_upper)
    keep_lower = as_float(has_lower)
    for buffer in (pot, med):
        for copy in range(3):
            for tile in range(tiles):
                for plane in (0, planes + 1):
                    for at in range(0, high, 8):
                        buffer[copy, tile, plane, at : at + 8] = zero

    def place(buffer, tile, plane, at, value):
        size = value.shape[0]
        buffer[0, tile, plane, at : at + size] = value
        buffer[1, tile, plane, at : at + size] = roll(value, LANES - 1)
        buffer[2, tile, plane, at : at + size] = roll(value, 1)

    half = 3 * planes * HALO
    for slot_group in range(groups):
        for slot in range(min(8, planes - 8 * slot_group)):
            z = 8 * slot_group + slot
            for kind, field in enumerate((0, 2)):
                buffer = (pot, med)[kind]
                block = field * groups + slot_group

                def split(own, strip_l, strip_r, keep):
                    size = own.shape[0]
                    ln = lane_iota((size, LANES))
                    a = roll(strip_l, LANES - SLOT * slot)
                    b = roll(strip_r, LANES - SLOT * (slot + 1))
                    if kind == 1:
                        a, b = a * keep_left, b * keep_right
                    low = jnp.where(ln < SLOT, a, roll(own, SLOT))
                    up = jnp.where(ln >= LANES - SLOT, b, roll(own, LANES - SLOT))
                    if kind == 1 and keep is not None:
                        low, up = low * keep, up * keep
                    return low, up

                own = joined[field, z]
                strip_l = from_left[block * rows : (block + 1) * rows]
                strip_r = from_right[block * rows : (block + 1) * rows]
                for tile, value in enumerate(split(own, strip_l, strip_r, None)):
                    place(buffer, tile, z + 1, TOP, value)
                for strip, keep, at in (
                    (from_upper, keep_upper, TOP - HALO),
                    (from_lower, keep_lower, TOP + rows),
                ):
                    r0 = (field * planes + z) * HALO
                    r1 = half + block * HALO
                    r2 = half + (3 * groups + block) * HALO
                    values = split(
                        strip[r0 : r0 + HALO], strip[r1 : r1 + HALO], strip[r2 : r2 + HALO], keep
                    )
                    for tile, value in enumerate(values):
                        for copy in range(3):
                            edge_at = 0 if at < TOP else high - 8
                            buffer[copy, tile, z + 1, edge_at : edge_at + 8] = zero
                        place(buffer, tile, z + 1, at, value)

    for slot_group in range(groups):
        for slot in range(min(8, planes - 8 * slot_group)):
            z = 8 * slot_group + slot
            block = groups + slot_group

            def spread(own, strip_l, strip_r):
                ln = lane_iota(own.shape)
                a = roll(strip_l, LANES - SLOT * slot)
                b = roll(strip_r, LANES - SLOT * (slot + 1))
                low = jnp.where(ln < SLOT, a, roll(own, SLOT))
                up = jnp.where(ln >= LANES - SLOT, b, roll(own, LANES - SLOT))
                return low, up

            own = joined[1, z]
            strip_l = from_left[block * rows : (block + 1) * rows]
            strip_r = from_right[block * rows : (block + 1) * rows]
            for tile, value in enumerate(spread(own, strip_l, strip_r)):
                vec[2, tile, z + 1, TOP : TOP + rows] = value
            for strip, at, skip in ((from_upper, TOP - 8, 1), (from_lower, TOP + rows, 0)):
                r0 = (planes + z) * HALO + skip
                r1 = half + block * HALO + skip
                r2 = half + (3 * groups + block) * HALO + skip
                values = spread(strip[r0 : r0 + 8], strip[r1 : r1 + 8], strip[r2 : r2 + 8])
                for tile, value in enumerate(values):
                    vec[2, tile, z + 1, at : at + 8] = value

    shifted = {0: 0, 1: 1, -1: 2}
    rolled = [column for column, offset in enumerate(OFFSETS) if offset[2]]

    for column, (dz, _, dy) in enumerate(OFFSETS):
        if dz:
            plane = 0 if dz > 0 else planes + 1
            for tile in range(tiles):
                for at in range(0, 8 * (inner + 1), 8):
                    if dy:
                        edge_r[rolled.index(column), tile, plane, at : at + 8] = zero
                    else:
                        edge[column, tile, plane, at : at + 8] = zero

    def edges_of(z, carry):
        here = layer[z + 1] * 18
        for tile in range(tiles):
            for block in range(inner + 1):
                at = 8 * block
                m = med[0, tile, z + 1, at : at + 8]
                inside = jnp.minimum(m, 1.0)
                tissue = jnp.maximum(m - 1.0, 0.0)
                bath = (inside - tissue) * (0.5 * bath_sigma)
                for column, (dz, dx, dy) in enumerate(OFFSETS):
                    there = layer[z + 1 + dz] * 18
                    if block == 0 and dx < 0:
                        raise ValueError("row order")
                    n = med[shifted[dy], tile, z + 1 + dz, at + dx : at + dx + 8]
                    n_in = jnp.minimum(n, 1.0)
                    n_ti = jnp.maximum(n - 1.0, 0.0)
                    weight = tissue * table[here + column] + n_ti * table[there + column]
                    if column < 3:
                        weight = weight + (bath + (n_in - n_ti) * (0.5 * bath_sigma))
                    weight = (inside * n_in) * weight
                    edge[column, tile, z + 1, at : at + 8] = weight
                    if dy:
                        edge_r[rolled.index(column), tile, z + 1, at : at + 8] = roll(weight, dy)
        return carry

    lax.fori_loop(0, planes, edges_of, 0)

    for copy in range(3):
        for tile in range(tiles):
            for plane in (0, planes + 1):
                for at in range(0, high, 8):
                    vec[copy, tile, plane, at : at + 8] = zero
                    if copy < 2:
                        vec_l[copy, tile, plane, at : at + 8] = zero
                        vec_r[copy, tile, plane, at : at + 8] = zero
            for plane in range(1, planes + 1):
                for at in (0, high - 8):
                    vec[copy, tile, plane, at : at + 8] = zero
                    if copy < 2:
                        vec_l[copy, tile, plane, at : at + 8] = zero
                        vec_r[copy, tile, plane, at : at + 8] = zero

    def backward(column, tile, z, at):
        dz, dx, dy = OFFSETS[column]
        if dy:
            return edge_r[rolled.index(column), tile, z + 1 - dz, at - dx : at - dx + 8]
        return edge[column, tile, z + 1 - dz, at - dx : at - dx + 8]

    def start_of(z, carry):
        here = layer[z + 1] * 18 + 9
        for tile in range(tiles):
            for block in range(inner):
                at = 8 + 8 * block
                m = med[0, tile, z + 1, at : at + 8]
                inside = jnp.minimum(m, 1.0)
                tissue = jnp.maximum(m - 1.0, 0.0)
                value = pot[0, tile, z + 1, at : at + 8]
                diagonal = zero
                flow = zero
                for column, (dz, dx, dy) in enumerate(OFFSETS):
                    forward_edge = edge[column, tile, z + 1, at : at + 8]
                    diagonal = diagonal + forward_edge + backward(column, tile, z, at)
                    for sign in (1, -1):
                        there = layer[z + 1 + sign * dz] * 18 + 9
                        scale = table[here + column] + table[there + column]
                        r = at + sign * dx
                        n = med[shifted[sign * dy], tile, z + 1 + sign * dz, r : r + 8]
                        v = pot[shifted[sign * dy], tile, z + 1 + sign * dz, r : r + 8]
                        flow = flow + (jnp.maximum(n - 1.0, 0.0) * scale) * (v - value)
                source = vec[2, tile, z + 1, at : at + 8]
                residual = tissue * flow + inside * source - inside * mean
                size = jnp.maximum(diagonal, 1.0)
                scale = inside / size
                jac[tile, z + 1, at : at + 8] = scale
                kap[tile, z + 1, at : at + 8] = jnp.where(
                    diagonal >= 1.0, 0.0, inside - scale * diagonal
                )
                first_vec = scale * residual
                vec[0, tile, z + 1, at : at + 8] = first_vec
                vec_l[0, tile, z + 1, at : at + 8] = roll(first_vec, LANES - 1)
                vec_r[0, tile, z + 1, at : at + 8] = roll(first_vec, 1)
                vec[1, tile, z + 1, at : at + 8] = inside * size
                vec_l[1, tile, z + 1, at : at + 8] = residual
        return carry

    lax.fori_loop(0, planes, start_of, 0)

    def merged(buffer, plane, at):
        low = roll(buffer[0, plane, at : at + 8], LANES - SLOT)
        up = roll(buffer[1, plane, at : at + 8], SLOT)
        return jnp.where(lane < LANES // 2, low, up)

    def own_of(z, carry):
        for block in range(rows // 8):
            at = TOP + 8 * block
            out = 8 * block
            metric[z, out : out + 8] = merged(vec.at[1], first + z + 1, at)
            extra[z, out : out + 8] = merged(vec_l.at[1], first + z + 1, at)
            basis[0, z, out : out + 8] = merged(vec.at[0], first + z + 1, at)
        return carry

    lax.fori_loop(0, own_planes, own_of, 0)

    for step in range(ITERS):
        now, later, before = step % 3, (step + 1) % 3, (step + 2) % 3
        side, side_next = step % 2, (step + 1) % 2
        reach = ITERS - 1 - step
        sources = {0: vec.at[now], 1: vec_l.at[side], -1: vec_r.at[side]}

        def apply(z, carry):
            for tile in range(tiles):
                for block in range(inner):
                    at = 8 + 8 * block
                    total = zero
                    for column, (dz, dx, dy) in enumerate(OFFSETS):
                        total = total + edge[column, tile, z + 1, at : at + 8] * sources[dy][
                            tile, z + 1 + dz, at + dx : at + dx + 8
                        ]
                        total = total + backward(column, tile, z, at) * sources[-dy][
                            tile, z + 1 - dz, at - dx : at - dx + 8
                        ]
                    value = (
                        jac[tile, z + 1, at : at + 8] * total
                        + kap[tile, z + 1, at : at + 8] * sources[0][tile, z + 1, at : at + 8]
                    )
                    if step:
                        value = 2.0 * value - vec[before, tile, z + 1, at : at + 8]
                    vec[later, tile, z + 1, at : at + 8] = value
                    if step + 1 < ITERS:
                        vec_l[side_next, tile, z + 1, at : at + 8] = roll(value, LANES - 1)
                        vec_r[side_next, tile, z + 1, at : at + 8] = roll(value, 1)
            return carry

        low = jnp.maximum(first - reach, 0)
        up = jnp.minimum(first + own_planes + reach, planes)
        lax.fori_loop(low, up, apply, 0)

        def keep(z, carry):
            for block in range(rows // 8):
                at = TOP + 8 * block
                out = 8 * block
                basis[step + 1, z, out : out + 8] = merged(vec.at[later], first + z + 1, at)
            return carry

        lax.fori_loop(0, own_planes, keep, 0)

    acc[...] = jnp.zeros(acc.shape, jnp.float32)
    pairs = [(i, j) for i in range(VECS) for j in range(i, VECS)]
    split_at = 26
    for part in (pairs[:split_at], pairs[split_at:]):
        plain = part is not pairs[:split_at] and part[-1] == pairs[-1]

        def gather(z, carry):
            carry = list(carry)
            for block in range(rows // 8):
                out = 8 * block
                weight = metric[z, out : out + 8]
                loaded = {}
                for i, j in part:
                    for index in (i, j):
                        if index not in loaded:
                            loaded[index] = basis[index, z, out : out + 8]
                scaled = {i: loaded[i] * weight for i in {i for i, _ in part}}
                for number, (i, j) in enumerate(part):
                    carry[number] = carry[number] + scaled[i] * loaded[j]
            return tuple(carry)

        done = lax.fori_loop(0, own_planes, gather, tuple(zero for _ in part))
        for (i, j), value in zip(part, done):
            value = jnp.sum(value, axis=0, keepdims=True)
            rowsum[VECS * i + j : VECS * i + j + 1] = value
            if i != j:
                rowsum[VECS * j + i : VECS * j + i + 1] = value

    def plain_sums(z, carry):
        carry = list(carry)
        for block in range(rows // 8):
            out = 8 * block
            for index in range(ITERS):
                carry[index] = carry[index] + basis[index, z, out : out + 8]
            carry[ITERS] = carry[ITERS] + extra[z, out : out + 8]
        return tuple(carry)

    done = lax.fori_loop(0, own_planes, plain_sums, tuple(zero for _ in range(ITERS + 1)))
    for index, value in enumerate(done):
        rowsum[SUMS + index : SUMS + index + 1] = jnp.sum(value, axis=0, keepdims=True)
    for index in range(SUMS + ITERS + 1, rowsum.shape[0]):
        rowsum[index : index + 1] = jnp.zeros((1, LANES), jnp.float32)
    gram[...] = lax.dot_general(
        jnp.ones((8, LANES), jnp.float32),
        rowsum[...],
        (((1,), (1,)), ((), ())),
        precision=lax.Precision.HIGHEST,
        preferred_element_type=jnp.float32,
    )


def finish(geometry, gathered, total_in, basis, metric, solution_ref, residual_ref, flag):
    own_planes, rows = geometry
    total = jnp.sum(gathered[...], axis=0, keepdims=True)
    count = jnp.sum(total_in[0:1], axis=1, keepdims=True)
    lane = lane_iota((16, LANES))
    sub = lax.broadcasted_iota(jnp.int32, (16, LANES), 0)
    matrix = jnp.zeros((16, LANES), jnp.float32)
    for i in range(VECS):
        line = roll(total, LANES - VECS * i)
        matrix = jnp.where(sub == i, jnp.broadcast_to(line, (16, LANES)), matrix)
    matrix = jnp.where(lane < VECS, matrix, 0.0)
    reflected = jnp.where(lane == 0, roll(matrix, LANES - 1), roll(matrix, 1))
    square = matrix - 0.5 * (roll(matrix, LANES - 1) + reflected)
    system = jnp.where(lane < ITERS, square, 0.0)
    system = jnp.where(lane == ITERS, roll(matrix, ITERS), system)[0:8]
    lane8 = lane[0:8]
    sub8 = sub[0:8]
    for k in range(ITERS):
        line = system[k : k + 1]
        pivot = jnp.sum(jnp.where(lane8[0:1] == k, line, 0.0), axis=1, keepdims=True)
        line = line / pivot
        column = jnp.sum(jnp.where(lane8 == k, system, 0.0), axis=1, keepdims=True)
        line8 = jnp.broadcast_to(line, (8, LANES))
        system = jnp.where(sub8 == k, line8, system - column * line8)
    answer = jnp.sum(jnp.where(lane8 == ITERS, system, 0.0), axis=1, keepdims=True)
    coef = [answer[k : k + 1] for k in range(ITERS)]
    zero = jnp.zeros((1, 1), jnp.float32)
    padded = coef + [zero, zero]
    weights = []
    for i in range(VECS):
        value = 0.5 * padded[i + 1] - padded[i]
        if i == 0:
            value = value + 1.0
        elif i == 1:
            value = value + padded[0]
        else:
            value = value + 0.5 * padded[i - 1]
        weights.append(value)
    sums = [total[:, SUMS + k : SUMS + k + 1] for k in range(ITERS + 1)]
    mean = zero
    for k in range(ITERS):
        mean = mean + coef[k] * sums[k]
    mean = mean / count
    drift = sums[ITERS] / count
    column = jnp.concatenate(weights + [zero] * (16 - VECS), axis=0)
    row = jnp.zeros((1, LANES), jnp.float32)
    for i in range(VECS):
        row = jnp.where(lane[0:1] == i, weights[i], row)
    size = jnp.sum(jnp.sum(matrix * column * row, axis=1, keepdims=True), axis=0, keepdims=True)
    diagonal = jnp.sum(jnp.where(lane == sub, matrix, 0.0), axis=1, keepdims=True)
    spread = jnp.sum(jnp.abs(column) * jnp.sqrt(diagonal), axis=0, keepdims=True)
    flag[...] = jnp.broadcast_to(spread * spread / size, (8, LANES))

    def combine(z, carry):
        for block in range(rows // 8):
            out = 8 * block
            weight = metric[z, out : out + 8]
            inside = jnp.minimum(weight, 1.0)
            phi = inside * (-mean)
            rest = jnp.zeros((8, LANES), jnp.float32)
            for k in range(VECS):
                value = basis[k, z, out : out + 8]
                if k < ITERS:
                    phi = phi + coef[k] * value
                rest = rest + weights[k] * value
            solution_ref[z, out : out + 8] = phi
            residual_ref[z, out : out + 8] = weight * rest - inside * drift
        return carry

    lax.fori_loop(0, own_planes, combine, 0)


def f32(*shape):
    return jax.ShapeDtypeStruct(shape, jnp.float32)


def cyclic(count, shift):
    return [(i, (i + shift) % count) for i in range(count)]


def fast(potential, tissue_mask, layer_index, source):
    own_planes, rows, width = tissue_mask.shape
    gx, gy, gz = (lax.axis_size(name) for name in ("gx", "gy", "gz"))
    at_x, at_y, at_z = (lax.axis_index(name) for name in ("gx", "gy", "gz"))
    params = pltpu.CompilerParams(vmem_limit_bytes=60 * 1024 * 1024)
    stacked = jnp.stack([potential, source, tissue_mask.astype(jnp.float32)])

    full = gz * own_planes <= own_planes + 2 * HALO
    if full:
        planes = gz * own_planes
        first = at_z * own_planes
        fields, layers, offsets = [stacked], [layer_index], [first]
        for shift in range(1, gz):
            pairs = cyclic(gz, shift)
            fields.append(lax.ppermute(stacked, "gz", pairs))
            layers.append(lax.ppermute(layer_index, "gz", pairs))
            offsets.append(((at_z + gz - shift) % gz) * own_planes)
        own_number = 0
    else:
        planes = own_planes + 2 * HALO
        first = HALO
        fields, layers, offsets = [stacked], [layer_index], [HALO]
        own_number = 0
        left = HALO
        hop = 1
        while left > 0:
            size = min(left, own_planes)
            up = [(i, i + hop) for i in range(gz - hop)]
            down = [(j, i) for i, j in up]
            fields.append(lax.ppermute(stacked[:, own_planes - size :], "gz", up))
            layers.append(lax.ppermute(layer_index[own_planes - size :], "gz", up))
            offsets.append(left - size)
            fields.append(lax.ppermute(stacked[:, :size], "gz", down))
            layers.append(lax.ppermute(layer_index[:size], "gz", down))
            offsets.append(HALO + own_planes + HALO - left)
            left -= size
            hop += 1
    pieces = tuple(field.shape[1] for field in fields)
    offs = jnp.stack([jnp.asarray(o, jnp.int32) for o in offsets])
    groups = -(-planes // 8)
    y_rows = 3 * groups * rows + 8

    joined, to_left, to_right, sums = pl.pallas_call(
        functools.partial(pack_y, (pieces, own_number, planes, rows, full)),
        out_shape=(f32(3, planes, rows, LANES), f32(y_rows, LANES), f32(y_rows, LANES), f32(8, LANES)),
        in_specs=[SMEM] + [VMEM] * len(pieces),
        out_specs=(VMEM,) * 4,
        compiler_params=params,
        name="pack_y",
    )(offs, *fields)
    from_left = lax.ppermute(to_right, "gy", cyclic(gy, 1))
    from_right = lax.ppermute(to_left, "gy", cyclic(gy, gy - 1))
    others = [sums] + [lax.ppermute(sums, "gy", cyclic(gy, s)) for s in range(2, gy - 1)]

    x_size = x_rows(planes) + 8
    upper, lower, sums = pl.pallas_call(
        functools.partial(pack_x, (planes, rows, len(others))),
        out_shape=(f32(x_size, LANES), f32(x_size, LANES), f32(8, LANES)),
        in_specs=[VMEM] * (3 + len(others)),
        out_specs=(VMEM,) * 3,
        compiler_params=params,
        name="pack_x",
    )(joined, from_left, from_right, *others)
    from_upper = lax.ppermute(lower, "gx", cyclic(gx, 1))
    from_lower = lax.ppermute(upper, "gx", cyclic(gx, gx - 1))
    total = sums + from_upper[x_size - 8 :] + from_lower[x_size - 8 :]
    for s in range(2, gx - 1):
        total = total + lax.ppermute(sums, "gx", cyclic(gx, s))
    if not full:
        total = lax.psum(total, "gz")

    info = jnp.stack(
        [
            (at_y > 0).astype(jnp.int32),
            (at_y < gy - 1).astype(jnp.int32),
            (at_x > 0).astype(jnp.int32),
            (at_x < gx - 1).astype(jnp.int32),
            jnp.asarray(first, jnp.int32),
        ]
    )
    table = np.concatenate(
        [
            0.5 * tensor_table(LAYERS, bulk_long, bulk_trans),
            0.5 * tensor_table(LAYERS, intra_long, intra_trans),
        ],
        axis=1,
    ).reshape(-1)
    high = TOP + rows + 16
    grid = (2, planes + 2, high, LANES)
    rolled = sum(1 for offset in OFFSETS if offset[2])
    scratch = [
        pltpu.SMEM((planes + 2,), jnp.int32),
        pltpu.VMEM((3,) + grid, jnp.float32),
        pltpu.VMEM((3,) + grid, jnp.float32),
        pltpu.VMEM((len(OFFSETS),) + grid, jnp.float32),
        pltpu.VMEM((rolled,) + grid, jnp.float32),
        pltpu.VMEM((3,) + grid, jnp.float32),
        pltpu.VMEM((2,) + grid, jnp.float32),
        pltpu.VMEM((2,) + grid, jnp.float32),
        pltpu.VMEM(grid, jnp.float32),
        pltpu.VMEM(grid, jnp.float32),
        pltpu.VMEM((8, LANES), jnp.float32),
        pltpu.VMEM((-(-(SUMS + ITERS + 1) // 8) * 8, LANES), jnp.float32),
    ]
    sums_rows = scratch[-1].shape[0]
    gram, basis, metric, _ = pl.pallas_call(
        functools.partial(krylov, (pieces, planes, own_planes, rows, 0)),
        out_shape=(
            f32(8, sums_rows),
            f32(VECS, own_planes, rows, LANES),
            f32(own_planes, rows, LANES),
            f32(own_planes, rows, LANES),
        ),
        in_specs=[SMEM] * (3 + len(pieces)) + [VMEM] * 6,
        out_specs=(VMEM,) * 4,
        scratch_shapes=scratch,
        compiler_params=params,
        name="krylov",
    )(info, offs, jnp.asarray(table), *layers, joined, from_left, from_right, from_upper, from_lower, total)

    everyone = gx * gy * gz
    row = jnp.pad(gram[0:1], ((0, 0), (0, LANES - sums_rows)))
    gathered = lax.all_to_all(
        jnp.broadcast_to(row, (everyone, LANES)), ("gx", "gy", "gz"), 0, 0, tiled=True
    )
    answer, residual, flag = pl.pallas_call(
        functools.partial(finish, (own_planes, rows)),
        out_shape=(f32(own_planes, rows, LANES), f32(own_planes, rows, LANES), f32(8, LANES)),
        in_specs=[VMEM] * 4,
        out_specs=(VMEM,) * 3,
        compiler_params=params,
        name="finish",
    )(gathered, total, basis, metric)
    return answer, residual, flag


def body(potential, tissue_mask, layer_index, source):
    answer, residual, flag = fast(potential, tissue_mask, layer_index, source)
    return (answer, residual)


def solution(mesh):
    placed = (P("gz", "gx", "gy"), P("gz", "gx", "gy"), P("gz"), P("gz", "gx", "gy"))
    return jax.shard_map(
        body,
        mesh=mesh,
        in_specs=placed,
        out_specs=(P("gz", "gx", "gy"), P("gz", "gx", "gy")),
        check_vma=False,
    )
```

time: 659 us -> 89.1 us (0.14)
  blocking collectives: 365 us -> 10.4 us
  starting transfers between devices: 123 us -> 11 us
  waiting for transfers between devices: 99 us -> 13.9 us
  Pallas kernels: 0 us -> 47 us
  between operations: 34.8 us -> 0.7 us
  other arithmetic: 28.8 us -> 2.3 us
    psum x9 -> x0, blocking collectives: 365 us -> none  [the longest x8 325 us: coupled(): lax.psum((jnp.sum(scaled), jnp.sum(current * scaled), jnp.sum(current), j...]
    ppermute x62 -> x8, starting transfers between devices: 123 us -> 11 us  [the longest x1 2.85 us: fast(): from_left = lax.ppermute(to_right, 'gy', cyclic(gy, 1))]
    ppermute x62 -> x8, waiting for transfers between devices: 99 us -> 13.9 us  [the longest x1 10.6 us: fast(): total = total + lax.ppermute(sums, 'gx', cyclic(gx, s))]
    pallas_call x0 -> x4, Pallas kernels: none -> 47 us  [the longest x1 38.9 us: fast(): pl.pallas_call(functools.partial(krylov, (pieces, planes, own_planes, row...]
    reduce_sum x10 -> x0, other arithmetic: 12.4 us -> none  [the longest x8 9.81 us: coupled(): jnp.sum(image)]
    all_to_all x0 -> x1, blocking collectives: none -> 10.4 us  [fast(): lax.all_to_all(jnp.broadcast_to(row, (everyone, LANES)), ('gx', 'gy', 'gz...]
    concatenate x38 -> x0, other arithmetic: 6.99 us -> none  [padded(): value = jnp.concatenate([before, value, after], axis=dim)]
  transfers between devices with their start and end apart: 62 -> 8, of which waited for: 35 -> 4; matrix products, arithmetic and copies ran while one was open for 1% -> 2% of each run, Pallas kernels for 0% -> 0%
where the time goes in v1:
time: 89.1 us; the launch traced here: 88.8 us
  Pallas kernels  47 us (53%)
  waiting for transfers between devices  13.9 us (16%)
  starting transfers between devices  11 us (12%)
  blocking collectives  10.4 us (12%)
  local copies, waits for them, and re-layouts  3.47 us (4%)
  other arithmetic  2.3 us (3%)
    pallas_call x1, Pallas kernels, fast(): pl.pallas_call(functools.partial(krylov, (pieces, planes, own_planes, row...  38.9 us
    ppermute x1, waiting for transfers between devices, fast(): total = total + lax.ppermute(sums, 'gx', cyclic(gx, s))  10.6 us
    all_to_all x1, blocking collectives, fast(): lax.all_to_all(jnp.broadcast_to(row, (everyone, LANES)), ('gx', 'gy', 'gz...  10.4 us
    pallas_call x1, Pallas kernels, fast(): pl.pallas_call(functools.partial(finish, (own_planes, rows)), out_shape=(...  3.98 us
    ppermute x1, starting transfers between devices, fast(): from_left = lax.ppermute(to_right, 'gy', cyclic(gy, 1))  2.85 us
    ppermute x1, starting transfers between devices, fast(): from_lower = lax.ppermute(upper, 'gx', cyclic(gx, gx - 1))  2.25 us
    unnamed x26, local copies, waits for them, and re-layouts  2.1 us
    pallas_call x1, Pallas kernels, fast(): pl.pallas_call(functools.partial(pack_y, (pieces, own_number, planes, row...  2.1 us
  transfers between devices with their start and end apart: 8, of which 4 were waited for; matrix products, arithmetic and copies ran while one was open for 2% of the time, Pallas kernels for 0%

profile of v1, /device:TPU:0, one launch (start us, length us, event | category | flops | bytes accessed | tf_op | source)
XLA Modules:
  0.0 88.8 jit_solution(6754190798571373293)
XLA Ops:
  0.6 0.0 copy-start.6
  0.6 0.0 copy-start.7
  0.6 0.9 %convert_bitcast_fusion = f32[1,8,24,128]{3,2,1,0:T(8,128)S(1)} fusion(s32[8,24,128]{2,1,0:T(8,128)} %param.6), kind=kLoop, calls=%fused_computation.1 | loop fusion | flops 24576 | bytes 196608 | tf_op jit(solution)/shard_map/stack | solution.py:557
  1.6 0.0 copy-done.6
  1.6 0.0 copy-done.7
  1.6 0.0 copy-start
  1.7 0.6 collective-permute-start.1
  2.2 0.7 pad_add_fusion.offs
  2.9 0.5 collective-permute-done.1.refs_1_
  3.4 0.0 copy-done
  3.4 0.0 copy-start.3
  3.4 0.7 copy-done.3
  4.1 2.1 %pack_y.1 = (f32[3,16,24,128]{3,2,1,0:T(8,128)}, f32[152,128]{1,0:T(8,128)}, f32[152,128]{1,0:T(8,128)}, f32[8,128]{1,0:T(8,128)}) custom-call(s32[2]{0:T(128)} %pad_add_fusion.offs, f32[3,8,24,128]{3,2,1,0:T(8,128)} %copy-done, f32[3,8,24,128]{3,2,1,0:T(8,128)} %copy-done.3), custom_call_target="tpu_custom_call" | custom-call | tf_op jit(solution)/shard_map/pack_y/pallas_call | solution.py:594
  6.2 0.0 copy-start.8
  6.2 2.8 %collective-permute-start.2 = (f32[152,128]{1,0:T(8,128)}, f32[152,128]{1,0:T(8,128)S(1)}, u32[]{:S(2)}, u32[]{:S(2)}) collective-permute-start(f32[152,128]{1,0:T(8,128)} %get-tuple-element.15), channel_id=1, source_target_pairs={{0,2},{2,4},{4,6},{6,0},{1,3},{3,5},{5,7},{7,1},{8,10},{10,12},{12... | collective-permute-start | bytes 233480 | tf_op jit(solution)/shard_map/ppermute | solution.py:602
  9.1 1.0 %collective-permute-start.3 = (f32[152,128]{1,0:T(8,128)}, f32[152,128]{1,0:T(8,128)S(1)}, u32[]{:S(2)}, u32[]{:S(2)}) collective-permute-start(f32[152,128]{1,0:T(8,128)} %get-tuple-element.16), channel_id=1, source_target_pairs={{0,6},{2,0},{4,2},{6,4},{1,7},{3,1},{5,3},{7,5},{8,14},{10,8},{12,... | collective-permute-start | bytes 233480 | tf_op jit(solution)/shard_map/ppermute | solution.py:603
  10.1 0.0 copy-done.8
  10.1 1.9 %collective-permute-start.4 = (f32[8,128]{1,0:T(8,128)S(1)}, f32[8,128]{1,0:T(8,128)S(1)}, u32[]{:S(2)}, u32[]{:S(2)}) collective-permute-start(f32[8,128]{1,0:T(8,128)S(1)} %copy-done.8), channel_id=1, source_target_pairs={{0,4},{2,6},{4,0},{6,2},{1,5},{3,7},{5,1},{7,3},{8,12},{10,14},{12... | collective-permute-start | bytes 12296 | tf_op jit(solution)/shard_map/ppermute | solution.py:604
  12.0 1.7 %collective-permute-done.4.refs_1_ = f32[8,128]{1,0:T(8,128)S(1)} collective-permute-done((f32[8,128]{1,0:T(8,128)S(1)}, f32[8,128]{1,0:T(8,128)S(1)}, u32[]{:S(2)}, u32[]{:S(2)}) %collective-permute-start.4) | collective-permute-done | bytes 4128 | tf_op jit(solution)/shard_map/ppermute | solution.py:604
  13.7 0.0 copy-start.9
  13.7 0.0 collective-permute-done.2.from_left.refs_3_
  13.7 0.0 copy-start.1
  13.7 1.1 %collective-permute-done.3.from_right.refs_4_ = f32[152,128]{1,0:T(8,128)S(1)} collective-permute-done((f32[152,128]{1,0:T(8,128)}, f32[152,128]{1,0:T(8,128)S(1)}, u32[]{:S(2)}, u32[]{:S(2)}) %collective-permute-start.3) | collective-permute-done | bytes 77856 | tf_op jit(solution)/shard_map/ppermute | solution.py:603
  14.8 0.0 copy-start.2
  14.8 0.0 copy-done.9
  14.8 0.0 copy-done.1
  14.8 0.6 copy-done.2
  15.4 2.0 %pack_x.1 = (f32[552,128]{1,0:T(8,128)}, f32[552,128]{1,0:T(8,128)}, f32[8,128]{1,0:T(8,128)}) custom-call(f32[3,16,24,128]{3,2,1,0:T(8,128)} %get-tuple-element.14.joined.refs_2_, f32[152,128]{1,0:T(8,128)} %copy-done.1, f32[152,128]{1,0:T(8,128)} %copy-done.2, f32[8,128]{1,0:T(8,128)} %get-tuple-element.17.refs_0_, f32[8,128]{1,0:T(8,128)} %copy-done.9), custom_call_target="tpu_custom_call" | custom-call | tf_op jit(solution)/shard_map/pack_x/pallas_call | solution.py:607
  17.4 1.6 %collective-permute-start.5 = (f32[552,128]{1,0:T(8,128)}, f32[552,128]{1,0:T(8,128)S(1)}, u32[]{:S(2)}, u32[]{:S(2)}) collective-permute-start(f32[552,128]{1,0:T(8,128)} %get-tuple-element.18), channel_id=1, source_target_pairs={{0,8},{8,16},{16,24},{24,0},{1,9},{9,17},{17,25},{25,1},{2,10},{10... | collective-permute-start | bytes 847880 | tf_op jit(solution)/shard_map/ppermute | solution.py:615
  19.0 2.2 %collective-permute-start.6 = (f32[552,128]{1,0:T(8,128)}, f32[552,128]{1,0:T(8,128)S(1)}, u32[]{:S(2)}, u32[]{:S(2)}) collective-permute-start(f32[552,128]{1,0:T(8,128)} %get-tuple-element.19), channel_id=1, source_target_pairs={{0,24},{8,0},{16,8},{24,16},{1,25},{9,1},{17,9},{25,17},{2,26},{10... | collective-permute-start | bytes 847880 | tf_op jit(solution)/shard_map/ppermute | solution.py:616
  21.2 0.0 copy-done.10
  21.2 0.8 collective-permute-start.7
  22.0 0.0 copy-done.11
  22.0 0.0 collective-permute-start
  22.0 0.7 stack.58.info
  22.7 10.6 %collective-permute-done.7 = f32[8,128]{1,0:T(8,128)S(1)} collective-permute-done((f32[8,128]{1,0:T(8,128)S(1)}, f32[8,128]{1,0:T(8,128)S(1)}, u32[]{:S(2)}, u32[]{:S(2)}) %collective-permute-start.7) | collective-permute-done | bytes 4128 | tf_op jit(solution)/shard_map/ppermute | solution.py:619
  33.3 0.0 collective-permute-done.5.refs_5_
  33.3 0.0 collective-permute-done.6.refs_6_
  33.3 0.0 copy-start.5
  33.3 0.7 fusion.refs_7_.total_in
  34.0 0.0 collective-permute-done.refs_1_
  34.0 0.0 copy-done.4
  34.0 0.1 copy-done.5
  34.2 0.6 copy-done.12
  34.7 38.9 %krylov.1 = (f32[8,96]{1,0:T(8,128)}, f32[9,8,24,128]{3,2,1,0:T(8,128)}, f32[8,24,128]{2,1,0:T(8,128)}, f32[8,24,128]{2,1,0:T(8,128)}) custom-call(s32[5]{0:T(128)} %stack.58.info, s32[2]{0:T(128)} %pad_add_fusion.offs, f32[288]{0:T(512)} %constant.36.clone.table, s32[8]{0:T(128)} %refs_0_.1, s32[8]{0:T(128)} %copy-done.12, ...), custom_call_target="tpu_custom_call" | custom-call | tf_op jit(solution)/shard_map/krylov/pallas_call | solution.py:657
  73.7 0.7 slice.11
  74.4 10.4 %all_to_all.8 = f32[32,1,128]{2,1,0:T(1,128)} all-to-all(f32[32,1,128]{2,1,0:T(1,128)S(1)} %broadcast_in_dim.2), channel_id=1, replica_groups=mesh['gx'=4,'gy'=4,'gz'=2] {'gx','gy','gz'}, dimensions={0} | all-to-all | bytes 32768 | tf_op jit(solution)/shard_map/all_to_all | solution.py:674
  84.8 4.0 %finish.1 = (f32[8,24,128]{2,1,0:T(8,128)}, f32[8,24,128]{2,1,0:T(8,128)}, f32[8,128]{1,0:T(8,128)}) custom-call(f32[32,128]{1,0:T(8,128)} %bitcast.15, f32[8,128]{1,0:T(8,128)} %fusion.refs_7_.total_in, f32[9,8,24,128]{3,2,1,0:T(8,128)} %get-tuple-element.22.basis, f32[8,24,128]{2,1,0:T(8,128)} %get-tuple-element.23.metric), custom_call_target="tpu_custom_call" | custom-call | tf_op jit(solution)/shard_map/finish/pallas_call | solution.py:677
  (7 shorter events, 0.0 us)
Async XLA Ops:
  0.6 1.0 %copy-start.6 = (f32[8,24,128]{2,1,0:T(8,128)S(1)}, f32[8,24,128]{2,1,0:T(8,128)}, u32[]{:S(2)}) copy-start(f32[8,24,128]{2,1,0:T(8,128)} %param.8) | copy-start | bytes 294916
  0.6 1.0 %copy-start.7 = (f32[8,24,128]{2,1,0:T(8,128)S(1)}, f32[8,24,128]{2,1,0:T(8,128)}, u32[]{:S(2)}) copy-start(f32[8,24,128]{2,1,0:T(8,128)} %param.5) | copy-start | bytes 294916
  1.6 1.8 %copy-start = (f32[3,8,24,128]{3,2,1,0:T(8,128)}, f32[3,8,24,128]{3,2,1,0:T(8,128)S(1)}, u32[]{:S(2)}) copy-start(f32[3,8,24,128]{3,2,1,0:T(8,128)S(1)} %pad_maximum_fusion.refs_0_) | copy-start | bytes 884740
  1.7 1.8 %collective-permute-start.1 = (f32[3,8,24,128]{3,2,1,0:T(8,128)S(1)}, f32[3,8,24,128]{3,2,1,0:T(8,128)S(1)}, u32[]{:S(2)}, u32[]{:S(2)}) collective-permute-start(f32[3,8,24,128]{3,2,1,0:T(8,128)S(1)} %pad_maximum_fusion.refs_0_), channel_id=1, source_target_pairs={{0,1},{1,0},{2,3},{3,2},{4,5},{5,4},{6,7},{7,6},{8,9},{9,8},{10,11... | collective-permute-start | bytes 884744 | tf_op jit(solution)/shard_map/ppermute | solution.py:566
  3.4 0.7 copy-start.3
  6.2 3.9 %copy-start.8 = (f32[8,128]{1,0:T(8,128)S(1)}, f32[8,128]{1,0:T(8,128)}, u32[]{:S(2)}) copy-start(f32[8,128]{1,0:T(8,128)} %get-tuple-element.17.refs_0_) | copy-start | bytes 12292
  6.2 7.5 %collective-permute-start.2 = (f32[152,128]{1,0:T(8,128)}, f32[152,128]{1,0:T(8,128)S(1)}, u32[]{:S(2)}, u32[]{:S(2)}) collective-permute-start(f32[152,128]{1,0:T(8,128)} %get-tuple-element.15), channel_id=1, source_target_pairs={{0,2},{2,4},{4,6},{6,0},{1,3},{3,5},{5,7},{7,1},{8,10},{10,12},{12... | collective-permute-start | bytes 233480 | tf_op jit(solution)/shard_map/ppermute | solution.py:602
  9.1 5.7 %collective-permute-start.3 = (f32[152,128]{1,0:T(8,128)}, f32[152,128]{1,0:T(8,128)S(1)}, u32[]{:S(2)}, u32[]{:S(2)}) collective-permute-start(f32[152,128]{1,0:T(8,128)} %get-tuple-element.16), channel_id=1, source_target_pairs={{0,6},{2,0},{4,2},{6,4},{1,7},{3,1},{5,3},{7,5},{8,14},{10,8},{12,... | collective-permute-start | bytes 233480 | tf_op jit(solution)/shard_map/ppermute | solution.py:603
  10.1 3.6 %collective-permute-start.4 = (f32[8,128]{1,0:T(8,128)S(1)}, f32[8,128]{1,0:T(8,128)S(1)}, u32[]{:S(2)}, u32[]{:S(2)}) collective-permute-start(f32[8,128]{1,0:T(8,128)S(1)} %copy-done.8), channel_id=1, source_target_pairs={{0,4},{2,6},{4,0},{6,2},{1,5},{3,7},{5,1},{7,3},{8,12},{10,14},{12... | collective-permute-start | bytes 12296 | tf_op jit(solution)/shard_map/ppermute | solution.py:604
  13.7 1.1 %copy-start.9 = (f32[8,128]{1,0:T(8,128)}, f32[8,128]{1,0:T(8,128)S(1)}, u32[]{:S(2)}) copy-start(f32[8,128]{1,0:T(8,128)S(1)} %collective-permute-done.4.refs_1_) | copy-start | bytes 12292
  13.7 1.1 %copy-start.1 = (f32[152,128]{1,0:T(8,128)}, f32[152,128]{1,0:T(8,128)S(1)}, u32[]{:S(2)}) copy-start(f32[152,128]{1,0:T(8,128)S(1)} %collective-permute-done.2.from_left.refs_3_) | copy-start | bytes 233476
  14.8 0.6 copy-start.2
  17.4 3.8 %copy-start.10 = (f32[8,128]{1,0:T(8,128)S(1)}, f32[8,128]{1,0:T(8,128)}, u32[]{:S(2)}) copy-start(f32[8,128]{1,0:T(8,128)} %get-tuple-element.20) | copy-start | bytes 12292
  17.4 15.9 %collective-permute-start.5 = (f32[552,128]{1,0:T(8,128)}, f32[552,128]{1,0:T(8,128)S(1)}, u32[]{:S(2)}, u32[]{:S(2)}) collective-permute-start(f32[552,128]{1,0:T(8,128)} %get-tuple-element.18), channel_id=1, source_target_pairs={{0,8},{8,16},{16,24},{24,0},{1,9},{9,17},{17,25},{25,1},{2,10},{10... | collective-permute-start | bytes 847880 | tf_op jit(solution)/shard_map/ppermute | solution.py:615
  19.0 3.0 %copy-start.11 = (s32[8]{0:T(128)S(1)}, s32[8]{0:T(128)}, u32[]{:S(2)}) copy-start(s32[8]{0:T(128)} %refs_0_.1) | copy-start | bytes 100
  19.0 14.3 %collective-permute-start.6 = (f32[552,128]{1,0:T(8,128)}, f32[552,128]{1,0:T(8,128)S(1)}, u32[]{:S(2)}, u32[]{:S(2)}) collective-permute-start(f32[552,128]{1,0:T(8,128)} %get-tuple-element.19), channel_id=1, source_target_pairs={{0,24},{8,0},{16,8},{24,16},{1,25},{9,1},{17,9},{25,17},{2,26},{10... | collective-permute-start | bytes 847880 | tf_op jit(solution)/shard_map/ppermute | solution.py:616
  21.2 12.1 %collective-permute-start.7 = (f32[8,128]{1,0:T(8,128)S(1)}, f32[8,128]{1,0:T(8,128)S(1)}, u32[]{:S(2)}, u32[]{:S(2)}) collective-permute-start(f32[8,128]{1,0:T(8,128)S(1)} %copy-done.10), channel_id=1, source_target_pairs={{0,16},{8,24},{16,0},{24,8},{1,17},{9,25},{17,1},{25,9},{2,18},{10... | collective-permute-start | bytes 12296 | tf_op jit(solution)/shard_map/ppermute | solution.py:619
  22.0 12.0 %collective-permute-start = (s32[8]{0:T(128)S(1)}, s32[8]{0:T(128)S(1)}, u32[]{:S(2)}, u32[]{:S(2)}) collective-permute-start(s32[8]{0:T(128)S(1)} %copy-done.11), channel_id=1, source_target_pairs={{0,1},{1,0},{2,3},{3,2},{4,5},{5,4},{6,7},{7,6},{8,9},{9,8},{10,11... | collective-permute-start | bytes 104 | tf_op jit(solution)/shard_map/ppermute | solution.py:567
  33.3 0.7 copy-start.4
  33.3 0.8 copy-start.5
  34.2 0.6 copy-start.12

commit v2 on v1

v2 whole, which is shorter than its diff:
```python
import functools
import math

import jax
import jax.numpy as jnp
import numpy as np
from jax import lax
from jax.experimental import pallas as pl
from jax.experimental.pallas import tpu as pltpu
from jax.sharding import PartitionSpec as P

ITERS = 8
LAYERS = 16
HALO = ITERS + 1
LANES = 128
SLOT = 16
TOP = 16
LEAD = 2
CHUNK = 2
VECS = ITERS + 1
SUMS = VECS * VECS

OFFSETS = [
    (0, 1, 0),
    (0, 0, 1),
    (1, 0, 0),
    (0, 1, 1),
    (0, -1, 1),
    (1, 1, 0),
    (-1, 1, 0),
    (1, 0, 1),
    (-1, 0, 1),
]
bulk_long = 7.99
bulk_trans = 2.55
intra_long = 1.74
intra_trans = 0.19
bath_sigma = 5.0

VMEM = pl.BlockSpec(memory_space=pltpu.VMEM)
SMEM = pl.BlockSpec(memory_space=pltpu.SMEM)


def tensor_table(layers, longitudinal, transverse):
    depth = np.arange(layers, dtype=np.float64) / (layers - 1)
    helix = math.pi / 3.0 * (1.0 - 2.0 * depth)
    tilted = 0.35 * np.cos(math.pi * depth)
    fiber_x = np.cos(tilted) * np.cos(helix)
    fiber_y = np.cos(tilted) * np.sin(helix)
    fiber_z = np.sin(tilted)
    spread = longitudinal - transverse
    s_xx = transverse + spread * fiber_x * fiber_x
    s_yy = transverse + spread * fiber_y * fiber_y
    s_zz = transverse + spread * fiber_z * fiber_z
    s_xy = spread * fiber_x * fiber_y
    s_xz = spread * fiber_x * fiber_z
    s_yz = spread * fiber_y * fiber_z
    columns = [
        s_xx - np.abs(s_xy) - np.abs(s_xz),
        s_yy - np.abs(s_xy) - np.abs(s_yz),
        s_zz - np.abs(s_xz) - np.abs(s_yz),
        np.maximum(s_xy, 0.0),
        np.maximum(-s_xy, 0.0),
        np.maximum(s_xz, 0.0),
        np.maximum(-s_xz, 0.0),
        np.maximum(s_yz, 0.0),
        np.maximum(-s_yz, 0.0),
    ]
    return np.stack(columns, axis=1).astype(np.float32)


def lane_iota(shape):
    return lax.broadcasted_iota(jnp.int32, shape, len(shape) - 1)


def roll(value, shift, axis=-1):
    axis = axis % value.ndim
    shift = shift % value.shape[axis]
    return value if shift == 0 else pltpu.roll(value, shift, axis)


def pack_y(geometry, *refs):
    pieces, summed, rows = geometry
    piece_refs = refs[: len(pieces)]
    left, right, sums = refs[len(pieces) :]
    listed = [(ref, plane) for ref, length in zip(piece_refs, pieces) for plane in range(length)]
    groups = -(-len(listed) // 8)
    lane = lane_iota((rows, LANES))
    count = jnp.zeros((rows, LANES), jnp.float32)
    total = jnp.zeros((rows, LANES), jnp.float32)
    for ref, plane in listed[:summed]:
        inside = jnp.minimum(ref[2, plane], 1.0)
        count = count + inside
        total = total + inside * ref[1, plane]
    sums[...] = jnp.zeros((8, LANES), jnp.float32)
    sums[0:1] = jnp.sum(count, axis=0, keepdims=True)
    sums[1:2] = jnp.sum(total, axis=0, keepdims=True)
    for field in range(3):
        for group in range(groups):
            to_left = jnp.zeros((rows, LANES), jnp.float32)
            to_right = jnp.zeros((rows, LANES), jnp.float32)
            for slot, (ref, plane) in enumerate(listed[8 * group : 8 * group + 8]):
                value = ref[field, plane]
                here = (lane >= SLOT * slot) & (lane < SLOT * (slot + 1))
                to_left = jnp.where(here, roll(value, SLOT * slot), to_left)
                to_right = jnp.where(here, roll(value, SLOT * (slot + 1)), to_right)
            base = (field * groups + group) * rows
            left[base : base + rows] = to_left
            right[base : base + rows] = to_right
    last = 3 * groups * rows
    left[last : last + 8] = sums[...]
    right[last : last + 8] = sums[...]


class Strip:
    def __init__(self, planes):
        self.planes = planes
        self.groups = -(-planes // 8)
        self.side = 3 * planes * 8
        self.ninth = self.side + 2 * 3 * self.groups * 8
        self.side_ninth = self.ninth + 2 * 8 * self.groups
        self.sums = self.side_ninth + -(-4 * self.groups // 8) * 8
        self.rows = self.sums + 8

    def own(self, field, plane):
        return (field * self.planes + plane) * 8

    def edge(self, side, field, group):
        return self.side + ((side * 3 + field) * self.groups + group) * 8

    def own_ninth(self, kind, group):
        return self.ninth + (kind * self.groups + group) * 8

    def edge_ninth(self, side, kind, group):
        return self.side_ninth + (side * 2 + kind) * self.groups + group


def pack_x(geometry, *refs):
    pieces, rows, others = geometry
    piece_refs = refs[: len(pieces)]
    from_left, from_right = refs[len(pieces) : len(pieces) + 2]
    other_refs = refs[len(pieces) + 2 : len(pieces) + 2 + others]
    upper, lower, sums = refs[len(pieces) + 2 + others :]
    listed = [(ref, plane) for ref, length in zip(piece_refs, pieces) for plane in range(length)]
    strip = Strip(len(listed))
    last = 3 * strip.groups * rows
    total = from_left[last : last + 8] + from_right[last : last + 8]
    for ref in other_refs:
        total = total + ref[...]
    sums[...] = total
    for out, first, ninth in ((upper, 0, 8), (lower, rows - 8, rows - 9)):
        out[strip.ninth : strip.sums] = jnp.zeros((strip.sums - strip.ninth, LANES), jnp.float32)
        out[strip.sums : strip.rows] = total
        for number, (ref, plane) in enumerate(listed):
            for field in range(3):
                at = strip.own(field, number)
                out[at : at + 8] = ref[field, plane, first : first + 8]
            for kind, field in enumerate((0, 2)):
                at = strip.own_ninth(kind, number // 8) + number % 8
                out[at : at + 1] = ref[field, plane, ninth : ninth + 1]
        for side, packed in enumerate((from_left, from_right)):
            for group in range(strip.groups):
                for field in range(3):
                    at = strip.edge(side, field, group)
                    base = (field * strip.groups + group) * rows
                    out[at : at + 8] = packed[base + first : base + first + 8]
                for kind, field in enumerate((0, 2)):
                    at = strip.edge_ninth(side, kind, group)
                    base = (field * strip.groups + group) * rows
                    out[at : at + 1] = packed[base + ninth : base + ninth + 1]


def krylov(geometry, table, *refs):
    pieces, planes, own_planes, rows, extras, full, gz, gy = geometry
    layer_refs = refs[: len(pieces)]
    refs = refs[len(pieces) :]
    piece_refs = refs[: len(pieces)]
    refs = refs[len(pieces) :]
    from_left, from_right, from_upper, from_lower, own_sums = refs[:5]
    extra_refs = refs[5 : 5 + extras]
    refs = refs[5 + extras :]
    gram, basis, metric, total_out = refs[:4]
    layer, pot, med, src, edge, vec, vec_l, jac, kap, met, rowsum = refs[4:]
    high = TOP + rows + 16
    inner = (rows + 16) // 8
    both = (0, 1)
    strip = Strip(planes)
    groups = strip.groups
    lane = lane_iota((8, LANES))
    zero = jnp.zeros((8, LANES), jnp.float32)
    at_z = lax.axis_index("gz")
    at_y = lax.axis_index("gy")
    keep_left = jnp.where(at_y > 0, 1.0, 0.0)
    keep_right = jnp.where(at_y < gy - 1, 1.0, 0.0)

    if full:
        offsets = [lax.rem(at_z + gz - shift, gz) * own_planes for shift in range(gz)]
        first = offsets[0]
    else:
        offsets = [HALO]
        left = HALO
        for size in pieces[1::2]:
            offsets += [left - size, HALO + own_planes + HALO - left]
            left -= size
        first = HALO
    listed = [
        (ref, plane, offset + plane)
        for ref, length, offset in zip(piece_refs, pieces, offsets)
        for plane in range(length)
    ]
    layer[0] = 0
    layer[planes + 1] = 0
    for number, length in enumerate(pieces):
        for plane in range(length):
            layer[offsets[number] + plane + 1] = layer_refs[number][plane]

    totals = own_sums[...]
    if extras:
        totals = totals + from_upper[strip.sums : strip.rows] + from_lower[strip.sums : strip.rows]
    for ref in extra_refs:
        totals = totals + ref[...]
    total_out[...] = totals
    mean = jnp.sum(totals[1:2], axis=1, keepdims=True) / jnp.sum(
        totals[0:1], axis=1, keepdims=True
    )

    outside = (LEAD - 1, LEAD + planes)
    for plane in outside:
        for tile in both:
            for at in range(0, high, 8):
                for copy in both:
                    pot[copy, tile, plane, at : at + 8] = zero
                    med[copy, tile, plane, at : at + 8] = zero
                    vec_l[copy, tile, plane, at : at + 8] = zero
                for slot in range(VECS + 1):
                    vec[slot, tile, plane, at : at + 8] = zero
                for column, (dz, _, _) in enumerate(OFFSETS):
                    if dz:
                        edge[column, tile, plane, at : at + 8] = zero

    def tiles_of(own, strip_l, strip_r, slot, kind):
        ln = lane_iota(own.shape)
        a = roll(strip_l, LANES - SLOT * slot)
        b = roll(strip_r, LANES - SLOT * (slot + 1))
        if kind == 2:
            a, b = a * keep_left, b * keep_right
        low = jnp.where(ln < SLOT, a, roll(own, SLOT))
        up = jnp.where(ln >= LANES - SLOT, b, roll(own, LANES - SLOT))
        return low, up

    targets = {0: pot, 1: src, 2: med}

    def place(kind, tile, plane, at, value):
        size = value.shape[0]
        if kind == 1:
            src[tile, plane, at : at + size] = value
        else:
            targets[kind][0, tile, plane, at : at + size] = value
            targets[kind][1, tile, plane, at : at + size] = roll(value, LANES - 1)

    for number, (ref, plane, z) in enumerate(listed):
        group, slot = divmod(number, 8)
        for field in range(3):
            base = (field * groups + group) * rows
            own = (
                ref[field, plane],
                from_left[base : base + rows],
                from_right[base : base + rows],
            )
            for tile, value in enumerate(tiles_of(*own, slot, field)):
                place(field, tile, z + LEAD, TOP, value)
            for packed, at in ((from_upper, TOP - 8), (from_lower, TOP + rows)):
                r0 = strip.own(field, number)
                r1 = strip.edge(0, field, group)
                r2 = strip.edge(1, field, group)
                halo = (packed[r0 : r0 + 8], packed[r1 : r1 + 8], packed[r2 : r2 + 8])
                for tile, value in enumerate(tiles_of(*halo, slot, field)):
                    place(field, tile, z + LEAD, at, value)
        for kind, field in enumerate((0, 2)):
            for packed, block, at in (
                (from_upper, 0, TOP - HALO),
                (from_lower, high - 8, TOP + rows + 8),
            ):
                r0 = strip.own_ninth(kind, group) + slot
                r1 = strip.edge_ninth(0, kind, group)
                r2 = strip.edge_ninth(1, kind, group)
                halo = (packed[r0 : r0 + 1], packed[r1 : r1 + 1], packed[r2 : r2 + 1])
                for tile, value in enumerate(tiles_of(*halo, slot, field)):
                    for copy in both:
                        targets[field][copy, tile, z + LEAD, block : block + 8] = zero
                    place(field, tile, z + LEAD, at, value)

    def edges_of(z, carry):
        here = layer[z + 1] * 18
        there = {d: layer[z + 1 + d] * 18 for d in (-1, 0, 1)}
        own_g = [table[here + c] for c in range(9)]
        next_g = [table[there[o[0]] + c] for c, o in enumerate(OFFSETS)]
        flow_g = [table[here + 9 + c] + table[there[o[0]] + 9 + c] for c, o in enumerate(OFFSETS)]
        for tile in both:
            for block in range(inner + 2):
                at = 8 * block
                m = med[0, tile, z + LEAD, at : at + 8]
                v = pot[0, tile, z + LEAD, at : at + 8]
                inside = jnp.minimum(m, 1.0)
                tissue = jnp.maximum(m - 1.0, 0.0)
                bath = (inside - tissue) * (0.5 * bath_sigma)
                for column, (dz, dx, dy) in enumerate(OFFSETS):
                    if block == (0 if dx < 0 else inner + 1):
                        continue
                    row = at + dx
                    n = med[dy, tile, z + LEAD + dz, row : row + 8]
                    w = pot[dy, tile, z + LEAD + dz, row : row + 8]
                    n_in = jnp.minimum(n, 1.0)
                    n_ti = jnp.maximum(n - 1.0, 0.0)
                    mine = tissue * own_g[column]
                    other = n_ti * next_g[column]
                    if column < 3:
                        mine = mine + bath
                        other = other + (n_in - n_ti) * (0.5 * bath_sigma)
                    edge[column, tile, z + LEAD, at : at + 8] = n_in * mine + inside * other
                    vec[column, tile, z + LEAD, at : at + 8] = (
                        (tissue * n_ti) * flow_g[column]
                    ) * (w - v)
        return carry

    lax.fori_loop(0, planes, edges_of, 0)

    def lift(slot, side, z):
        for plane in range(CHUNK):
            for tile in both:
                for block in range(inner):
                    at = 8 + 8 * block
                    vec_l[side, tile, z + plane + LEAD, at : at + 8] = roll(
                        vec[slot, tile, z + plane + LEAD, at : at + 8], LANES - 1
                    )

    slot_of = lambda number: number - 1 if number else VECS

    def start_of(step, carry):
        base = step * CHUNK
        lift(slot_of(0), 0, base - CHUNK)
        for tile in both:
            for plane in range(CHUNK):
                z = base + plane
                for block in range(inner):
                    at = 8 + 8 * block
                    late_e, late_f = zero, zero
                    diagonal, flow = zero, zero
                    for column, (dz, dx, dy) in enumerate(OFFSETS):
                        back = (tile, z + LEAD - dz, slice(at - dx, at - dx + 8))
                        e = edge[(column,) + back]
                        f = vec[(column,) + back]
                        if dy:
                            late_e, late_f = late_e + e, late_f + f
                        else:
                            diagonal, flow = diagonal + e, flow - f
                        diagonal = diagonal + edge[column, tile, z + LEAD, at : at + 8]
                        flow = flow + vec[column, tile, z + LEAD, at : at + 8]
                    diagonal = diagonal + roll(late_e, 1)
                    flow = flow - roll(late_f, 1)
                    inside = jnp.minimum(med[0, tile, z + LEAD, at : at + 8], 1.0)
                    residual = flow + inside * (src[tile, z + LEAD, at : at + 8] - mean)
                    size = jnp.maximum(diagonal, 1.0)
                    scale = inside / size
                    jac[tile, z + LEAD, at : at + 8] = scale
                    kap[tile, z + LEAD, at : at + 8] = jnp.maximum(inside - diagonal, 0.0)
                    met[tile, z + LEAD, at : at + 8] = inside * size
                    vec[slot_of(0), tile, z + LEAD, at : at + 8] = scale * residual
        return carry

    lax.fori_loop(0, planes // CHUNK, start_of, 0)
    lift(slot_of(0), 0, planes - CHUNK)

    for step in range(ITERS):
        now, later, before = slot_of(step), slot_of(step + 1), slot_of(max(step - 1, 0))
        side, side_next = step % 2, (step + 1) % 2
        reach = ITERS - 1 - step
        low = jnp.maximum(first - reach, 0) // CHUNK
        up = (jnp.minimum(first + own_planes + reach, planes) + CHUNK - 1) // CHUNK

        def apply(number, carry):
            base = number * CHUNK
            if step + 1 < ITERS:
                lift(later, side_next, base - CHUNK)
            for tile in both:
                for block in range(inner):
                    at = 8 + 8 * block
                    for plane in range(CHUNK):
                        z = base + plane
                        total, late = zero, zero
                        for column, (dz, dx, dy) in enumerate(OFFSETS):
                            back = (tile, z + LEAD - dz, slice(at - dx, at - dx + 8))
                            product = edge[(column,) + back] * vec[(now,) + back]
                            if dy:
                                late = late + product
                            else:
                                total = total + product
                            ahead = (tile, z + LEAD + dz, slice(at + dx, at + dx + 8))
                            value = vec_l[(side,) + ahead] if dy else vec[(now,) + ahead]
                            total = total + edge[column, tile, z + LEAD, at : at + 8] * value
                        cell = (tile, z + LEAD, slice(at, at + 8))
                        total = total + kap[cell] * vec[(now,) + cell]
                        value = jac[cell] * (total + roll(late, 1))
                        if step:
                            value = 2.0 * value - vec[(before,) + cell]
                        vec[(later,) + cell] = value
            return carry

        lax.fori_loop(low, up, apply, 0)
        if step + 1 < ITERS:
            lift(later, side_next, (up - 1) * CHUNK)

    def joined(value):
        low = roll(value[0], LANES - SLOT)
        up = roll(value[1], SLOT)
        return jnp.where(lane < LANES // 2, low, up)

    def own_of(number, carry):
        for plane in range(CHUNK):
            z = number * CHUNK + plane
            for block in range(rows // 8):
                at = TOP + 8 * block
                out = 8 * block
                cell = lambda tile: (tile, first + z + LEAD, slice(at, at + 8))
                metric[z, out : out + 8] = joined([met[cell(tile)] for tile in both])
                for index in range(VECS):
                    basis[index, z, out : out + 8] = joined(
                        [vec[(slot_of(index),) + cell(tile)] for tile in both]
                    )
        return carry

    lax.fori_loop(0, own_planes // CHUNK, own_of, 0)

    pairs = [(i, j) for i in range(VECS) for j in range(i, VECS)]
    half = 26
    rowsum[...] = jnp.zeros(rowsum.shape, jnp.float32)
    for part, plain in ((pairs[:half], False), (pairs[half:], True)):

        def gather(z, carry):
            carry = list(carry)
            for block in range(rows // 8):
                out = 8 * block
                weight = metric[z, out : out + 8]
                used = range(VECS) if plain else sorted({k for pair in part for k in pair})
                loaded = {k: basis[k, z, out : out + 8] for k in used}
                scaled = {i: loaded[i] * weight for i in {i for i, _ in part} | ({0} if plain else set())}
                for number, (i, j) in enumerate(part):
                    carry[number] = carry[number] + scaled[i] * loaded[j]
                if plain:
                    for k in range(ITERS):
                        carry[len(part) + k] = carry[len(part) + k] + loaded[k]
                    carry[-1] = carry[-1] + scaled[0]
            return tuple(carry)

        count = len(part) + (ITERS + 1 if plain else 0)
        done = lax.fori_loop(0, own_planes, gather, tuple(zero for _ in range(count)))
        done = [jnp.sum(value, axis=0, keepdims=True) for value in done]
        for (i, j), value in zip(part, done):
            rowsum[VECS * i + j : VECS * i + j + 1] = value
            if i != j:
                rowsum[VECS * j + i : VECS * j + i + 1] = value
        for k, value in enumerate(done[len(part) :]):
            rowsum[SUMS + k : SUMS + k + 1] = value
    row = lax.dot_general(
        jnp.ones((8, LANES), jnp.float32),
        rowsum[...],
        (((1,), (1,)), ((), ())),
        precision=lax.Precision.HIGHEST,
        preferred_element_type=jnp.float32,
    )
    for at in range(0, gram.shape[0], 8):
        gram[at : at + 8] = row


def finish(geometry, gathered, total_in, basis, metric, solution_ref, residual_ref, flag):
    own_planes, rows = geometry
    total = jnp.sum(gathered[...], axis=0, keepdims=True)
    count = jnp.sum(total_in[0:1], axis=1, keepdims=True)
    lane = lane_iota((16, LANES))
    sub = lax.broadcasted_iota(jnp.int32, (16, LANES), 0)
    matrix = jnp.zeros((16, LANES), jnp.float32)
    for i in range(VECS):
        line = roll(total, LANES - VECS * i)
        matrix = jnp.where(sub == i, jnp.broadcast_to(line, (16, LANES)), matrix)
    matrix = jnp.where(lane < VECS, matrix, 0.0)
    reflected = jnp.where(lane == 0, roll(matrix, LANES - 1), roll(matrix, 1))
    square = matrix - 0.5 * (roll(matrix, LANES - 1) + reflected)
    system = jnp.where(lane < ITERS, square, 0.0)
    system = jnp.where(lane == ITERS, roll(matrix, ITERS), system)[0:8]
    lane8 = lane[0:8]
    sub8 = sub[0:8]
    for k in range(ITERS):
        line = system[k : k + 1]
        pivot = jnp.sum(jnp.where(lane8[0:1] == k, line, 0.0), axis=1, keepdims=True)
        line = line / pivot
        column = jnp.sum(jnp.where(lane8 == k, system, 0.0), axis=1, keepdims=True)
        line8 = jnp.broadcast_to(line, (8, LANES))
        system = jnp.where(sub8 == k, line8, system - column * line8)
    answer = jnp.sum(jnp.where(lane8 == ITERS, system, 0.0), axis=1, keepdims=True)
    coef = [answer[k : k + 1] for k in range(ITERS)]
    zero = jnp.zeros((1, 1), jnp.float32)
    padded = coef + [zero, zero]
    weights = []
    for i in range(VECS):
        value = 0.5 * padded[i + 1] - padded[i]
        if i == 0:
            value = value + 1.0
        elif i == 1:
            value = value + padded[0]
        else:
            value = value + 0.5 * padded[i - 1]
        weights.append(value)
    sums = [total[:, SUMS + k : SUMS + k + 1] for k in range(ITERS + 1)]
    mean = zero
    for k in range(ITERS):
        mean = mean + coef[k] * sums[k]
    mean = mean / count
    drift = sums[ITERS] / count
    column = jnp.concatenate(weights + [zero] * (16 - VECS), axis=0)
    row = jnp.zeros((1, LANES), jnp.float32)
    for i in range(VECS):
        row = jnp.where(lane[0:1] == i, weights[i], row)
    size = jnp.sum(jnp.sum(matrix * column * row, axis=1, keepdims=True), axis=0, keepdims=True)
    diagonal = jnp.sum(jnp.where(lane == sub, matrix, 0.0), axis=1, keepdims=True)
    spread = jnp.sum(jnp.abs(column) * jnp.sqrt(diagonal), axis=0, keepdims=True)
    flag[...] = jnp.broadcast_to(spread * spread / size, (8, LANES))

    def combine(z, carry):
        for block in range(rows // 8):
            out = 8 * block
            weight = metric[z, out : out + 8]
            inside = jnp.minimum(weight, 1.0)
            phi = inside * (-mean)
            rest = jnp.zeros((8, LANES), jnp.float32)
            for k in range(VECS):
                value = basis[k, z, out : out + 8]
                if k < ITERS:
                    phi = phi + coef[k] * value
                rest = rest + weights[k] * value
            solution_ref[z, out : out + 8] = phi
            residual_ref[z, out : out + 8] = weight * rest - inside * drift
        return carry

    lax.fori_loop(0, own_planes, combine, 0)


def f32(*shape):
    return jax.ShapeDtypeStruct(shape, jnp.float32)


def cyclic(count, shift):
    return [(i, (i + shift) % count) for i in range(count)]


def fast(potential, tissue_mask, layer_index, source):
    own_planes, rows, width = tissue_mask.shape
    gx, gy, gz = (lax.axis_size(name) for name in ("gx", "gy", "gz"))
    params = pltpu.CompilerParams(vmem_limit_bytes=60 * 1024 * 1024)
    stacked = jnp.stack([potential, source, tissue_mask.astype(jnp.float32)])

    full = gz * own_planes <= own_planes + 2 * HALO
    fields, layers = [stacked], [layer_index]
    if full:
        planes = gz * own_planes
        for shift in range(1, gz):
            fields.append(lax.ppermute(stacked, "gz", cyclic(gz, shift)))
            layers.append(lax.ppermute(layer_index, "gz", cyclic(gz, shift)))
    else:
        planes = own_planes + 2 * HALO
        left, hop = HALO, 1
        while left > 0:
            size = min(left, own_planes)
            up = [(i, i + hop) for i in range(gz - hop)]
            down = [(j, i) for i, j in up]
            fields.append(lax.ppermute(stacked[:, own_planes - size :], "gz", up))
            layers.append(lax.ppermute(layer_index[own_planes - size :], "gz", up))
            fields.append(lax.ppermute(stacked[:, :size], "gz", down))
            layers.append(lax.ppermute(layer_index[:size], "gz", down))
            left -= size
            hop += 1
    pieces = tuple(field.shape[1] for field in fields)
    summed = planes if full else own_planes
    groups = -(-planes // 8)
    y_rows = 3 * groups * rows + 8

    to_left, to_right, sums = pl.pallas_call(
        functools.partial(pack_y, (pieces, summed, rows)),
        out_shape=(f32(y_rows, LANES), f32(y_rows, LANES), f32(8, LANES)),
        in_specs=[VMEM] * len(pieces),
        out_specs=(VMEM,) * 3,
        compiler_params=params,
        name="pack_y",
    )(*fields)
    from_left = lax.ppermute(to_right, "gy", cyclic(gy, 1))
    from_right = lax.ppermute(to_left, "gy", cyclic(gy, gy - 1))
    others = [sums] + [lax.ppermute(sums, "gy", cyclic(gy, s)) for s in range(2, gy - 1)]

    strip = Strip(planes)
    upper, lower, sums = pl.pallas_call(
        functools.partial(pack_x, (pieces, rows, len(others))),
        out_shape=(f32(strip.rows, LANES), f32(strip.rows, LANES), f32(8, LANES)),
        in_specs=[VMEM] * (len(pieces) + 2 + len(others)),
        out_specs=(VMEM,) * 3,
        compiler_params=params,
        name="pack_x",
    )(*fields, from_left, from_right, *others)
    forth = [(i, i + 1) for i in range(gx - 1)]
    from_upper = lax.ppermute(lower, "gx", forth)
    from_lower = lax.ppermute(upper, "gx", [(j, i) for i, j in forth])
    extra = [lax.ppermute(sums, "gx", cyclic(gx, s)) for s in range(2, gx - 1)]
    extra.append(lax.ppermute(sums, "gx", [(0, gx - 1), (gx - 1, 0)]))
    if not full:
        sums = sums + from_upper[strip.sums :] + from_lower[strip.sums :] + sum(extra)
        sums = lax.psum(sums, "gz")
        extra = []

    table = np.concatenate(
        [
            0.5 * tensor_table(LAYERS, bulk_long, bulk_trans),
            0.5 * tensor_table(LAYERS, intra_long, intra_trans),
        ],
        axis=1,
    ).reshape(-1)
    high = TOP + rows + 16
    grid = (2, planes + LEAD + 1, high, LANES)
    everyone = gx * gy * gz
    gram, basis, metric, total = pl.pallas_call(
        functools.partial(krylov, (pieces, planes, own_planes, rows, len(extra), full, gz, gy)),
        out_shape=(
            f32(everyone, LANES),
            f32(VECS, own_planes, rows, LANES),
            f32(own_planes, rows, LANES),
            f32(8, LANES),
        ),
        in_specs=[SMEM] * (1 + len(pieces)) + [VMEM] * (len(pieces) + 5 + len(extra)),
        out_specs=(VMEM,) * 4,
        scratch_shapes=[
            pltpu.SMEM((planes + 2,), jnp.int32),
            pltpu.VMEM((2,) + grid, jnp.float32),
            pltpu.VMEM((2,) + grid, jnp.float32),
            pltpu.VMEM(grid, jnp.float32),
            pltpu.VMEM((len(OFFSETS),) + grid, jnp.float32),
            pltpu.VMEM((VECS + 1,) + grid, jnp.float32),
            pltpu.VMEM((2,) + grid, jnp.float32),
            pltpu.VMEM(grid, jnp.float32),
            pltpu.VMEM(grid, jnp.float32),
            pltpu.VMEM(grid, jnp.float32),
            pltpu.VMEM((LANES, LANES), jnp.float32),
        ],
        compiler_params=params,
        name="krylov",
    )(
        jnp.asarray(table),
        *layers,
        *fields,
        from_left,
        from_right,
        from_upper,
        from_lower,
        sums,
        *extra,
    )
    gathered = lax.all_to_all(gram, ("gx", "gy", "gz"), 0, 0, tiled=True)
    answer, residual, flag = pl.pallas_call(
        functools.partial(finish, (own_planes, rows)),
        out_shape=(f32(own_planes, rows, LANES), f32(own_planes, rows, LANES), f32(8, LANES)),
        in_specs=[VMEM] * 4,
        out_specs=(VMEM,) * 3,
        compiler_params=params,
        name="finish",
    )(gathered, total, basis, metric)
    return answer, residual, flag


def body(potential, tissue_mask, layer_index, source):
    answer, residual, flag = fast(potential, tissue_mask, layer_index, source)
    return (answer, residual)


def solution(mesh):
    placed = (P("gz", "gx", "gy"), P("gz", "gx", "gy"), P("gz"), P("gz", "gx", "gy"))
    return jax.shard_map(
        body,
        mesh=mesh,
        in_specs=placed,
        out_specs=(P("gz", "gx", "gy"), P("gz", "gx", "gy")),
        check_vma=False,
    )
```

time: 89.1 us -> 80.7 us (0.906)
  Pallas kernels: 47 us -> 39.2 us
  starting transfers between devices: 11 us -> 18 us
  waiting for transfers between devices: 13.9 us -> 8.39 us
  other arithmetic: 2.3 us -> 0.96 us
    pallas_call x1, Pallas kernels: 38.9 us -> 31.3 us  [fast(): pl.pallas_call(functools.partial(krylov, (pieces, planes, own_planes, row...]
    ppermute x5 -> x6, starting transfers between devices: 5.18 us -> 12.2 us  [the longest x1 6.58 us: fast(): extra.append(lax.ppermute(sums, 'gx', [(0, gx - 1), (gx - 1, 0)]))]
    ppermute x5 -> x6, waiting for transfers between devices: 11.2 us -> 5.61 us  [the longest x1 2.13 us: fast(): extra.append(lax.ppermute(sums, 'gx', [(0, gx - 1), (gx - 1, 0)]))]
    unnamed x26 -> x30, local copies, waits for them, and re-layouts: 2.1 us -> 2.78 us
  transfers between devices with their start and end apart: 8 -> 9, of which waited for: 4 -> 6; matrix products, arithmetic and copies ran while one was open for 2% -> 0% of each run, Pallas kernels for 0% -> 0%
where the time goes in v2:
time: 80.7 us; the launch traced here: 80.3 us
  Pallas kernels  39.2 us (49%)
  starting transfers between devices  18 us (22%)
  blocking collectives  10.2 us (13%)
  waiting for transfers between devices  8.39 us (10%)
  local copies, waits for them, and re-layouts  2.78 us (3%)
  other arithmetic  0.96 us (1%)
    pallas_call x1, Pallas kernels, fast(): pl.pallas_call(functools.partial(krylov, (pieces, planes, own_planes, row...  31.3 us
    all_to_all x1, blocking collectives, fast(): gathered = lax.all_to_all(gram, ('gx', 'gy', 'gz'), 0, 0, tiled=True)  10.2 us
    ppermute x1, starting transfers between devices, fast(): extra.append(lax.ppermute(sums, 'gx', [(0, gx - 1), (gx - 1, 0)]))  6.58 us
    pallas_call x1, Pallas kernels, fast(): pl.pallas_call(functools.partial(finish, (own_planes, rows)), out_shape=(...  3.98 us
    ppermute x1, starting transfers between devices, fast(): from_upper = lax.ppermute(lower, 'gx', forth)  3.62 us
    ppermute x1, starting transfers between devices, fast(): from_left = lax.ppermute(to_right, 'gy', cyclic(gy, 1))  2.85 us
    unnamed x30, local copies, waits for them, and re-layouts  2.78 us
    ppermute x1, waiting for transfers between devices, fast(): extra.append(lax.ppermute(sums, 'gx', [(0, gx - 1), (gx - 1, 0)]))  2.13 us
  transfers between devices with their start and end apart: 9, of which 6 were waited for; matrix products, arithmetic and copies ran while one was open for 0% of the time, Pallas kernels for 0%

profile of v2, /device:TPU:0, one launch (start us, length us, event | category | flops | bytes accessed | tf_op | source)
XLA Modules:
  0.0 80.3 jit_solution(15302056031984890235)
XLA Ops:
  0.6 0.0 copy-start.6
  0.6 0.0 copy-start.7
  0.6 0.9 %convert_bitcast_fusion = f32[1,8,24,128]{3,2,1,0:T(8,128)S(1)} fusion(s32[8,24,128]{2,1,0:T(8,128)} %param.6), kind=kLoop, calls=%fused_computation.1 | loop fusion | flops 24576 | bytes 196608 | tf_op jit(solution)/shard_map/stack | solution.py:559
  1.6 0.0 copy-done.6
  1.6 0.0 copy-done.7
  1.6 0.0 copy-start
  1.7 0.6 collective-permute-start.1
  2.2 1.2 %collective-permute-done.1.refs_1_.refs_3_ = f32[3,8,24,128]{3,2,1,0:T(8,128)S(1)} collective-permute-done((f32[3,8,24,128]{3,2,1,0:T(8,128)S(1)}, f32[3,8,24,128]{3,2,1,0:T(8,128)S(1)}, u32[]{:S(2)}, u32[]{:S(2)}) %collective-permute-start.1) | collective-permute-done | bytes 294944 | tf_op jit(solution)/shard_map/ppermute | solution.py:566
  3.4 0.0 copy-done
  3.4 0.0 copy-start.1
  3.4 0.7 copy-done.1
  4.1 2.0 %pack_y.1 = (f32[152,128]{1,0:T(8,128)}, f32[152,128]{1,0:T(8,128)}, f32[8,128]{1,0:T(8,128)}) custom-call(f32[3,8,24,128]{3,2,1,0:T(8,128)} %copy-done, f32[3,8,24,128]{3,2,1,0:T(8,128)} %copy-done.1), custom_call_target="tpu_custom_call" | custom-call | tf_op jit(solution)/shard_map/pack_y/pallas_call | solution.py:586
  6.2 0.0 copy-start.11
  6.2 2.8 %collective-permute-start.2 = (f32[152,128]{1,0:T(8,128)}, f32[152,128]{1,0:T(8,128)S(1)}, u32[]{:S(2)}, u32[]{:S(2)}) collective-permute-start(f32[152,128]{1,0:T(8,128)} %get-tuple-element.14), channel_id=1, source_target_pairs={{0,2},{2,4},{4,6},{6,0},{1,3},{3,5},{5,7},{7,1},{8,10},{10,12},{12... | collective-permute-start | bytes 233480 | tf_op jit(solution)/shard_map/ppermute | solution.py:594
  9.0 1.0 %collective-permute-start.3 = (f32[152,128]{1,0:T(8,128)}, f32[152,128]{1,0:T(8,128)S(1)}, u32[]{:S(2)}, u32[]{:S(2)}) collective-permute-start(f32[152,128]{1,0:T(8,128)} %get-tuple-element.15), channel_id=1, source_target_pairs={{0,6},{2,0},{4,2},{6,4},{1,7},{3,1},{5,3},{7,5},{8,14},{10,8},{12,... | collective-permute-start | bytes 233480 | tf_op jit(solution)/shard_map/ppermute | solution.py:595
  10.0 0.0 copy-done.11
  10.0 1.9 %collective-permute-start.4 = (f32[8,128]{1,0:T(8,128)S(1)}, f32[8,128]{1,0:T(8,128)S(1)}, u32[]{:S(2)}, u32[]{:S(2)}) collective-permute-start(f32[8,128]{1,0:T(8,128)S(1)} %copy-done.11), channel_id=1, source_target_pairs={{0,4},{2,6},{4,0},{6,2},{1,5},{3,7},{5,1},{7,3},{8,12},{10,14},{12... | collective-permute-start | bytes 12296 | tf_op jit(solution)/shard_map/ppermute | solution.py:596
  12.0 1.7 %collective-permute-done.4.refs_5_ = f32[8,128]{1,0:T(8,128)S(1)} collective-permute-done((f32[8,128]{1,0:T(8,128)S(1)}, f32[8,128]{1,0:T(8,128)S(1)}, u32[]{:S(2)}, u32[]{:S(2)}) %collective-permute-start.4) | collective-permute-done | bytes 4128 | tf_op jit(solution)/shard_map/ppermute | solution.py:596
  13.6 0.0 copy-start.12
  13.6 0.0 collective-permute-done.2.refs_2_.refs_4_
  13.6 0.0 copy-start.2
  13.6 1.1 %collective-permute-done.3.refs_3_.refs_5_ = f32[152,128]{1,0:T(8,128)S(1)} collective-permute-done((f32[152,128]{1,0:T(8,128)}, f32[152,128]{1,0:T(8,128)S(1)}, u32[]{:S(2)}, u32[]{:S(2)}) %collective-permute-start.3) | collective-permute-done | bytes 77856 | tf_op jit(solution)/shard_map/ppermute | solution.py:595
  14.8 0.0 copy-done.12
  14.8 0.0 copy-done.2
  14.8 0.0 copy-start.3
  14.8 0.6 copy-done.3
  15.4 2.0 %pack_x.1 = (f32[528,128]{1,0:T(8,128)}, f32[528,128]{1,0:T(8,128)}, f32[8,128]{1,0:T(8,128)}) custom-call(f32[3,8,24,128]{3,2,1,0:T(8,128)} %copy-done, f32[3,8,24,128]{3,2,1,0:T(8,128)} %copy-done.1, f32[152,128]{1,0:T(8,128)} %copy-done.2, f32[152,128]{1,0:T(8,128)} %copy-done.3, f32[8,128]{1,0:T(8,128)} %get-tuple-element.16.refs_4_, f32[8,128]{1,0:T(8,128)} %copy-done.12), custom_call_target="tpu_custom_call" | custom-call | tf_op jit(solution)/shard_map/pack_x/pallas_call | solution.py:599
  17.4 3.6 %collective-permute-start.5 = (f32[528,128]{1,0:T(8,128)}, f32[528,128]{1,0:T(8,128)S(1)}, u32[]{:S(2)}, u32[]{:S(2)}) collective-permute-start(f32[528,128]{1,0:T(8,128)} %get-tuple-element.17), channel_id=1, source_target_pairs={{0,8},{8,16},{16,24},{1,9},{9,17},{17,25},{2,10},{10,18},{18,26},{... | collective-permute-start | bytes 811016 | tf_op jit(solution)/shard_map/ppermute | solution.py:608
  21.0 0.0 copy-start.13
  21.0 1.3 %collective-permute-start.6 = (f32[528,128]{1,0:T(8,128)}, f32[528,128]{1,0:T(8,128)S(1)}, u32[]{:S(2)}, u32[]{:S(2)}) collective-permute-start(f32[528,128]{1,0:T(8,128)} %get-tuple-element.18), channel_id=1, source_target_pairs={{8,0},{16,8},{24,16},{9,1},{17,9},{25,17},{10,2},{18,10},{26,18},{... | collective-permute-start | bytes 811016 | tf_op jit(solution)/shard_map/ppermute | solution.py:609
  22.3 0.0 copy-done.8
  22.3 6.6 %collective-permute-start.8 = (f32[8,128]{1,0:T(8,128)S(1)}, f32[8,128]{1,0:T(8,128)S(1)}, u32[]{:S(2)}, u32[]{:S(2)}) collective-permute-start(f32[8,128]{1,0:T(8,128)S(1)} %copy-done.8), channel_id=1, source_target_pairs={{0,24},{24,0},{1,25},{25,1},{2,26},{26,2},{3,27},{27,3},{4,28},{28... | collective-permute-start | bytes 12296 | tf_op jit(solution)/shard_map/ppermute | solution.py:611
  28.9 0.1 collective-permute-start.7
  29.0 0.0 copy-done.13
  29.0 0.1 collective-permute-start
  29.1 1.1 %collective-permute-done.refs_1_ = s32[8]{0:T(128)S(1)} collective-permute-done((s32[8]{0:T(128)S(1)}, s32[8]{0:T(128)S(1)}, u32[]{:S(2)}, u32[]{:S(2)}) %collective-permute-start) | collective-permute-done | bytes 64 | tf_op jit(solution)/shard_map/ppermute | solution.py:567
  30.2 2.1 %collective-permute-done.8.refs_10_ = f32[8,128]{1,0:T(8,128)S(1)} collective-permute-done((f32[8,128]{1,0:T(8,128)S(1)}, f32[8,128]{1,0:T(8,128)S(1)}, u32[]{:S(2)}, u32[]{:S(2)}) %collective-permute-start.8) | collective-permute-done | bytes 4128 | tf_op jit(solution)/shard_map/ppermute | solution.py:611
  32.3 1.1 %collective-permute-done.7.refs_9_ = f32[8,128]{1,0:T(8,128)S(1)} collective-permute-done((f32[8,128]{1,0:T(8,128)S(1)}, f32[8,128]{1,0:T(8,128)S(1)}, u32[]{:S(2)}, u32[]{:S(2)}) %collective-permute-start.7) | collective-permute-done | bytes 4128 | tf_op jit(solution)/shard_map/ppermute | solution.py:610
  33.5 0.0 collective-permute-done.5.refs_6_
  33.5 0.0 collective-permute-done.6.refs_7_
  33.5 0.0 copy-done.14
  33.5 0.0 copy-done.9
  33.5 0.6 copy-done.10
  34.0 0.1 copy-done.4
  34.2 0.7 copy-done.5
  34.9 31.3 %krylov.1 = (f32[32,128]{1,0:T(8,128)}, f32[9,8,24,128]{3,2,1,0:T(8,128)}, f32[8,24,128]{2,1,0:T(8,128)}, f32[8,128]{1,0:T(8,128)}) custom-call(f32[288]{0:T(512)} %constant.2.clone.table, s32[8]{0:T(128)} %refs_0_.1, s32[8]{0:T(128)} %copy-done.14, f32[3,8,24,128]{3,2,1,0:T(8,128)} %copy-done, f32[3,8,24,128]{3,2,1,0:T(8,128)} %copy-done.1, ...), custom_call_target="tpu_custom_call" | custom-call | tf_op jit(solution)/shard_map/krylov/pallas_call | solution.py:627
  66.1 10.2 %all_to_all.11 = f32[32,1,128]{2,1,0:T(1,128)} all-to-all(f32[32,1,128]{2,1,0:T(1,128)} %bitcast.11), channel_id=1, replica_groups=mesh['gx'=4,'gy'=4,'gz'=2] {'gx','gy','gz'}, dimensions={0} | all-to-all | bytes 32768 | tf_op jit(solution)/shard_map/all_to_all | solution.py:663
  76.3 4.0 %finish.1 = (f32[8,24,128]{2,1,0:T(8,128)}, f32[8,24,128]{2,1,0:T(8,128)}, f32[8,128]{1,0:T(8,128)}) custom-call(f32[32,128]{1,0:T(8,128)} %bitcast.10, f32[8,128]{1,0:T(8,128)} %get-tuple-element.21.total_in, f32[9,8,24,128]{3,2,1,0:T(8,128)} %get-tuple-element.22.basis, f32[8,24,128]{2,1,0:T(8,128)} %get-tuple-element.23.metric), custom_call_target="tpu_custom_call" | custom-call | tf_op jit(solution)/shard_map/finish/pallas_call | solution.py:664
  (7 shorter events, 0.0 us)
Async XLA Ops:
  0.6 1.0 %copy-start.6 = (f32[8,24,128]{2,1,0:T(8,128)S(1)}, f32[8,24,128]{2,1,0:T(8,128)}, u32[]{:S(2)}) copy-start(f32[8,24,128]{2,1,0:T(8,128)} %param.8) | copy-start | bytes 294916
  0.6 1.0 %copy-start.7 = (f32[8,24,128]{2,1,0:T(8,128)S(1)}, f32[8,24,128]{2,1,0:T(8,128)}, u32[]{:S(2)}) copy-start(f32[8,24,128]{2,1,0:T(8,128)} %param.5) | copy-start | bytes 294916
  1.6 1.8 %copy-start = (f32[3,8,24,128]{3,2,1,0:T(8,128)}, f32[3,8,24,128]{3,2,1,0:T(8,128)S(1)}, u32[]{:S(2)}) copy-start(f32[3,8,24,128]{3,2,1,0:T(8,128)S(1)} %pad_maximum_fusion.refs_0_.refs_2_) | copy-start | bytes 884740
  1.7 1.8 %collective-permute-start.1 = (f32[3,8,24,128]{3,2,1,0:T(8,128)S(1)}, f32[3,8,24,128]{3,2,1,0:T(8,128)S(1)}, u32[]{:S(2)}, u32[]{:S(2)}) collective-permute-start(f32[3,8,24,128]{3,2,1,0:T(8,128)S(1)} %pad_maximum_fusion.refs_0_.refs_2_), channel_id=1, source_target_pairs={{0,1},{1,0},{2,3},{3,2},{4,5},{5,4},{6,7},{7,6},{8,9},{9,8},{10,11... | collective-permute-start | bytes 884744 | tf_op jit(solution)/shard_map/ppermute | solution.py:566
  3.4 0.7 copy-start.1
  6.2 3.9 %copy-start.11 = (f32[8,128]{1,0:T(8,128)S(1)}, f32[8,128]{1,0:T(8,128)}, u32[]{:S(2)}) copy-start(f32[8,128]{1,0:T(8,128)} %get-tuple-element.16.refs_4_) | copy-start | bytes 12292
  6.2 7.5 %collective-permute-start.2 = (f32[152,128]{1,0:T(8,128)}, f32[152,128]{1,0:T(8,128)S(1)}, u32[]{:S(2)}, u32[]{:S(2)}) collective-permute-start(f32[152,128]{1,0:T(8,128)} %get-tuple-element.14), channel_id=1, source_target_pairs={{0,2},{2,4},{4,6},{6,0},{1,3},{3,5},{5,7},{7,1},{8,10},{10,12},{12... | collective-permute-start | bytes 233480 | tf_op jit(solution)/shard_map/ppermute | solution.py:594
  9.0 5.7 %collective-permute-start.3 = (f32[152,128]{1,0:T(8,128)}, f32[152,128]{1,0:T(8,128)S(1)}, u32[]{:S(2)}, u32[]{:S(2)}) collective-permute-start(f32[152,128]{1,0:T(8,128)} %get-tuple-element.15), channel_id=1, source_target_pairs={{0,6},{2,0},{4,2},{6,4},{1,7},{3,1},{5,3},{7,5},{8,14},{10,8},{12,... | collective-permute-start | bytes 233480 | tf_op jit(solution)/shard_map/ppermute | solution.py:595
  10.0 3.6 %collective-permute-start.4 = (f32[8,128]{1,0:T(8,128)S(1)}, f32[8,128]{1,0:T(8,128)S(1)}, u32[]{:S(2)}, u32[]{:S(2)}) collective-permute-start(f32[8,128]{1,0:T(8,128)S(1)} %copy-done.11), channel_id=1, source_target_pairs={{0,4},{2,6},{4,0},{6,2},{1,5},{3,7},{5,1},{7,3},{8,12},{10,14},{12... | collective-permute-start | bytes 12296 | tf_op jit(solution)/shard_map/ppermute | solution.py:596
  13.6 1.1 %copy-start.12 = (f32[8,128]{1,0:T(8,128)}, f32[8,128]{1,0:T(8,128)S(1)}, u32[]{:S(2)}) copy-start(f32[8,128]{1,0:T(8,128)S(1)} %collective-permute-done.4.refs_5_) | copy-start | bytes 12292
  13.6 1.1 %copy-start.2 = (f32[152,128]{1,0:T(8,128)}, f32[152,128]{1,0:T(8,128)S(1)}, u32[]{:S(2)}) copy-start(f32[152,128]{1,0:T(8,128)S(1)} %collective-permute-done.2.refs_2_.refs_4_) | copy-start | bytes 233476
  14.8 0.6 copy-start.3
  17.4 4.9 %copy-start.8 = (f32[8,128]{1,0:T(8,128)S(1)}, f32[8,128]{1,0:T(8,128)}, u32[]{:S(2)}) copy-start(f32[8,128]{1,0:T(8,128)} %get-tuple-element.19.refs_8_) | copy-start | bytes 12292
  17.4 16.1 %collective-permute-start.5 = (f32[528,128]{1,0:T(8,128)}, f32[528,128]{1,0:T(8,128)S(1)}, u32[]{:S(2)}, u32[]{:S(2)}) collective-permute-start(f32[528,128]{1,0:T(8,128)} %get-tuple-element.17), channel_id=1, source_target_pairs={{0,8},{8,16},{16,24},{1,9},{9,17},{17,25},{2,10},{10,18},{18,26},{... | collective-permute-start | bytes 811016 | tf_op jit(solution)/shard_map/ppermute | solution.py:608
  21.0 8.0 %copy-start.13 = (s32[8]{0:T(128)S(1)}, s32[8]{0:T(128)}, u32[]{:S(2)}) copy-start(s32[8]{0:T(128)} %refs_0_.1) | copy-start | bytes 100
  21.0 12.5 %collective-permute-start.6 = (f32[528,128]{1,0:T(8,128)}, f32[528,128]{1,0:T(8,128)S(1)}, u32[]{:S(2)}, u32[]{:S(2)}) collective-permute-start(f32[528,128]{1,0:T(8,128)} %get-tuple-element.18), channel_id=1, source_target_pairs={{8,0},{16,8},{24,16},{9,1},{17,9},{25,17},{10,2},{18,10},{26,18},{... | collective-permute-start | bytes 811016 | tf_op jit(solution)/shard_map/ppermute | solution.py:609
  22.3 10.0 %collective-permute-start.8 = (f32[8,128]{1,0:T(8,128)S(1)}, f32[8,128]{1,0:T(8,128)S(1)}, u32[]{:S(2)}, u32[]{:S(2)}) collective-permute-start(f32[8,128]{1,0:T(8,128)S(1)} %copy-done.8), channel_id=1, source_target_pairs={{0,24},{24,0},{1,25},{25,1},{2,26},{26,2},{3,27},{27,3},{4,28},{28... | collective-permute-start | bytes 12296 | tf_op jit(solution)/shard_map/ppermute | solution.py:611
  28.9 4.6 %collective-permute-start.7 = (f32[8,128]{1,0:T(8,128)S(1)}, f32[8,128]{1,0:T(8,128)S(1)}, u32[]{:S(2)}, u32[]{:S(2)}) collective-permute-start(f32[8,128]{1,0:T(8,128)S(1)} %copy-done.8), channel_id=1, source_target_pairs={{0,16},{8,24},{16,0},{24,8},{1,17},{9,25},{17,1},{25,9},{2,18},{10... | collective-permute-start | bytes 12296 | tf_op jit(solution)/shard_map/ppermute | solution.py:610
  29.0 1.2 %collective-permute-start = (s32[8]{0:T(128)S(1)}, s32[8]{0:T(128)S(1)}, u32[]{:S(2)}, u32[]{:S(2)}) collective-permute-start(s32[8]{0:T(128)S(1)} %copy-done.13), channel_id=1, source_target_pairs={{0,1},{1,0},{2,3},{3,2},{4,5},{5,4},{6,7},{7,6},{8,9},{9,8},{10,11... | collective-permute-start | bytes 104 | tf_op jit(solution)/shard_map/ppermute | solution.py:567
  30.2 3.3 %copy-start.14 = (s32[8]{0:T(128)}, s32[8]{0:T(128)S(1)}, u32[]{:S(2)}) copy-start(s32[8]{0:T(128)S(1)} %collective-permute-done.refs_1_) | copy-start | bytes 100
  32.3 1.1 %copy-start.9 = (f32[8,128]{1,0:T(8,128)}, f32[8,128]{1,0:T(8,128)S(1)}, u32[]{:S(2)}) copy-start(f32[8,128]{1,0:T(8,128)S(1)} %collective-permute-done.8.refs_10_) | copy-start | bytes 12292
  33.5 0.6 copy-start.10
  33.5 0.7 copy-start.4
  34.2 0.7 copy-start.5

commit v3 on v2

--- a/solution.py
+++ b/solution.py
@@ -136,18 +136,12 @@
 
 
 def pack_x(geometry, *refs):
-    pieces, rows, others = geometry
+    pieces, rows = geometry
     piece_refs = refs[: len(pieces)]
-    from_left, from_right = refs[len(pieces) : len(pieces) + 2]
-    other_refs = refs[len(pieces) + 2 : len(pieces) + 2 + others]
-    upper, lower, sums = refs[len(pieces) + 2 + others :]
+    from_left, from_right, total_ref, upper, lower = refs[len(pieces) :]
     listed = [(ref, plane) for ref, length in zip(piece_refs, pieces) for plane in range(length)]
     strip = Strip(len(listed))
-    last = 3 * strip.groups * rows
-    total = from_left[last : last + 8] + from_right[last : last + 8]
-    for ref in other_refs:
-        total = total + ref[...]
-    sums[...] = total
+    total = total_ref[...]
     for out, first, ninth in ((upper, 0, 8), (lower, rows - 8, rows - 9)):
         out[strip.ninth : strip.sums] = jnp.zeros((strip.sums - strip.ninth, LANES), jnp.float32)
         out[strip.sums : strip.rows] = total
@@ -256,7 +250,6 @@
             src[tile, plane, at : at + size] = value
         else:
             targets[kind][0, tile, plane, at : at + size] = value
-            targets[kind][1, tile, plane, at : at + size] = roll(value, LANES - 1)
 
     for number, (ref, plane, z) in enumerate(listed):
         group, slot = divmod(number, 8)
@@ -286,9 +279,19 @@
                 r2 = strip.edge_ninth(1, kind, group)
                 halo = (packed[r0 : r0 + 1], packed[r1 : r1 + 1], packed[r2 : r2 + 1])
                 for tile, value in enumerate(tiles_of(*halo, slot, field)):
-                    for copy in both:
-                        targets[field][copy, tile, z + LEAD, block : block + 8] = zero
+                    targets[field][0, tile, z + LEAD, block : block + 8] = zero
                     place(field, tile, z + LEAD, at, value)
+
+    def ahead_of(number, carry):
+        for plane in range(CHUNK):
+            for buffer in (pot, med):
+                for tile in both:
+                    for at in range(0, high, 8):
+                        cell = (tile, number * CHUNK + plane + LEAD, slice(at, at + 8))
+                        buffer[(1,) + cell] = roll(buffer[(0,) + cell], LANES - 1)
+        return carry
+
+    lax.fori_loop(0, planes // CHUNK, ahead_of, 0)
 
     def edges_of(z, carry):
         here = layer[z + 1] * 18
@@ -383,7 +386,7 @@
             if step + 1 < ITERS:
                 lift(later, side_next, base - CHUNK)
             for tile in both:
-                for block in range(inner):
+                for block in range(inner) if step + 1 < ITERS else range(1, inner - 1):
                     at = 8 + 8 * block
                     for plane in range(CHUNK):
                         z = base + plane
@@ -583,7 +586,7 @@
     groups = -(-planes // 8)
     y_rows = 3 * groups * rows + 8
 
-    to_left, to_right, sums = pl.pallas_call(
+    to_left, to_right, sums_own = pl.pallas_call(
         functools.partial(pack_y, (pieces, summed, rows)),
         out_shape=(f32(y_rows, LANES), f32(y_rows, LANES), f32(8, LANES)),
         in_specs=[VMEM] * len(pieces),
@@ -593,22 +596,25 @@
     )(*fields)
     from_left = lax.ppermute(to_right, "gy", cyclic(gy, 1))
     from_right = lax.ppermute(to_left, "gy", cyclic(gy, gy - 1))
-    others = [sums] + [lax.ppermute(sums, "gy", cyclic(gy, s)) for s in range(2, gy - 1)]
+    last = 3 * groups * rows
+    sums = sums_own + from_left[last:] + from_right[last:]
+    for s in range(2, gy - 1):
+        sums = sums + lax.ppermute(sums_own, "gy", cyclic(gy, s))
+    extra = [lax.ppermute(sums, "gx", cyclic(gx, s)) for s in range(2, gx - 1)]
+    extra.append(lax.ppermute(sums, "gx", [(0, gx - 1), (gx - 1, 0)]))
 
     strip = Strip(planes)
-    upper, lower, sums = pl.pallas_call(
-        functools.partial(pack_x, (pieces, rows, len(others))),
-        out_shape=(f32(strip.rows, LANES), f32(strip.rows, LANES), f32(8, LANES)),
-        in_specs=[VMEM] * (len(pieces) + 2 + len(others)),
-        out_specs=(VMEM,) * 3,
+    upper, lower = pl.pallas_call(
+        functools.partial(pack_x, (pieces, rows)),
+        out_shape=(f32(strip.rows, LANES), f32(strip.rows, LANES)),
+        in_specs=[VMEM] * (len(pieces) + 3),
+        out_specs=(VMEM,) * 2,
         compiler_params=params,
         name="pack_x",
-    )(*fields, from_left, from_right, *others)
+    )(*fields, from_left, from_right, sums)
     forth = [(i, i + 1) for i in range(gx - 1)]
     from_upper = lax.ppermute(lower, "gx", forth)
     from_lower = lax.ppermute(upper, "gx", [(j, i) for i, j in forth])
-    extra = [lax.ppermute(sums, "gx", cyclic(gx, s)) for s in range(2, gx - 1)]
-    extra.append(lax.ppermute(sums, "gx", [(0, gx - 1), (gx - 1, 0)]))
     if not full:
         sums = sums + from_upper[strip.sums :] + from_lower[strip.sums :] + sum(extra)
         sums = lax.psum(sums, "gz")

time: 80.7 us -> 71.5 us (0.89)
  Pallas kernels: 39.2 us -> 30 us
    pallas_call x1, Pallas kernels: 31.3 us -> 22 us  [fast(): pl.pallas_call(functools.partial(krylov, (pieces, planes, own_planes, row...]
    unnamed x30 -> x28, local copies, waits for them, and re-layouts: 2.78 us -> 2.19 us
where the time goes in v3:
time: 71.5 us; the launch traced here: 71.1 us
  Pallas kernels  30 us (42%)
  starting transfers between devices  18 us (25%)
  blocking collectives  10.3 us (14%)
  waiting for transfers between devices  8.39 us (12%)
  local copies, waits for them, and re-layouts  2.19 us (3%)
  other arithmetic  1.56 us (2%)
  between operations  0.75 us (1%)
    pallas_call x1, Pallas kernels, fast(): pl.pallas_call(functools.partial(krylov, (pieces, planes, own_planes, row...  22 us
    all_to_all x1, blocking collectives, fast(): gathered = lax.all_to_all(gram, ('gx', 'gy', 'gz'), 0, 0, tiled=True)  10.3 us
    ppermute x1, starting transfers between devices, fast(): extra.append(lax.ppermute(sums, 'gx', [(0, gx - 1), (gx - 1, 0)]))  6.58 us
    pallas_call x1, Pallas kernels, fast(): pl.pallas_call(functools.partial(finish, (own_planes, rows)), out_shape=(...  3.98 us
    ppermute x1, starting transfers between devices, fast(): from_upper = lax.ppermute(lower, 'gx', forth)  3.62 us
    ppermute x1, starting transfers between devices, fast(): from_left = lax.ppermute(to_right, 'gy', cyclic(gy, 1))  2.85 us
    unnamed x28, local copies, waits for them, and re-layouts  2.19 us
    ppermute x1, waiting for transfers between devices, fast(): extra.append(lax.ppermute(sums, 'gx', [(0, gx - 1), (gx - 1, 0)]))  2.13 us
  transfers between devices with their start and end apart: 9, of which 6 were waited for; matrix products, arithmetic and copies ran while one was open for 0% of the time, Pallas kernels for 0%

profile of v3, /device:TPU:0, one launch (start us, length us, event | category | flops | bytes accessed | tf_op | source)
XLA Modules:
  0.0 71.1 jit_solution(7816452382758817478)
XLA Ops:
  0.6 0.0 copy-start.6
  0.6 0.0 copy-start.7
  0.6 0.9 %convert_bitcast_fusion = f32[1,8,24,128]{3,2,1,0:T(8,128)S(1)} fusion(s32[8,24,128]{2,1,0:T(8,128)} %param.6), kind=kLoop, calls=%fused_computation.1 | loop fusion | flops 24576 | bytes 196608 | tf_op jit(solution)/shard_map/stack | solution.py:562
  1.6 0.0 copy-done.6
  1.6 0.0 copy-done.7
  1.6 0.0 copy-start
  1.7 0.6 collective-permute-start.1
  2.2 1.2 %collective-permute-done.1.refs_1_.refs_3_ = f32[3,8,24,128]{3,2,1,0:T(8,128)S(1)} collective-permute-done((f32[3,8,24,128]{3,2,1,0:T(8,128)S(1)}, f32[3,8,24,128]{3,2,1,0:T(8,128)S(1)}, u32[]{:S(2)}, u32[]{:S(2)}) %collective-permute-start.1) | collective-permute-done | bytes 294944 | tf_op jit(solution)/shard_map/ppermute | solution.py:569
  3.4 0.0 copy-done
  3.4 0.0 copy-start.1
  3.4 0.7 copy-done.1
  4.1 2.0 %pack_y.1 = (f32[152,128]{1,0:T(8,128)}, f32[152,128]{1,0:T(8,128)}, f32[8,128]{1,0:T(8,128)}) custom-call(f32[3,8,24,128]{3,2,1,0:T(8,128)} %copy-done, f32[3,8,24,128]{3,2,1,0:T(8,128)} %copy-done.1), custom_call_target="tpu_custom_call" | custom-call | tf_op jit(solution)/shard_map/pack_y/pallas_call | solution.py:589
  6.2 0.0 copy-start.11
  6.2 2.8 %collective-permute-start.2 = (f32[152,128]{1,0:T(8,128)}, f32[152,128]{1,0:T(8,128)S(1)}, u32[]{:S(2)}, u32[]{:S(2)}) collective-permute-start(f32[152,128]{1,0:T(8,128)} %get-tuple-element.13), channel_id=1, source_target_pairs={{0,2},{2,4},{4,6},{6,0},{1,3},{3,5},{5,7},{7,1},{8,10},{10,12},{12... | collective-permute-start | bytes 233480 | tf_op jit(solution)/shard_map/ppermute | solution.py:597
  9.0 1.0 %collective-permute-start.3 = (f32[152,128]{1,0:T(8,128)}, f32[152,128]{1,0:T(8,128)S(1)}, u32[]{:S(2)}, u32[]{:S(2)}) collective-permute-start(f32[152,128]{1,0:T(8,128)} %get-tuple-element.14), channel_id=1, source_target_pairs={{0,6},{2,0},{4,2},{6,4},{1,7},{3,1},{5,3},{7,5},{8,14},{10,8},{12,... | collective-permute-start | bytes 233480 | tf_op jit(solution)/shard_map/ppermute | solution.py:598
  10.0 0.0 copy-done.11
  10.0 1.9 %collective-permute-start.4 = (f32[8,128]{1,0:T(8,128)S(1)}, f32[8,128]{1,0:T(8,128)S(1)}, u32[]{:S(2)}, u32[]{:S(2)}) collective-permute-start(f32[8,128]{1,0:T(8,128)S(1)} %copy-done.11), channel_id=1, source_target_pairs={{0,4},{2,6},{4,0},{6,2},{1,5},{3,7},{5,1},{7,3},{8,12},{10,14},{12... | collective-permute-start | bytes 12296 | tf_op jit(solution)/shard_map/ppermute | solution.py:602
  12.0 1.7 %collective-permute-done.4 = f32[8,128]{1,0:T(8,128)S(1)} collective-permute-done((f32[8,128]{1,0:T(8,128)S(1)}, f32[8,128]{1,0:T(8,128)S(1)}, u32[]{:S(2)}, u32[]{:S(2)}) %collective-permute-start.4) | collective-permute-done | bytes 4128 | tf_op jit(solution)/shard_map/ppermute | solution.py:602
  13.6 0.0 collective-permute-done.2.refs_2_.refs_4_
  13.6 0.0 copy-start.2
  13.7 1.1 %collective-permute-done.3.refs_3_.refs_5_ = f32[152,128]{1,0:T(8,128)S(1)} collective-permute-done((f32[152,128]{1,0:T(8,128)}, f32[152,128]{1,0:T(8,128)S(1)}, u32[]{:S(2)}, u32[]{:S(2)}) %collective-permute-start.3) | collective-permute-done | bytes 77856 | tf_op jit(solution)/shard_map/ppermute | solution.py:598
  14.8 0.0 copy-start.3
  14.8 0.6 fusion.refs_4_.refs_8_
  15.4 0.0 copy-done.2
  15.4 0.0 copy-done.3
  15.4 0.0 copy-start.8
  15.4 1.9 %pack_x.1 = (f32[528,128]{1,0:T(8,128)}, f32[528,128]{1,0:T(8,128)}) custom-call(f32[3,8,24,128]{3,2,1,0:T(8,128)} %copy-done, f32[3,8,24,128]{3,2,1,0:T(8,128)} %copy-done.1, f32[152,128]{1,0:T(8,128)} %copy-done.2, f32[152,128]{1,0:T(8,128)} %copy-done.3, f32[8,128]{1,0:T(8,128)} %fusion.refs_4_.refs_8_), custom_call_target="tpu_custom_call" | custom-call | tf_op jit(solution)/shard_map/pack_x/pallas_call | solution.py:607
  17.4 0.0 copy-start.12
  17.4 3.6 %collective-permute-start.5 = (f32[528,128]{1,0:T(8,128)}, f32[528,128]{1,0:T(8,128)S(1)}, u32[]{:S(2)}, u32[]{:S(2)}) collective-permute-start(f32[528,128]{1,0:T(8,128)} %get-tuple-element.16), channel_id=1, source_target_pairs={{0,8},{8,16},{16,24},{1,9},{9,17},{17,25},{2,10},{10,18},{18,26},{... | collective-permute-start | bytes 811016 | tf_op jit(solution)/shard_map/ppermute | solution.py:616
  21.0 1.3 %collective-permute-start.6 = (f32[528,128]{1,0:T(8,128)}, f32[528,128]{1,0:T(8,128)S(1)}, u32[]{:S(2)}, u32[]{:S(2)}) collective-permute-start(f32[528,128]{1,0:T(8,128)} %get-tuple-element.17), channel_id=1, source_target_pairs={{8,0},{16,8},{24,16},{9,1},{17,9},{25,17},{10,2},{18,10},{26,18},{... | collective-permute-start | bytes 811016 | tf_op jit(solution)/shard_map/ppermute | solution.py:617
  22.3 0.0 copy-done.8
  22.3 6.6 %collective-permute-start.8 = (f32[8,128]{1,0:T(8,128)S(1)}, f32[8,128]{1,0:T(8,128)S(1)}, u32[]{:S(2)}, u32[]{:S(2)}) collective-permute-start(f32[8,128]{1,0:T(8,128)S(1)} %copy-done.8), channel_id=1, source_target_pairs={{0,24},{24,0},{1,25},{25,1},{2,26},{26,2},{3,27},{27,3},{4,28},{28... | collective-permute-start | bytes 12296 | tf_op jit(solution)/shard_map/ppermute | solution.py:604
  28.9 0.1 collective-permute-start.7
  29.0 0.0 copy-done.12
  29.0 0.1 collective-permute-start
  29.0 1.1 %collective-permute-done.refs_1_ = s32[8]{0:T(128)S(1)} collective-permute-done((s32[8]{0:T(128)S(1)}, s32[8]{0:T(128)S(1)}, u32[]{:S(2)}, u32[]{:S(2)}) %collective-permute-start) | collective-permute-done | bytes 64 | tf_op jit(solution)/shard_map/ppermute | solution.py:570
  30.2 2.1 %collective-permute-done.8.refs_10_ = f32[8,128]{1,0:T(8,128)S(1)} collective-permute-done((f32[8,128]{1,0:T(8,128)S(1)}, f32[8,128]{1,0:T(8,128)S(1)}, u32[]{:S(2)}, u32[]{:S(2)}) %collective-permute-start.8) | collective-permute-done | bytes 4128 | tf_op jit(solution)/shard_map/ppermute | solution.py:604
  32.3 1.1 %collective-permute-done.7.refs_9_ = f32[8,128]{1,0:T(8,128)S(1)} collective-permute-done((f32[8,128]{1,0:T(8,128)S(1)}, f32[8,128]{1,0:T(8,128)S(1)}, u32[]{:S(2)}, u32[]{:S(2)}) %collective-permute-start.7) | collective-permute-done | bytes 4128 | tf_op jit(solution)/shard_map/ppermute | solution.py:603
  33.4 0.0 collective-permute-done.5.refs_6_
  33.5 0.0 collective-permute-done.6.refs_7_
  33.5 0.0 copy-done.13
  33.5 0.0 copy-done.9
  33.5 0.6 copy-done.10
  34.0 0.1 copy-done.4
  34.2 0.7 copy-done.5
  34.9 22.0 %krylov.1 = (f32[32,128]{1,0:T(8,128)}, f32[9,8,24,128]{3,2,1,0:T(8,128)}, f32[8,24,128]{2,1,0:T(8,128)}, f32[8,128]{1,0:T(8,128)}) custom-call(f32[288]{0:T(512)} %constant.2.clone.table, s32[8]{0:T(128)} %refs_0_.1, s32[8]{0:T(128)} %copy-done.13, f32[3,8,24,128]{3,2,1,0:T(8,128)} %copy-done, f32[3,8,24,128]{3,2,1,0:T(8,128)} %copy-done.1, ...), custom_call_target="tpu_custom_call" | custom-call | tf_op jit(solution)/shard_map/krylov/pallas_call | solution.py:633
  56.9 10.3 %all_to_all.11 = f32[32,1,128]{2,1,0:T(1,128)} all-to-all(f32[32,1,128]{2,1,0:T(1,128)} %bitcast.11), channel_id=1, replica_groups=mesh['gx'=4,'gy'=4,'gz'=2] {'gx','gy','gz'}, dimensions={0} | all-to-all | bytes 32768 | tf_op jit(solution)/shard_map/all_to_all | solution.py:669
  67.2 4.0 %finish.1 = (f32[8,24,128]{2,1,0:T(8,128)}, f32[8,24,128]{2,1,0:T(8,128)}, f32[8,128]{1,0:T(8,128)}) custom-call(f32[32,128]{1,0:T(8,128)} %bitcast.10, f32[8,128]{1,0:T(8,128)} %get-tuple-element.19.total_in, f32[9,8,24,128]{3,2,1,0:T(8,128)} %get-tuple-element.20.basis, f32[8,24,128]{2,1,0:T(8,128)} %get-tuple-element.21.metric), custom_call_target="tpu_custom_call" | custom-call | tf_op jit(solution)/shard_map/finish/pallas_call | solution.py:670
  (6 shorter events, 0.0 us)
Async XLA Ops:
  0.6 1.0 %copy-start.6 = (f32[8,24,128]{2,1,0:T(8,128)S(1)}, f32[8,24,128]{2,1,0:T(8,128)}, u32[]{:S(2)}) copy-start(f32[8,24,128]{2,1,0:T(8,128)} %param.8) | copy-start | bytes 294916
  0.6 1.0 %copy-start.7 = (f32[8,24,128]{2,1,0:T(8,128)S(1)}, f32[8,24,128]{2,1,0:T(8,128)}, u32[]{:S(2)}) copy-start(f32[8,24,128]{2,1,0:T(8,128)} %param.5) | copy-start | bytes 294916
  1.6 1.8 %copy-start = (f32[3,8,24,128]{3,2,1,0:T(8,128)}, f32[3,8,24,128]{3,2,1,0:T(8,128)S(1)}, u32[]{:S(2)}) copy-start(f32[3,8,24,128]{3,2,1,0:T(8,128)S(1)} %pad_maximum_fusion.refs_0_.refs_2_) | copy-start | bytes 884740
  1.7 1.8 %collective-permute-start.1 = (f32[3,8,24,128]{3,2,1,0:T(8,128)S(1)}, f32[3,8,24,128]{3,2,1,0:T(8,128)S(1)}, u32[]{:S(2)}, u32[]{:S(2)}) collective-permute-start(f32[3,8,24,128]{3,2,1,0:T(8,128)S(1)} %pad_maximum_fusion.refs_0_.refs_2_), channel_id=1, source_target_pairs={{0,1},{1,0},{2,3},{3,2},{4,5},{5,4},{6,7},{7,6},{8,9},{9,8},{10,11... | collective-permute-start | bytes 884744 | tf_op jit(solution)/shard_map/ppermute | solution.py:569
  3.4 0.7 copy-start.1
  6.2 3.9 %copy-start.11 = (f32[8,128]{1,0:T(8,128)S(1)}, f32[8,128]{1,0:T(8,128)}, u32[]{:S(2)}) copy-start(f32[8,128]{1,0:T(8,128)} %get-tuple-element.15) | copy-start | bytes 12292
  6.2 7.5 %collective-permute-start.2 = (f32[152,128]{1,0:T(8,128)}, f32[152,128]{1,0:T(8,128)S(1)}, u32[]{:S(2)}, u32[]{:S(2)}) collective-permute-start(f32[152,128]{1,0:T(8,128)} %get-tuple-element.13), channel_id=1, source_target_pairs={{0,2},{2,4},{4,6},{6,0},{1,3},{3,5},{5,7},{7,1},{8,10},{10,12},{12... | collective-permute-start | bytes 233480 | tf_op jit(solution)/shard_map/ppermute | solution.py:597
  9.0 5.7 %collective-permute-start.3 = (f32[152,128]{1,0:T(8,128)}, f32[152,128]{1,0:T(8,128)S(1)}, u32[]{:S(2)}, u32[]{:S(2)}) collective-permute-start(f32[152,128]{1,0:T(8,128)} %get-tuple-element.14), channel_id=1, source_target_pairs={{0,6},{2,0},{4,2},{6,4},{1,7},{3,1},{5,3},{7,5},{8,14},{10,8},{12,... | collective-permute-start | bytes 233480 | tf_op jit(solution)/shard_map/ppermute | solution.py:598
  10.0 3.6 %collective-permute-start.4 = (f32[8,128]{1,0:T(8,128)S(1)}, f32[8,128]{1,0:T(8,128)S(1)}, u32[]{:S(2)}, u32[]{:S(2)}) collective-permute-start(f32[8,128]{1,0:T(8,128)S(1)} %copy-done.11), channel_id=1, source_target_pairs={{0,4},{2,6},{4,0},{6,2},{1,5},{3,7},{5,1},{7,3},{8,12},{10,14},{12... | collective-permute-start | bytes 12296 | tf_op jit(solution)/shard_map/ppermute | solution.py:602
  13.6 1.7 %copy-start.2 = (f32[152,128]{1,0:T(8,128)}, f32[152,128]{1,0:T(8,128)S(1)}, u32[]{:S(2)}) copy-start(f32[152,128]{1,0:T(8,128)S(1)} %collective-permute-done.2.refs_2_.refs_4_) | copy-start | bytes 233476
  14.8 0.6 copy-start.3
  15.4 6.9 %copy-start.8 = (f32[8,128]{1,0:T(8,128)S(1)}, f32[8,128]{1,0:T(8,128)}, u32[]{:S(2)}) copy-start(f32[8,128]{1,0:T(8,128)} %fusion.refs_4_.refs_8_) | copy-start | bytes 12292
  17.4 11.6 %copy-start.12 = (s32[8]{0:T(128)S(1)}, s32[8]{0:T(128)}, u32[]{:S(2)}) copy-start(s32[8]{0:T(128)} %refs_0_.1) | copy-start | bytes 100
  17.4 16.1 %collective-permute-start.5 = (f32[528,128]{1,0:T(8,128)}, f32[528,128]{1,0:T(8,128)S(1)}, u32[]{:S(2)}, u32[]{:S(2)}) collective-permute-start(f32[528,128]{1,0:T(8,128)} %get-tuple-element.16), channel_id=1, source_target_pairs={{0,8},{8,16},{16,24},{1,9},{9,17},{17,25},{2,10},{10,18},{18,26},{... | collective-permute-start | bytes 811016 | tf_op jit(solution)/shard_map/ppermute | solution.py:616
  21.0 12.5 %collective-permute-start.6 = (f32[528,128]{1,0:T(8,128)}, f32[528,128]{1,0:T(8,128)S(1)}, u32[]{:S(2)}, u32[]{:S(2)}) collective-permute-start(f32[528,128]{1,0:T(8,128)} %get-tuple-element.17), channel_id=1, source_target_pairs={{8,0},{16,8},{24,16},{9,1},{17,9},{25,17},{10,2},{18,10},{26,18},{... | collective-permute-start | bytes 811016 | tf_op jit(solution)/shard_map/ppermute | solution.py:617
  22.3 10.0 %collective-permute-start.8 = (f32[8,128]{1,0:T(8,128)S(1)}, f32[8,128]{1,0:T(8,128)S(1)}, u32[]{:S(2)}, u32[]{:S(2)}) collective-permute-start(f32[8,128]{1,0:T(8,128)S(1)} %copy-done.8), channel_id=1, source_target_pairs={{0,24},{24,0},{1,25},{25,1},{2,26},{26,2},{3,27},{27,3},{4,28},{28... | collective-permute-start | bytes 12296 | tf_op jit(solution)/shard_map/ppermute | solution.py:604
  28.9 4.6 %collective-permute-start.7 = (f32[8,128]{1,0:T(8,128)S(1)}, f32[8,128]{1,0:T(8,128)S(1)}, u32[]{:S(2)}, u32[]{:S(2)}) collective-permute-start(f32[8,128]{1,0:T(8,128)S(1)} %copy-done.8), channel_id=1, source_target_pairs={{0,16},{8,24},{16,0},{24,8},{1,17},{9,25},{17,1},{25,9},{2,18},{10... | collective-permute-start | bytes 12296 | tf_op jit(solution)/shard_map/ppermute | solution.py:603
  29.0 1.2 %collective-permute-start = (s32[8]{0:T(128)S(1)}, s32[8]{0:T(128)S(1)}, u32[]{:S(2)}, u32[]{:S(2)}) collective-permute-start(s32[8]{0:T(128)S(1)} %copy-done.12), channel_id=1, source_target_pairs={{0,1},{1,0},{2,3},{3,2},{4,5},{5,4},{6,7},{7,6},{8,9},{9,8},{10,11... | collective-permute-start | bytes 104 | tf_op jit(solution)/shard_map/ppermute | solution.py:570
  30.2 3.3 %copy-start.13 = (s32[8]{0:T(128)}, s32[8]{0:T(128)S(1)}, u32[]{:S(2)}) copy-start(s32[8]{0:T(128)S(1)} %collective-permute-done.refs_1_) | copy-start | bytes 100
  32.3 1.1 %copy-start.9 = (f32[8,128]{1,0:T(8,128)}, f32[8,128]{1,0:T(8,128)S(1)}, u32[]{:S(2)}) copy-start(f32[8,128]{1,0:T(8,128)S(1)} %collective-permute-done.8.refs_10_) | copy-start | bytes 12292
  33.4 0.6 copy-start.10
  33.5 0.7 %copy-start.4 = (f32[528,128]{1,0:T(8,128)}, f32[528,128]{1,0:T(8,128)S(1)}, u32[]{:S(2)}) copy-start(f32[528,128]{1,0:T(8,128)S(1)} %collective-permute-done.5.refs_6_) | copy-start | bytes 811012
  34.2 0.7 copy-start.5

commit v4 on v3

--- a/solution.py
+++ b/solution.py
@@ -8,6 +8,7 @@
 from jax.experimental import pallas as pl
 from jax.experimental.pallas import tpu as pltpu
 from jax.sharding import PartitionSpec as P
+
 
 ITERS = 8
 LAYERS = 16
@@ -18,6 +19,8 @@
 LEAD = 2
 CHUNK = 2
 VECS = ITERS + 1
+LEAST_PIVOT = 0.02
+SPREAD_LIMIT = 1e4
 SUMS = VECS * VECS
 
 OFFSETS = [
@@ -31,6 +34,7 @@
     (1, 0, 1),
     (-1, 0, 1),
 ]
+STEPS = [(-dz, 1, -1) if (dz, dx, dy) == (0, -1, 1) else (dz, dx, dy) for dz, dx, dy in OFFSETS]
 bulk_long = 7.99
 bulk_trans = 2.55
 intra_long = 1.74
@@ -479,60 +483,67 @@
     own_planes, rows = geometry
     total = jnp.sum(gathered[...], axis=0, keepdims=True)
     count = jnp.sum(total_in[0:1], axis=1, keepdims=True)
-    lane = lane_iota((16, LANES))
-    sub = lax.broadcasted_iota(jnp.int32, (16, LANES), 0)
-    matrix = jnp.zeros((16, LANES), jnp.float32)
-    for i in range(VECS):
+    lane = lane_iota((8, LANES))
+    sub = lax.broadcasted_iota(jnp.int32, (8, LANES), 0)
+    pick = lambda index: jnp.sum(
+        jnp.where(lane[0:1] == index, total, 0.0), axis=1, keepdims=True
+    )
+    last = pick(VECS * VECS - 1)
+    sums = [pick(SUMS + k) for k in range(ITERS + 1)]
+    matrix = jnp.zeros((8, LANES), jnp.float32)
+    for i in range(ITERS):
         line = roll(total, LANES - VECS * i)
-        matrix = jnp.where(sub == i, jnp.broadcast_to(line, (16, LANES)), matrix)
-    matrix = jnp.where(lane < VECS, matrix, 0.0)
-    reflected = jnp.where(lane == 0, roll(matrix, LANES - 1), roll(matrix, 1))
-    square = matrix - 0.5 * (roll(matrix, LANES - 1) + reflected)
-    system = jnp.where(lane < ITERS, square, 0.0)
-    system = jnp.where(lane == ITERS, roll(matrix, ITERS), system)[0:8]
-    lane8 = lane[0:8]
-    sub8 = sub[0:8]
+        matrix = jnp.where(sub == i, jnp.broadcast_to(line, (8, LANES)), matrix)
+    columns = [
+        jnp.broadcast_to(
+            jnp.sum(jnp.where(lane == k, matrix, 0.0), axis=1, keepdims=True), (8, LANES)
+        )
+        for k in range(VECS)
+    ]
+    row_of = lambda value, k: jnp.broadcast_to(value[k : k + 1], (8, LANES))
+    system = [columns[k] - 0.5 * (columns[k + 1] + columns[abs(k - 1)]) for k in range(ITERS)]
+    diagonal = [row_of(system[k], k) for k in range(ITERS)]
+    system.append(columns[0])
+    least = jnp.ones((8, LANES), jnp.float32)
     for k in range(ITERS):
-        line = system[k : k + 1]
-        pivot = jnp.sum(jnp.where(lane8[0:1] == k, line, 0.0), axis=1, keepdims=True)
-        line = line / pivot
-        column = jnp.sum(jnp.where(lane8 == k, system, 0.0), axis=1, keepdims=True)
-        line8 = jnp.broadcast_to(line, (8, LANES))
-        system = jnp.where(sub8 == k, line8, system - column * line8)
-    answer = jnp.sum(jnp.where(lane8 == ITERS, system, 0.0), axis=1, keepdims=True)
-    coef = [answer[k : k + 1] for k in range(ITERS)]
-    zero = jnp.zeros((1, 1), jnp.float32)
-    padded = coef + [zero, zero]
-    weights = []
-    for i in range(VECS):
-        value = 0.5 * padded[i + 1] - padded[i]
-        if i == 0:
-            value = value + 1.0
-        elif i == 1:
-            value = value + padded[0]
-        else:
-            value = value + 0.5 * padded[i - 1]
-        weights.append(value)
-    sums = [total[:, SUMS + k : SUMS + k + 1] for k in range(ITERS + 1)]
-    mean = zero
+        pivot = row_of(system[k], k)
+        least = jnp.minimum(least, pivot / diagonal[k])
+        inverse = 1.0 / pivot
+        for m in range(k + 1, ITERS + 1):
+            line = row_of(system[m], k) * inverse
+            system[m] = jnp.where(sub == k, line, system[m] - system[k] * line)
+    answer = system[ITERS]
+    coef = [row_of(answer, k) for k in range(ITERS)]
+    after = jnp.where(sub == ITERS - 1, 0.0, roll(answer, 7, 0))
+    before = jnp.where(sub == 0, 0.0, roll(answer, 1, 0))
+    weight = 0.5 * (after + jnp.where(sub == 1, 2.0, 1.0) * before) - answer
+    weight = jnp.where(sub == 0, weight + 1.0, weight)
+    weights = [row_of(weight, k) for k in range(ITERS)] + [0.5 * coef[ITERS - 1]]
+    mean = jnp.zeros((8, LANES), jnp.float32)
     for k in range(ITERS):
         mean = mean + coef[k] * sums[k]
     mean = mean / count
-    drift = sums[ITERS] / count
-    column = jnp.concatenate(weights + [zero] * (16 - VECS), axis=0)
-    row = jnp.zeros((1, LANES), jnp.float32)
-    for i in range(VECS):
-        row = jnp.where(lane[0:1] == i, weights[i], row)
-    size = jnp.sum(jnp.sum(matrix * column * row, axis=1, keepdims=True), axis=0, keepdims=True)
-    diagonal = jnp.sum(jnp.where(lane == sub, matrix, 0.0), axis=1, keepdims=True)
-    spread = jnp.sum(jnp.abs(column) * jnp.sqrt(diagonal), axis=0, keepdims=True)
-    flag[...] = jnp.broadcast_to(spread * spread / size, (8, LANES))
+    drift = jnp.broadcast_to(sums[ITERS] / count, (8, LANES))
+
+    product = jnp.zeros((8, LANES), jnp.float32)
+    norms = jnp.zeros((8, LANES), jnp.float32)
+    for k in range(VECS):
+        product = product + weights[k] * columns[k]
+        if k < ITERS:
+            norms = jnp.where(sub == k, columns[k], norms)
+    corner = jnp.sum(weight * columns[ITERS], axis=0, keepdims=True) + weights[ITERS] * last
+    size = jnp.sum(weight * product, axis=0, keepdims=True) + weights[ITERS] * corner
+    spread = jnp.sum(jnp.abs(weight) * jnp.sqrt(norms), axis=0, keepdims=True) + jnp.abs(
+        weights[ITERS]
+    ) * jnp.sqrt(last)
+    fine = (least > LEAST_PIVOT) & (size > 0.0) & (spread * spread < SPREAD_LIMIT * size)
+    flag[...] = jnp.where(fine, 1.0, 0.0)
 
     def combine(z, carry):
         for block in range(rows // 8):
             out = 8 * block
-            weight = metric[z, out : out + 8]
-            inside = jnp.minimum(weight, 1.0)
+            scale = metric[z, out : out + 8]
+            inside = jnp.minimum(scale, 1.0)
             phi = inside * (-mean)
             rest = jnp.zeros((8, LANES), jnp.float32)
             for k in range(VECS):
@@ -541,7 +552,7 @@
                     phi = phi + coef[k] * value
                 rest = rest + weights[k] * value
             solution_ref[z, out : out + 8] = phi
-            residual_ref[z, out : out + 8] = weight * rest - inside * drift
+            residual_ref[z, out : out + 8] = scale * rest - inside * drift
         return carry
 
     lax.fori_loop(0, own_planes, combine, 0)
@@ -556,7 +567,7 @@
 
 
 def fast(potential, tissue_mask, layer_index, source):
-    own_planes, rows, width = tissue_mask.shape
+    own_planes, rows, _ = tissue_mask.shape
     gx, gy, gz = (lax.axis_size(name) for name in ("gx", "gy", "gz"))
     params = pltpu.CompilerParams(vmem_limit_bytes=60 * 1024 * 1024)
     stacked = jnp.stack([potential, source, tissue_mask.astype(jnp.float32)])
@@ -600,8 +611,10 @@
     sums = sums_own + from_left[last:] + from_right[last:]
     for s in range(2, gy - 1):
         sums = sums + lax.ppermute(sums_own, "gy", cyclic(gy, s))
-    extra = [lax.ppermute(sums, "gx", cyclic(gx, s)) for s in range(2, gx - 1)]
-    extra.append(lax.ppermute(sums, "gx", [(0, gx - 1), (gx - 1, 0)]))
+    far = [cyclic(gx, s) for s in range(2, gx - 1)] + [[(0, gx - 1), (gx - 1, 0)]]
+    extra = []
+    for pairs in far:
+        extra.append(lax.ppermute(sums, "gx", pairs))
 
     strip = Strip(planes)
     upper, lower = pl.pallas_call(
@@ -678,9 +691,158 @@
     return answer, residual, flag
 
 
+def padded(value, sides, width):
+    for axis, dim in sides:
+        count, length = (lax.axis_size(axis), value.shape[dim])
+        up = [(i, (i + 1) % count) for i in range(count - 1)]
+        down = [(j, i) for i, j in up]
+        last = lax.slice_in_dim(value, length - width, length, axis=dim)
+        first = lax.slice_in_dim(value, 0, width, axis=dim)
+        before = lax.ppermute(last, axis, up)
+        after = lax.ppermute(first, axis, down)
+        value = jnp.concatenate([before, value, after], axis=dim)
+    return value
+
+
+def window(array, offset, extent):
+    return array[
+        1 + offset[0] : 1 + offset[0] + extent[0],
+        1 + offset[1] : 1 + offset[1] + extent[1],
+        1 + offset[2] : 1 + offset[2] + extent[2],
+    ]
+
+
+def cell_weight(planes, column, tissue_pad, bath_pad):
+    weight = tissue_pad * planes[:, column][:, None, None]
+    if bath_pad is not None and column < 3:
+        weight = weight + bath_sigma * bath_pad
+    return weight
+
+
+def edge_pair(weight, medium_pad, offset, extent):
+    backward = (-offset[0], -offset[1], -offset[2])
+    centre = window(medium_pad, (0, 0, 0), extent)
+    own_weight = window(weight, (0, 0, 0), extent)
+    forward_edge = (
+        centre
+        * window(medium_pad, offset, extent)
+        * (0.5 * (own_weight + window(weight, offset, extent)))
+    )
+    backward_edge = (
+        centre
+        * window(medium_pad, backward, extent)
+        * (0.5 * (own_weight + window(weight, backward, extent)))
+    )
+    return (forward_edge, backward_edge)
+
+
+def with_rim(field):
+    return padded(field, (("gx", 1), ("gy", 2), ("gz", 0)), 1)
+
+
+def operate(field, edge_list):
+    extent = field.shape
+    field_pad = with_rim(field)
+    summed = jnp.zeros(extent, jnp.float32)
+    for column, offset in enumerate(STEPS):
+        backward = (-offset[0], -offset[1], -offset[2])
+        forward_edge, backward_edge = edge_list[column]
+        summed = (
+            summed
+            + forward_edge * (field - window(field_pad, offset, extent))
+            + backward_edge * (field - window(field_pad, backward, extent))
+        )
+    return summed
+
+
+def plain(potential, tissue_mask, layer_index, source):
+    extent = tissue_mask.shape
+    mask_pad = padded(tissue_mask, (("gx", 1), ("gy", 2), ("gz", 0)), 1)
+    layer_pad = padded(layer_index, (("gz", 0),), 1)
+    selector = (layer_pad[:, None] == jnp.arange(LAYERS, dtype=jnp.int32)[None, :]).astype(
+        jnp.float32
+    )
+    bulk_planes = jnp.dot(
+        selector,
+        jnp.asarray(tensor_table(LAYERS, bulk_long, bulk_trans)),
+        precision=lax.Precision.HIGHEST,
+    )
+    intra_planes = jnp.dot(
+        selector,
+        jnp.asarray(tensor_table(LAYERS, intra_long, intra_trans)),
+        precision=lax.Precision.HIGHEST,
+    )
+    tissue_pad = (mask_pad == 2).astype(jnp.float32)
+    bath_pad = (mask_pad == 1).astype(jnp.float32)
+    inside_pad = (mask_pad > 0).astype(jnp.float32)
+    inside = window(inside_pad, (0, 0, 0), extent)
+    bulk_edges = [
+        edge_pair(
+            cell_weight(bulk_planes, column, tissue_pad, bath_pad), inside_pad, offset, extent
+        )
+        for column, offset in enumerate(STEPS)
+    ]
+    intra_edges = [
+        edge_pair(cell_weight(intra_planes, column, tissue_pad, None), tissue_pad, offset, extent)
+        for column, offset in enumerate(STEPS)
+    ]
+    diagonal = jnp.zeros(extent, jnp.float32)
+    for forward_edge, backward_edge in bulk_edges:
+        diagonal = diagonal + forward_edge + backward_edge
+    jacobi = inside / jnp.maximum(diagonal, 1.0)
+    rhs = -operate(potential, intra_edges) + inside * source
+    count, rhs_total = lax.psum((jnp.sum(inside), jnp.sum(rhs)), ("gx", "gy", "gz"))
+    residual = rhs - inside * (rhs_total / count)
+    solution = jnp.zeros(extent, jnp.float32)
+
+    def coupled(current):
+        scaled = jacobi * current
+        image = operate(scaled, bulk_edges)
+        scaled_total, cross_total, current_total, energy_total, image_total = lax.psum(
+            (
+                jnp.sum(scaled),
+                jnp.sum(current * scaled),
+                jnp.sum(current),
+                jnp.sum(scaled * image),
+                jnp.sum(image),
+            ),
+            ("gx", "gy", "gz"),
+        )
+        mean_value = scaled_total / count
+        precond = scaled - inside * mean_value
+        gamma_value = cross_total - mean_value * current_total
+        delta_value = energy_total - mean_value * image_total
+        return (precond, image, gamma_value, delta_value)
+
+    def step(number, state):
+        solution, residual, direction, along, gamma_now, alpha = state
+        precond, image, gamma_next, delta = coupled(residual)
+        begin = number == 0
+        beta = jnp.where(begin, 0.0, gamma_next / jnp.where(begin, 1.0, gamma_now))
+        scaled = jnp.where(begin, 0.0, beta * gamma_next / jnp.where(begin, 1.0, alpha))
+        alpha = gamma_next / (delta - scaled)
+        direction = precond + beta * direction
+        along = image + beta * along
+        solution = solution + alpha * direction
+        residual = residual - alpha * along
+        return (solution, residual, direction, along, gamma_next, alpha)
+
+    empty = jnp.zeros(extent, jnp.float32)
+    one = jnp.ones((), jnp.float32)
+    state = (solution, residual, empty, empty, one, one)
+    state = lax.fori_loop(0, ITERS, step, state)
+    return state[:2]
+
+
 def body(potential, tissue_mask, layer_index, source):
-    answer, residual, flag = fast(potential, tissue_mask, layer_index, source)
-    return (answer, residual)
+    args = (potential, tissue_mask, layer_index, source)
+    answer, residual, flag = fast(*args)
+    return lax.cond(
+        flag[0, 0] > 0.5,
+        lambda *_: (answer, residual),
+        plain,
+        *args,
+    )
 
 
 def solution(mesh):

time: 71.5 us -> 72.1 us (level)
  blocking collectives: 10.3 us -> 0 us
  waiting for transfers between devices: 8.39 us -> 15.1 us
  starting transfers between devices: 18 us -> 21 us
  local copies, waits for them, and re-layouts: 2.19 us -> 4.01 us
  Pallas kernels: 30 us -> 28.3 us
  between operations: 0.75 us -> 1.59 us
    all_to_all x1 -> x0, blocking collectives: 10.3 us -> none  [fast(): gathered = lax.all_to_all(gram, ('gx', 'gy', 'gz'), 0, 0, tiled=True)]
    all_to_all x0 -> x1, waiting for transfers between devices: none -> 7.17 us  [fast(): gathered = lax.all_to_all(gram, ('gx', 'gy', 'gz'), 0, 0, tiled=True)]
    all_to_all x0 -> x1, starting transfers between devices: none -> 2.65 us  [fast(): gathered = lax.all_to_all(gram, ('gx', 'gy', 'gz'), 0, 0, tiled=True)]
    pallas_call x1, Pallas kernels: 3.98 us -> 2.36 us  [fast(): pl.pallas_call(functools.partial(finish, (own_planes, rows)), out_shape=(...]
    slice x0 -> x1, local copies, waits for them, and re-layouts: none -> 1.21 us  [body(): flag[0, 0] > 0.5]
    unnamed x28 -> x32, local copies, waits for them, and re-layouts: 2.19 us -> 2.8 us
  transfers between devices with their start and end apart: 9 -> 10, of which waited for: 6 -> 7; matrix products, arithmetic and copies ran while one was open for 0% -> 0% of each run, Pallas kernels for 0% -> 0%
where the time goes in v4:
time: 72.1 us; the launch traced here: 71.8 us
  Pallas kernels  28.3 us (39%)
  starting transfers between devices  21 us (29%)
  waiting for transfers between devices  15.1 us (21%)
  local copies, waits for them, and re-layouts  4.01 us (6%)
  between operations  1.59 us (2%)
  other arithmetic  1.57 us (2%)
    pallas_call x1, Pallas kernels, fast(): pl.pallas_call(functools.partial(krylov, (pieces, planes, own_planes, row...  22 us
    all_to_all x1, waiting for transfers between devices, fast(): gathered = lax.all_to_all(gram, ('gx', 'gy', 'gz'), 0, 0, tiled=True)  7.17 us
    ppermute x2, starting transfers between devices, fast(): extra.append(lax.ppermute(sums, 'gx', pairs))  6.96 us
    ppermute x1, starting transfers between devices, fast(): from_upper = lax.ppermute(lower, 'gx', forth)  3.62 us
    ppermute x1, starting transfers between devices, fast(): from_left = lax.ppermute(to_right, 'gy', cyclic(gy, 1))  2.85 us
    unnamed x32, local copies, waits for them, and re-layouts  2.8 us
    ppermute x2, waiting for transfers between devices, fast(): extra.append(lax.ppermute(sums, 'gx', pairs))  2.78 us
    all_to_all x1, starting transfers between devices, fast(): gathered = lax.all_to_all(gram, ('gx', 'gy', 'gz'), 0, 0, tiled=True)  2.65 us
  transfers between devices with their start and end apart: 10, of which 7 were waited for; matrix products, arithmetic and copies ran while one was open for 0% of the time, Pallas kernels for 0%

profile of v4, /device:TPU:0, one launch (start us, length us, event | category | flops | bytes accessed | tf_op | source)
XLA Modules:
  0.0 71.8 jit_solution(4268205942403558613)
XLA Ops:
  0.6 0.0 copy-start.5
  0.6 0.0 copy-start.1
  0.6 0.9 %convert_bitcast_fusion = f32[1,8,24,128]{3,2,1,0:T(8,128)S(1)} fusion(s32[8,24,128]{2,1,0:T(8,128)} %param.12), kind=kLoop, calls=%fused_computation.340 | loop fusion | flops 24576 | bytes 196608 | tf_op jit(solution)/shard_map/stack | solution.py:573
  1.6 0.0 copy-done.5
  1.6 0.0 copy-done.1
  1.6 0.0 copy-start
  1.7 0.6 collective-permute-start.21
  2.2 1.2 %collective-permute-done.21.refs_1_.refs_3_ = f32[3,8,24,128]{3,2,1,0:T(8,128)S(1)} collective-permute-done((f32[3,8,24,128]{3,2,1,0:T(8,128)S(1)}, f32[3,8,24,128]{3,2,1,0:T(8,128)S(1)}, u32[]{:S(2)}, u32[]{:S(2)}) %collective-permute-start.21) | collective-permute-done | bytes 294944 | tf_op jit(solution)/shard_map/ppermute | solution.py:580
  3.4 0.0 copy-done
  3.4 0.0 copy-start.2
  3.4 0.7 %copy-done.2 = f32[3,8,24,128]{3,2,1,0:T(8,128)} copy-done((f32[3,8,24,128]{3,2,1,0:T(8,128)}, f32[3,8,24,128]{3,2,1,0:T(8,128)S(1)}, u32[]{:S(2)}) %copy-start.2) | copy-done | bytes 294936
  4.2 2.0 %pack_y.1 = (f32[152,128]{1,0:T(8,128)}, f32[152,128]{1,0:T(8,128)}, f32[8,128]{1,0:T(8,128)}) custom-call(f32[3,8,24,128]{3,2,1,0:T(8,128)} %copy-done, f32[3,8,24,128]{3,2,1,0:T(8,128)} %copy-done.2), custom_call_target="tpu_custom_call" | custom-call | tf_op jit(solution)/shard_map/pack_y/pallas_call | solution.py:600
  6.2 2.8 %collective-permute-start.22 = (f32[152,128]{1,0:T(8,128)}, f32[152,128]{1,0:T(8,128)S(1)}, u32[]{:S(2)}, u32[]{:S(2)}) collective-permute-start(f32[152,128]{1,0:T(8,128)} %get-tuple-element.476), channel_id=1, source_target_pairs={{0,2},{2,4},{4,6},{6,0},{1,3},{3,5},{5,7},{7,1},{8,10},{10,12},{12... | collective-permute-start | bytes 233480 | tf_op jit(solution)/shard_map/ppermute | solution.py:608
  9.1 1.0 %collective-permute-start.23 = (f32[152,128]{1,0:T(8,128)}, f32[152,128]{1,0:T(8,128)S(1)}, u32[]{:S(2)}, u32[]{:S(2)}) collective-permute-start(f32[152,128]{1,0:T(8,128)} %get-tuple-element.477), channel_id=1, source_target_pairs={{0,6},{2,0},{4,2},{6,4},{1,7},{3,1},{5,3},{7,5},{8,14},{10,8},{12,... | collective-permute-start | bytes 233480 | tf_op jit(solution)/shard_map/ppermute | solution.py:609
  10.1 0.0 copy-done.15
  10.1 1.9 %collective-permute-start.24 = (f32[8,128]{1,0:T(8,128)S(1)}, f32[8,128]{1,0:T(8,128)S(1)}, u32[]{:S(2)}, u32[]{:S(2)}) collective-permute-start(f32[8,128]{1,0:T(8,128)S(1)} %copy-done.15), channel_id=1, source_target_pairs={{0,4},{2,6},{4,0},{6,2},{1,5},{3,7},{5,1},{7,3},{8,12},{10,14},{12... | collective-permute-start | bytes 12296 | tf_op jit(solution)/shard_map/ppermute | solution.py:613
  12.0 1.7 %collective-permute-done.24 = f32[8,128]{1,0:T(8,128)S(1)} collective-permute-done((f32[8,128]{1,0:T(8,128)S(1)}, f32[8,128]{1,0:T(8,128)S(1)}, u32[]{:S(2)}, u32[]{:S(2)}) %collective-permute-start.24) | collective-permute-done | bytes 4128 | tf_op jit(solution)/shard_map/ppermute | solution.py:613
  13.7 0.0 collective-permute-done.22.refs_2_.refs_4_
  13.7 1.1 %collective-permute-done.23.refs_3_.refs_5_ = f32[152,128]{1,0:T(8,128)S(1)} collective-permute-done((f32[152,128]{1,0:T(8,128)}, f32[152,128]{1,0:T(8,128)S(1)}, u32[]{:S(2)}, u32[]{:S(2)}) %collective-permute-start.23) | collective-permute-done | bytes 77856 | tf_op jit(solution)/shard_map/ppermute | solution.py:609
  14.8 0.6 fusion.154.refs_4_.refs_8_
  15.4 0.0 copy-done.6
  15.4 0.0 copy-done.7
  15.4 1.9 %pack_x.1 = (f32[528,128]{1,0:T(8,128)}, f32[528,128]{1,0:T(8,128)}) custom-call(f32[3,8,24,128]{3,2,1,0:T(8,128)} %copy-done, f32[3,8,24,128]{3,2,1,0:T(8,128)} %copy-done.2, f32[152,128]{1,0:T(8,128)} %copy-done.6, f32[152,128]{1,0:T(8,128)} %copy-done.7, f32[8,128]{1,0:T(8,128)} %fusion.154.refs_4_.refs_8_), custom_call_target="tpu_custom_call" | custom-call | tf_op jit(solution)/shard_map/pack_x/pallas_call | solution.py:620
  17.4 3.6 %collective-permute-start.25 = (f32[528,128]{1,0:T(8,128)}, f32[528,128]{1,0:T(8,128)S(1)}, u32[]{:S(2)}, u32[]{:S(2)}) collective-permute-start(f32[528,128]{1,0:T(8,128)} %get-tuple-element.479), channel_id=1, source_target_pairs={{0,8},{8,16},{16,24},{1,9},{9,17},{17,25},{2,10},{10,18},{18,26},{... | collective-permute-start | bytes 811016 | tf_op jit(solution)/shard_map/ppermute | solution.py:629
  21.0 1.3 %collective-permute-start.26 = (f32[528,128]{1,0:T(8,128)}, f32[528,128]{1,0:T(8,128)S(1)}, u32[]{:S(2)}, u32[]{:S(2)}) collective-permute-start(f32[528,128]{1,0:T(8,128)} %get-tuple-element.480), channel_id=1, source_target_pairs={{8,0},{16,8},{24,16},{9,1},{17,9},{25,17},{10,2},{18,10},{26,18},{... | collective-permute-start | bytes 811016 | tf_op jit(solution)/shard_map/ppermute | solution.py:630
  22.3 0.0 copy-done.11
  22.3 3.7 %collective-permute-start.27 = (f32[8,128]{1,0:T(8,128)S(1)}, f32[8,128]{1,0:T(8,128)S(1)}, u32[]{:S(2)}, u32[]{:S(2)}) collective-permute-start(f32[8,128]{1,0:T(8,128)S(1)} %copy-done.11), channel_id=1, source_target_pairs={{0,16},{8,24},{16,0},{24,8},{1,17},{9,25},{17,1},{25,9},{2,18},{10... | collective-permute-start | bytes 12296 | tf_op jit(solution)/shard_map/ppermute | solution.py:617
  26.0 3.3 %collective-permute-start.28 = (f32[8,128]{1,0:T(8,128)S(1)}, f32[8,128]{1,0:T(8,128)S(1)}, u32[]{:S(2)}, u32[]{:S(2)}) collective-permute-start(f32[8,128]{1,0:T(8,128)S(1)} %copy-done.11), channel_id=1, source_target_pairs={{0,24},{24,0},{1,25},{25,1},{2,26},{26,2},{3,27},{27,3},{4,28},{28... | collective-permute-start | bytes 12296 | tf_op jit(solution)/shard_map/ppermute | solution.py:617
  29.3 0.0 copy-done.12
  29.3 0.1 collective-permute-start.20
  29.4 1.1 %collective-permute-done.20.refs_1_ = s32[8]{0:T(128)S(1)} collective-permute-done((s32[8]{0:T(128)S(1)}, s32[8]{0:T(128)S(1)}, u32[]{:S(2)}, u32[]{:S(2)}) %collective-permute-start.20) | collective-permute-done | bytes 64 | tf_op jit(solution)/shard_map/ppermute | solution.py:581
  30.5 0.9 %collective-permute-done.27.refs_9_ = f32[8,128]{1,0:T(8,128)S(1)} collective-permute-done((f32[8,128]{1,0:T(8,128)S(1)}, f32[8,128]{1,0:T(8,128)S(1)}, u32[]{:S(2)}, u32[]{:S(2)}) %collective-permute-start.27) | collective-permute-done | bytes 4128 | tf_op jit(solution)/shard_map/ppermute | solution.py:617
  31.4 1.9 %collective-permute-done.28.refs_10_ = f32[8,128]{1,0:T(8,128)S(1)} collective-permute-done((f32[8,128]{1,0:T(8,128)S(1)}, f32[8,128]{1,0:T(8,128)S(1)}, u32[]{:S(2)}, u32[]{:S(2)}) %collective-permute-start.28) | collective-permute-done | bytes 4128 | tf_op jit(solution)/shard_map/ppermute | solution.py:617
  33.3 0.0 collective-permute-done.25.refs_6_
  33.3 0.0 collective-permute-done.26.refs_7_
  33.3 0.0 copy-done.16
  33.3 0.0 copy-done.13
  33.3 0.6 copy-done.14
  33.9 0.1 copy-done.8
  34.0 0.7 copy-done.9
  34.7 22.0 %krylov.1 = (f32[32,128]{1,0:T(8,128)}, f32[9,8,24,128]{3,2,1,0:T(8,128)}, f32[8,24,128]{2,1,0:T(8,128)}, f32[8,128]{1,0:T(8,128)}) custom-call(f32[288]{0:T(512)} %constant.73.clone.table, s32[8]{0:T(128)S(1)} %copy-done.12, s32[8]{0:T(128)} %copy-done.16, f32[3,8,24,128]{3,2,1,0:T(8,128)} %copy-done, f32[3,8,24,128]{3,2,1,0:T(8,128)} %copy-done.2, ...), custom_call_target="tpu_custom_call" | custom-call | tf_op jit(solution)/shard_map/krylov/pallas_call | solution.py:646
  56.7 2.7 %all-to-all-start = ((f32[32,1,128]{2,1,0:T(1,128)}), f32[32,1,128]{2,1,0:T(1,128)S(1)}, u32[]{:S(2)}, u32[]{:S(2)}) async-start(f32[32,1,128]{2,1,0:T(1,128)} %bitcast.50), calls=%async_computation | async-start | bytes 32768 | tf_op jit(solution)/shard_map/all_to_all | solution.py:682
  59.4 7.2 %all-to-all-done = f32[32,1,128]{2,1,0:T(1,128)S(1)} async-done(((f32[32,1,128]{2,1,0:T(1,128)}), f32[32,1,128]{2,1,0:T(1,128)S(1)}, u32[]{:S(2)}, u32[]{:S(2)}) %all-to-all-start) | async-done | bytes 16416 | tf_op jit(solution)/shard_map/all_to_all | solution.py:682
  66.5 0.6 copy-done.10
  67.1 2.4 %finish.1 = (f32[8,24,128]{2,1,0:T(8,128)}, f32[8,24,128]{2,1,0:T(8,128)}, f32[8,128]{1,0:T(8,128)}) custom-call(f32[32,128]{1,0:T(8,128)} %bitcast.49, f32[8,128]{1,0:T(8,128)} %get-tuple-element.482.total_in, f32[9,8,24,128]{3,2,1,0:T(8,128)} %get-tuple-element.483.basis, f32[8,24,128]{2,1,0:T(8,128)} %get-tuple-element.484.metric), custom_call_target="tpu_custom_call" | custom-call | tf_op jit(solution)/shard_map/finish/pallas_call | solution.py:683
  69.5 1.2 %slice.658 = f32[1,1]{1,0:T(1,128)} slice(f32[8,128]{1,0:T(8,128)} %get-tuple-element.485), slice={[0:1], [0:1]} | slice | bytes 8 | tf_op jit(solution)/shard_map/slice | solution.py:841
  71.3 0.0 copy-done.3
  71.4 0.2 conditional.1
  (13 shorter events, 0.0 us)
Async XLA Ops:
  0.6 1.0 %copy-start.5 = (f32[8,24,128]{2,1,0:T(8,128)S(1)}, f32[8,24,128]{2,1,0:T(8,128)}, u32[]{:S(2)}) copy-start(f32[8,24,128]{2,1,0:T(8,128)} %param.14) | copy-start | bytes 294916
  0.6 1.0 %copy-start.1 = (f32[8,24,128]{2,1,0:T(8,128)S(1)}, f32[8,24,128]{2,1,0:T(8,128)}, u32[]{:S(2)}) copy-start(f32[8,24,128]{2,1,0:T(8,128)} %param.11) | copy-start | bytes 294916
  1.6 1.8 %copy-start = (f32[3,8,24,128]{3,2,1,0:T(8,128)}, f32[3,8,24,128]{3,2,1,0:T(8,128)S(1)}, u32[]{:S(2)}) copy-start(f32[3,8,24,128]{3,2,1,0:T(8,128)S(1)} %pad_maximum_fusion.20.refs_0_.refs_2_) | copy-start | bytes 884740
  1.7 1.8 %collective-permute-start.21 = (f32[3,8,24,128]{3,2,1,0:T(8,128)S(1)}, f32[3,8,24,128]{3,2,1,0:T(8,128)S(1)}, u32[]{:S(2)}, u32[]{:S(2)}) collective-permute-start(f32[3,8,24,128]{3,2,1,0:T(8,128)S(1)} %pad_maximum_fusion.20.refs_0_.refs_2_), channel_id=1, source_target_pairs={{0,1},{1,0},{2,3},{3,2},{4,5},{5,4},{6,7},{7,6},{8,9},{9,8},{10,11... | collective-permute-start | bytes 884744 | tf_op jit(solution)/shard_map/ppermute | solution.py:580
  3.4 0.7 %copy-start.2 = (f32[3,8,24,128]{3,2,1,0:T(8,128)}, f32[3,8,24,128]{3,2,1,0:T(8,128)S(1)}, u32[]{:S(2)}) copy-start(f32[3,8,24,128]{3,2,1,0:T(8,128)S(1)} %collective-permute-done.21.refs_1_.refs_3_) | copy-start | bytes 884740
  6.2 3.9 %copy-start.15 = (f32[8,128]{1,0:T(8,128)S(1)}, f32[8,128]{1,0:T(8,128)}, u32[]{:S(2)}) copy-start(f32[8,128]{1,0:T(8,128)} %get-tuple-element.478) | copy-start | bytes 12292
  6.2 7.5 %collective-permute-start.22 = (f32[152,128]{1,0:T(8,128)}, f32[152,128]{1,0:T(8,128)S(1)}, u32[]{:S(2)}, u32[]{:S(2)}) collective-permute-start(f32[152,128]{1,0:T(8,128)} %get-tuple-element.476), channel_id=1, source_target_pairs={{0,2},{2,4},{4,6},{6,0},{1,3},{3,5},{5,7},{7,1},{8,10},{10,12},{12... | collective-permute-start | bytes 233480 | tf_op jit(solution)/shard_map/ppermute | solution.py:608
  9.1 5.7 %collective-permute-start.23 = (f32[152,128]{1,0:T(8,128)}, f32[152,128]{1,0:T(8,128)S(1)}, u32[]{:S(2)}, u32[]{:S(2)}) collective-permute-start(f32[152,128]{1,0:T(8,128)} %get-tuple-element.477), channel_id=1, source_target_pairs={{0,6},{2,0},{4,2},{6,4},{1,7},{3,1},{5,3},{7,5},{8,14},{10,8},{12,... | collective-permute-start | bytes 233480 | tf_op jit(solution)/shard_map/ppermute | solution.py:609
  10.1 3.6 %collective-permute-start.24 = (f32[8,128]{1,0:T(8,128)S(1)}, f32[8,128]{1,0:T(8,128)S(1)}, u32[]{:S(2)}, u32[]{:S(2)}) collective-permute-start(f32[8,128]{1,0:T(8,128)S(1)} %copy-done.15), channel_id=1, source_target_pairs={{0,4},{2,6},{4,0},{6,2},{1,5},{3,7},{5,1},{7,3},{8,12},{10,14},{12... | collective-permute-start | bytes 12296 | tf_op jit(solution)/shard_map/ppermute | solution.py:613
  13.7 1.7 %copy-start.6 = (f32[152,128]{1,0:T(8,128)}, f32[152,128]{1,0:T(8,128)S(1)}, u32[]{:S(2)}) copy-start(f32[152,128]{1,0:T(8,128)S(1)} %collective-permute-done.22.refs_2_.refs_4_) | copy-start | bytes 233476
  14.8 0.6 copy-start.7
  15.4 6.9 %copy-start.11 = (f32[8,128]{1,0:T(8,128)S(1)}, f32[8,128]{1,0:T(8,128)}, u32[]{:S(2)}) copy-start(f32[8,128]{1,0:T(8,128)} %fusion.154.refs_4_.refs_8_) | copy-start | bytes 12292
  17.4 11.9 %copy-start.12 = (s32[8]{0:T(128)S(1)}, s32[8]{0:T(128)}, u32[]{:S(2)}) copy-start(s32[8]{0:T(128)} %refs_0_.1) | copy-start | bytes 100
  17.4 15.9 %collective-permute-start.25 = (f32[528,128]{1,0:T(8,128)}, f32[528,128]{1,0:T(8,128)S(1)}, u32[]{:S(2)}, u32[]{:S(2)}) collective-permute-start(f32[528,128]{1,0:T(8,128)} %get-tuple-element.479), channel_id=1, source_target_pairs={{0,8},{8,16},{16,24},{1,9},{9,17},{17,25},{2,10},{10,18},{18,26},{... | collective-permute-start | bytes 811016 | tf_op jit(solution)/shard_map/ppermute | solution.py:629
  21.0 12.3 %collective-permute-start.26 = (f32[528,128]{1,0:T(8,128)}, f32[528,128]{1,0:T(8,128)S(1)}, u32[]{:S(2)}, u32[]{:S(2)}) collective-permute-start(f32[528,128]{1,0:T(8,128)} %get-tuple-element.480), channel_id=1, source_target_pairs={{8,0},{16,8},{24,16},{9,1},{17,9},{25,17},{10,2},{18,10},{26,18},{... | collective-permute-start | bytes 811016 | tf_op jit(solution)/shard_map/ppermute | solution.py:630
  22.3 9.1 %collective-permute-start.27 = (f32[8,128]{1,0:T(8,128)S(1)}, f32[8,128]{1,0:T(8,128)S(1)}, u32[]{:S(2)}, u32[]{:S(2)}) collective-permute-start(f32[8,128]{1,0:T(8,128)S(1)} %copy-done.11), channel_id=1, source_target_pairs={{0,16},{8,24},{16,0},{24,8},{1,17},{9,25},{17,1},{25,9},{2,18},{10... | collective-permute-start | bytes 12296 | tf_op jit(solution)/shard_map/ppermute | solution.py:617
  26.0 7.3 %collective-permute-start.28 = (f32[8,128]{1,0:T(8,128)S(1)}, f32[8,128]{1,0:T(8,128)S(1)}, u32[]{:S(2)}, u32[]{:S(2)}) collective-permute-start(f32[8,128]{1,0:T(8,128)S(1)} %copy-done.11), channel_id=1, source_target_pairs={{0,24},{24,0},{1,25},{25,1},{2,26},{26,2},{3,27},{27,3},{4,28},{28... | collective-permute-start | bytes 12296 | tf_op jit(solution)/shard_map/ppermute | solution.py:617
  29.3 1.2 %collective-permute-start.20 = (s32[8]{0:T(128)S(1)}, s32[8]{0:T(128)S(1)}, u32[]{:S(2)}, u32[]{:S(2)}) collective-permute-start(s32[8]{0:T(128)S(1)} %copy-done.12), channel_id=1, source_target_pairs={{0,1},{1,0},{2,3},{3,2},{4,5},{5,4},{6,7},{7,6},{8,9},{9,8},{10,11... | collective-permute-start | bytes 104 | tf_op jit(solution)/shard_map/ppermute | solution.py:581
  30.5 2.8 %copy-start.16 = (s32[8]{0:T(128)}, s32[8]{0:T(128)S(1)}, u32[]{:S(2)}) copy-start(s32[8]{0:T(128)S(1)} %collective-permute-done.20.refs_1_) | copy-start | bytes 100
  31.4 2.0 %copy-start.13 = (f32[8,128]{1,0:T(8,128)}, f32[8,128]{1,0:T(8,128)S(1)}, u32[]{:S(2)}) copy-start(f32[8,128]{1,0:T(8,128)S(1)} %collective-permute-done.27.refs_9_) | copy-start | bytes 12292
  33.3 0.6 copy-start.14
  33.3 0.7 copy-start.8
  34.0 0.7 copy-start.9
  56.7 9.8 %all-to-all-start = ((f32[32,1,128]{2,1,0:T(1,128)}), f32[32,1,128]{2,1,0:T(1,128)S(1)}, u32[]{:S(2)}, u32[]{:S(2)}) async-start(f32[32,1,128]{2,1,0:T(1,128)} %bitcast.50), calls=%async_computation | async-start | bytes 32768 | tf_op jit(solution)/shard_map/all_to_all | solution.py:682
  66.5 0.6 copy-start.10
  67.1 4.2 %copy-start.3 = (s32[8,24,128]{2,1,0:T(8,128)S(1)}, s32[8,24,128]{2,1,0:T(8,128)}, u32[]{:S(2)}) copy-start(s32[8,24,128]{2,1,0:T(8,128)} %param.12) | copy-start | bytes 294916
